TPU v7x, 16 devices: a 4x2x1 block of a 4x4x8 slice. The times are simulated.
16 devices in a mesh: dp: 2 (over y, z), tp: 8 (over x, core).
Axes of the slice: x: 4, y: 2, z: 1, core: 2. Of those that a mesh axis runs over, the one named last changes fastest.
The devices are a block of a 4x4x8 slice.
Arguments:
- hidden: bfloat16 [32, 384, 3072], P('dp', 'tp'), parts along dimension 0
- positions: int32 [32, 384], P('dp', 'tp'), parts along dimension 0
- doc_ids: int32 [32, 384], P('dp', 'tp'), parts along dimension 0
- norm_gain: bfloat16 [3072], replicated
- w_query: bfloat16 [3072, 3072], P(None, 'tp')
- w_key: bfloat16 [3072, 1024], P(None, 'tp')
- w_value: bfloat16 [3072, 1024], P(None, 'tp')
- w_out: bfloat16 [3072, 3072], P('tp')
- grad_out: bfloat16 [32, 384, 3072], P('dp', 'tp'), parts along dimension 0
Outputs:
- output 1: bfloat16 [32, 384, 3072], P('dp', 'tp'), parts along dimension 0
- output 2: bfloat16 [32, 384, 3072], P('dp', 'tp'), parts along dimension 0
- output 3: float32 [6144], P('dp'), parts along dimension 0
- output 4: float32 [6144, 3072], P('dp', 'tp'), parts along dimension 0
- output 5: float32 [6144, 1024], P('dp', 'tp'), parts along dimension 0
- output 6: float32 [6144, 1024], P('dp', 'tp'), parts along dimension 0
- output 7: float32 [6144, 3072], P(('dp', 'tp')), parts along dimension 0
There are 2 independent parts. A program takes and returns all parts, laid end to end along the dimension named above; an argument that names none is the same for every part.
All inputs are finite; a program needn't handle non-finite values.
Results may differ from a plain program's by a relative error of at most 0.00998037.
Values are sent between devices in bfloat16 or wider.
A program may use at most 768 MiB of HBM per device.

v0:
```python
import jax
import jax.numpy as jnp
from jax import lax
from jax.sharding import PartitionSpec as P

HEAD_DIM = 128
NORM_EPS = 1e-5
ROPE_BASE = 10000.0


def rope_tables(positions):
    inv_freq = ROPE_BASE ** (-jnp.arange(0, HEAD_DIM, 2, dtype=jnp.float32) / HEAD_DIM)
    angles = positions.astype(jnp.float32)[:, :, None] * inv_freq
    return jnp.cos(angles)[:, :, None, :], jnp.sin(angles)[:, :, None, :]


def rotate_pairs(values, cos_tab, sin_tab):
    pair_view = values.reshape(values.shape[:-1] + (HEAD_DIM // 2, 2))
    even_part = pair_view[..., 0]
    odd_part = pair_view[..., 1]
    turned = jnp.stack([even_part * cos_tab - odd_part * sin_tab, even_part * sin_tab + odd_part * cos_tab], axis=-1)
    return turned.reshape(values.shape)


def attend_mask(doc_full):
    seq_len = doc_full.shape[1]
    rows_iota = lax.broadcasted_iota(jnp.int32, (seq_len, seq_len), 0)
    cols_iota = lax.broadcasted_iota(jnp.int32, (seq_len, seq_len), 1)
    return (doc_full[:, :, None] == doc_full[:, None, :]) & (cols_iota <= rows_iota)[None]


def rms_norm(hidden, norm_gain):
    hidden_f = hidden.astype(jnp.float32)
    inv_rms = lax.rsqrt(jnp.mean(hidden_f * hidden_f, axis=-1, keepdims=True) + NORM_EPS)
    return (hidden_f * inv_rms * norm_gain.astype(jnp.float32)).astype(jnp.bfloat16), inv_rms


def norm_backward(hidden, norm_gain, inv_rms, grad_normed):
    hidden_f = hidden.astype(jnp.float32)
    gain_grad_in = grad_normed * norm_gain.astype(jnp.float32)
    grad_gain = jnp.sum(grad_normed * hidden_f * inv_rms, axis=(0, 1))
    mean_term = jnp.mean(gain_grad_in * hidden_f, axis=-1, keepdims=True)
    grad_hidden = inv_rms * gain_grad_in - hidden_f * (inv_rms * inv_rms * inv_rms) * mean_term
    return grad_hidden, grad_gain


def attention_forward(normed_full, w_query, w_key, w_value, cos_tab, sin_tab, allowed):
    batch_rows = normed_full.shape[0]
    seq_len = normed_full.shape[1]
    kv_heads = w_key.shape[1] // HEAD_DIM
    group_size = w_query.shape[1] // w_key.shape[1]
    query_raw = jnp.einsum('bsd,dn->bsn', normed_full, w_query, preferred_element_type=jnp.float32)
    key_raw = jnp.einsum('bsd,dn->bsn', normed_full, w_key, preferred_element_type=jnp.float32)
    value_raw = jnp.einsum('bsd,dn->bsn', normed_full, w_value, preferred_element_type=jnp.float32)
    query_rot = rotate_pairs(query_raw.reshape(batch_rows, seq_len, kv_heads * group_size, HEAD_DIM), cos_tab, sin_tab)
    query_rot = query_rot.astype(jnp.bfloat16).reshape(batch_rows, seq_len, kv_heads, group_size, HEAD_DIM)
    key_rot = rotate_pairs(key_raw.reshape(batch_rows, seq_len, kv_heads, HEAD_DIM), cos_tab, sin_tab).astype(jnp.bfloat16)
    value_rows = value_raw.astype(jnp.bfloat16).reshape(batch_rows, seq_len, kv_heads, HEAD_DIM)
    scores = jnp.einsum('bqhgd,bkhd->bhgqk', query_rot, key_rot, preferred_element_type=jnp.float32) * (HEAD_DIM ** -0.5)
    attn_probs = jax.nn.softmax(jnp.where(allowed[:, None, None], scores, -1e30), axis=-1)
    probs_low = attn_probs.astype(jnp.bfloat16)
    heads_out = jnp.einsum('bhgqk,bkhd->bqhgd', probs_low, value_rows, preferred_element_type=jnp.float32)
    heads_out = heads_out.astype(jnp.bfloat16).reshape(batch_rows, seq_len, kv_heads * group_size * HEAD_DIM)
    return heads_out, (query_rot, key_rot, value_rows, attn_probs, probs_low)


def attention_backward(normed_full, saved_fwd, grad_heads, w_query, w_key, w_value, cos_tab, sin_tab):
    query_rot, key_rot, value_rows, attn_probs, probs_low = saved_fwd
    batch_rows = query_rot.shape[0]
    seq_len = query_rot.shape[1]
    kv_heads = query_rot.shape[2]
    group_size = query_rot.shape[3]
    grad_o = grad_heads.reshape(batch_rows, seq_len, kv_heads, group_size, HEAD_DIM)
    grad_probs = jnp.einsum('bqhgd,bkhd->bhgqk', grad_o, value_rows, preferred_element_type=jnp.float32)
    grad_value = jnp.einsum('bhgqk,bqhgd->bkhd', probs_low, grad_o, preferred_element_type=jnp.float32)
    row_dot = jnp.sum(attn_probs * grad_probs, axis=-1, keepdims=True)
    grad_scores = (attn_probs * (grad_probs - row_dot) * (HEAD_DIM ** -0.5)).astype(jnp.bfloat16)
    grad_query = jnp.einsum('bhgqk,bkhd->bqhgd', grad_scores, key_rot, preferred_element_type=jnp.float32)
    grad_key = jnp.einsum('bhgqk,bqhgd->bkhd', grad_scores, query_rot, preferred_element_type=jnp.float32)
    grad_query = rotate_pairs(grad_query.reshape(batch_rows, seq_len, kv_heads * group_size, HEAD_DIM), cos_tab, -sin_tab)
    grad_query = grad_query.astype(jnp.bfloat16).reshape(batch_rows, seq_len, kv_heads * group_size * HEAD_DIM)
    grad_key = rotate_pairs(grad_key, cos_tab, -sin_tab).astype(jnp.bfloat16).reshape(batch_rows, seq_len, kv_heads * HEAD_DIM)
    grad_value = grad_value.astype(jnp.bfloat16).reshape(batch_rows, seq_len, kv_heads * HEAD_DIM)
    grad_wq = jnp.einsum('bsd,bsn->dn', normed_full, grad_query, preferred_element_type=jnp.float32)
    grad_wk = jnp.einsum('bsd,bsn->dn', normed_full, grad_key, preferred_element_type=jnp.float32)
    grad_wv = jnp.einsum('bsd,bsn->dn', normed_full, grad_value, preferred_element_type=jnp.float32)
    grad_normed = (jnp.einsum('bsn,dn->bsd', grad_query, w_query, preferred_element_type=jnp.float32)
                   + jnp.einsum('bsn,dn->bsd', grad_key, w_key, preferred_element_type=jnp.float32)
                   + jnp.einsum('bsn,dn->bsd', grad_value, w_value, preferred_element_type=jnp.float32))
    return grad_normed, grad_wq, grad_wk, grad_wv


def sum_scatter_rows(partial, tp_size):
    batch_rows = partial.shape[0]
    seq_len = partial.shape[1]
    pieces = partial.astype(jnp.bfloat16).reshape(batch_rows, tp_size, seq_len // tp_size, partial.shape[2])
    received = lax.all_to_all(pieces, 'tp', 1, 1, tiled=True)
    return jnp.sum(received, axis=1, dtype=jnp.float32)


def solution(mesh):
    tp_size = mesh.shape['tp']

    def device_step(hidden, positions, doc_ids, norm_gain, w_query, w_key, w_value, w_out, grad_out):
        normed, inv_rms = rms_norm(hidden, norm_gain)
        normed_full = lax.all_gather(normed, 'tp', axis=1, tiled=True)
        pos_full = lax.all_gather(positions, 'tp', axis=1, tiled=True)
        doc_full = lax.all_gather(doc_ids, 'tp', axis=1, tiled=True)
        cos_tab, sin_tab = rope_tables(pos_full)
        allowed = attend_mask(doc_full)
        heads_out, saved_fwd = attention_forward(normed_full, w_query, w_key, w_value, cos_tab, sin_tab, allowed)
        partial = jnp.einsum('bsn,nd->bsd', heads_out, w_out, preferred_element_type=jnp.float32)
        attn_rows = sum_scatter_rows(partial, tp_size).astype(jnp.bfloat16)
        attn_out = hidden + attn_rows
        grad_full = lax.all_gather(grad_out, 'tp', axis=1, tiled=True)
        grad_w_out = jnp.einsum('bsn,bsd->nd', heads_out, grad_full, preferred_element_type=jnp.float32)
        grad_heads = jnp.einsum('bsd,nd->bsn', grad_full, w_out, preferred_element_type=jnp.float32).astype(jnp.bfloat16)
        grad_normed_part, grad_wq, grad_wk, grad_wv = attention_backward(normed_full, saved_fwd, grad_heads, w_query, w_key, w_value, cos_tab, sin_tab)
        grad_normed = sum_scatter_rows(grad_normed_part, tp_size)
        grad_norm_in, gain_part = norm_backward(hidden, norm_gain, inv_rms, grad_normed)
        grad_gain = lax.psum(gain_part, 'tp')
        grad_hidden = (grad_out.astype(jnp.float32) + grad_norm_in).astype(jnp.bfloat16)
        return (attn_out, grad_hidden, grad_gain, grad_wq, grad_wk, grad_wv, grad_w_out)

    row_spec = P('dp', 'tp', None)
    tok_spec = P('dp', 'tp')
    col_spec = P(None, 'tp')
    return jax.shard_map(
        device_step, mesh=mesh,
        in_specs=(row_spec, tok_spec, tok_spec, P(), col_spec, col_spec, col_spec, P('tp', None), row_spec),
        out_specs=(row_spec, row_spec, P('dp'), P('dp', 'tp'), P('dp', 'tp'), P('dp', 'tp'), P(('dp', 'tp'), None)),
        check_vma=False)
```

profile of v0, /device:TPU:112, one launch (start us, length us, event | category | flops | bytes accessed | tf_op | source)
XLA Modules:
  0.0 1270.7 jit_solution(7024477036836926010)
XLA Ops:
  7.2 0.1 all-gather.5.cloned.1.call-start
  7.3 3.5 fusion.12
  10.8 0.6 multiply_multiply_fusion
  11.4 0.6 copy-done.23
  12.0 4.1 fusion.14
  16.1 0.1 all-gather.5.cloned.1.call-update
  16.1 0.1 all-gather.7.cloned.1.call-start
  16.2 0.7 all-gather.7.cloned.1.call-update
  17.0 24.6 %all-gather.1 = s32[8,48,16]{1,2,0:T(8,128)S(1)} all-gather(s32[1,48,16]{1,2,0:T(8,128)S(1)} %bitcast.179), channel_id=1, replica_groups=mesh['dp'=2,'tp'=8] {'tp'}, dimensions={0}, use_global_device_ids=true | all-gather | bytes 27648 | tf_op jit(solution)/shard_map/all_gather | solution.py:107
  41.7 0.1 reshape.199
  41.8 22.0 %all-gather = s32[8,48,16]{1,2,0:T(8,128)S(1)} all-gather(s32[1,48,16]{1,2,0:T(8,128)S(1)} %bitcast.180), channel_id=1, replica_groups=mesh['dp'=2,'tp'=8] {'tp'}, dimensions={0}, use_global_device_ids=true | all-gather | bytes 27648 | tf_op jit(solution)/shard_map/all_gather | solution.py:108
  63.8 0.1 reshape.196
  63.9 7.2 fusion.71
  71.2 3.1 compare_and_fusion
  74.3 117.5 %all-gather.5.cloned.1.call-done = bf16[16,384,3072]{2,1,0:T(8,128)(2,1)} async-done(((bf16[16,48,3072]{2,1,0:T(8,128)(2,1)}), bf16[16,384,3072]{2,1,0:T(8,128)(2,1)}) %all-gather.5.cloned.1.call-update) | async-done | bytes 37748752 | tf_op jit(solution)/shard_map/all_gather | solution.py:106
  191.8 19.5 %fusion.67 = f32[16,384,128]{1,2,0:T(8,128)} fusion(bf16[16,384,3072]{2,1,0:T(8,128)(2,1)} %all-gather.5.cloned.1.call-done, bf16[3072,128]{1,0:T(8,128)(2,1)S(1)} %copy-done.15), kind=kOutput, calls=%fused_computation.94 | convolution fusion | flops 4831838208 | bytes 41680896 | tf_op jit(solution)/shard_map/bsd,dn->bsn/dot_general | solution.py:53
  211.4 3.7 copy.117
  215.1 22.3 %fusion.34 = f32[16,384,384]{1,2,0:T(8,128)} fusion(bf16[16,384,3072]{2,1,0:T(8,128)(2,1)} %all-gather.5.cloned.1.call-done, bf16[3072,384]{1,0:T(8,128)(2,1)} %param.13), kind=kOutput, calls=%fused_computation.58 | convolution fusion | flops 14495514624 | bytes 49545216 | tf_op jit(solution)/shard_map/bsd,dn->bsn/dot_general | solution.py:52
  237.4 9.1 copy.118
  246.6 6.6 fusion.55
  253.2 1.3 pad_maximum_fusion.2
  254.6 1.6 subtract_convert_fusion.1
  256.2 0.5 pad_maximum_fusion
  256.8 1.5 copy-done.5
  258.3 14.6 %fusion.6 = (f32[16,3,384]{2,1,0:T(4,128)S(1)}, f32[16,384,384,3]{2,1,3,0:T(8,128)}) fusion(pred[16,384,384]{1,2,0:T(8,128)(4,1)S(1)} %copy-done.5, bf16[16,384,3,128]{1,0,3,2:T(8,128)(2,1)S(1)} %bitcast.165, bf16[16,384,128,1]{1,0,2,3:T(8,128)(2,1)} %bitcast.172), kind=kOutput, calls=%fused_computation.12 | convolution fusion | flops 1833154560 | bytes 37036032 | tf_op jit(solution)/shard_map/bqhgd,bkhd->bhgqk/dot_general | solution.py:59
  272.9 13.6 %fusion.5 = f32[16,3,384]{2,1,0:T(4,128)S(1)} fusion(f32[16,384,384,3]{2,1,3,0:T(8,128)} %get-tuple-element.23, f32[16,3,384]{2,1,0:T(4,128)S(1)} %get-tuple-element.22, pred[16,384,384]{1,2,0:T(8,128)(4,1)S(1)} %copy-done.5), kind=kLoop, calls=%fused_computation.11 | loop fusion | flops 28293120 | bytes 30818304 | tf_op jit(solution)/shard_map/reduce_sum | solution.py:60
  286.5 16.6 %convolution_convert_fusion.2 = bf16[16,384,128]{2,1,0:T(8,128)(2,1)S(1)} fusion(bf16[16,384,3072]{2,1,0:T(8,128)(2,1)} %all-gather.5.cloned.1.call-done, bf16[3072,128]{1,0:T(8,128)(2,1)S(1)} %copy-done.17), kind=kOutput, calls=%fused_computation.74 | convolution fusion | flops 4832624640 | bytes 40108032 | tf_op jit(solution)/shard_map/bsd,dn->bsn/dot_general | solution.py:54
  303.2 16.3 %fusion.27 = bf16[16,128,3,384]{3,1,2,0:T(8,128)(2,1)} fusion(bf16[16,384,128]{2,1,0:T(8,128)(2,1)S(1)} %convolution_convert_fusion.2, f32[16,3,384]{2,1,0:T(4,128)S(1)} %fusion.5, f32[16,3,384]{2,1,0:T(4,128)S(1)} %get-tuple-element.22, f32[16,384,384,3]{2,1,3,0:T(8,128)} %get-tuple-element.23, pred[16,384,384]{1,2,0:T(8,128)(4,1)S(1)} %copy-done.5), kind=kOutput, calls=%fused_computation.53 | convolution fusion | flops 1849688064 | bytes 37109760 | tf_op jit(solution)/shard_map/bhgqk,bkhd->bqhgd/dot_general | solution.py:62
  319.4 26.7 %convolution_convert_fusion = bf16[16,384,3072]{2,1,0:T(8,128)(2,1)} fusion(bf16[16,384,384]{1,2,0:T(8,128)(2,1)} %bitcast.181, bf16[384,3072]{1,0:T(8,128)(2,1)S(1)} %copy-done), kind=kOutput, calls=%fused_computation.13 | convolution fusion | flops 14514388992 | bytes 44826624 | tf_op jit(solution)/shard_map/bsn,nd->bsd/dot_general | solution.py:112
  346.1 25.7 %copy.75 = bf16[16,8,48,3072]{3,2,0,1:T(8,128)(2,1)} copy(bf16[16,8,48,3072]{3,2,1,0:T(8,128)(2,1)} %bitcast.162) | data formatting | bytes 75497472 | tf_op jit(solution)/shard_map/reshape | solution.py:96
  371.8 8.2 all-to-all-start
  380.1 20.6 %convolution_convert_fusion.1 = bf16[16,384,384]{1,2,0:T(8,128)(2,1)} fusion(bf16[16,384,3072]{2,1,0:T(8,128)(2,1)} %all-gather.7.cloned.1.call-done, bf16[384,3072]{1,0:T(8,128)(2,1)S(1)} %copy-done), kind=kOutput, calls=%fused_computation.52 | convolution fusion | flops 14497873920 | bytes 44826624 | tf_op jit(solution)/shard_map/bsd,nd->bsn/dot_general | solution.py:117
  400.7 25.7 %fusion = (f32[16,3,384]{2,1,0:T(4,128)S(1)}, f32[16,384,384,3]{2,1,3,0:T(8,128)}) fusion(f32[16,3,384]{2,1,0:T(4,128)S(1)} %fusion.5, f32[16,3,384]{2,1,0:T(4,128)S(1)} %get-tuple-element.22, f32[16,384,384,3]{2,1,3,0:T(8,128)} %get-tuple-element.23, pred[16,384,384]{1,2,0:T(8,128)(4,1)S(1)} %copy-done.6, bf16[16,384,3,128]{1,3,2,0:T(8,128)(2,1)} %bitcast.183, ...), kind=kOutput, calls=%fused_computation.5 | convolution fusion | flops 1854388224 | bytes 65495040 | tf_op jit(solution)/shard_map/bqhgd,bkhd->bhgqk/dot_general | solution.py:74
  426.4 20.8 %fusion.7 = bf16[16,3,384,384]{2,3,1,0:T(8,128)(2,1)S(1)} fusion(f32[16,384,384,3]{2,1,3,0:T(8,128)} %get-tuple-element.25, f32[16,3,384]{2,1,0:T(4,128)S(1)} %get-tuple-element.24, f32[16,3,384]{2,1,0:T(4,128)S(1)} %fusion.5, f32[16,3,384]{2,1,0:T(4,128)S(1)} %get-tuple-element.22, f32[16,384,384,3]{2,1,3,0:T(8,128)} %get-tuple-element.23, ...), kind=kLoop, calls=%fused_computation.19 | loop fusion | flops 56623104 | bytes 73359360 | tf_op jit(solution)/shard_map/reshape.28
  447.2 5.0 copy-done.2
  452.2 5.5 convolution_bitcast_fusion.4
  457.7 9.3 copy.119
  467.1 1.6 subtract_convert_fusion
  468.7 2.7 pad_maximum_fusion.1
  471.4 7.2 copy.81
  478.6 12.2 fusion.47
  490.8 3.7 copy.120
  494.6 6.7 fusion.51
  501.3 1.3 pad_maximum_fusion.3
  502.6 2.1 copy.86
  504.8 1.1 copy-done.10
  505.9 26.9 %fusion.65 = f32[16,384,3072]{2,1,0:T(8,128)} fusion(bf16[16,384,128]{2,1,0:T(8,128)(2,1)S(1)} %copy.86, bf16[3072,128]{1,0:T(8,128)(2,1)S(1)} %copy-done.16), kind=kOutput, calls=%fused_computation.92 | convolution fusion | flops 4831838208 | bytes 77856768 | tf_op jit(solution)/shard_map/bsn,dn->bsd/dot_general | solution.py:88
  532.8 33.5 %fusion.32 = f32[16,384,3072]{2,1,0:T(8,128)} fusion(bf16[16,384,384]{2,1,0:T(8,128)(2,1)} %copy.81, bf16[3072,384]{1,0:T(8,128)(2,1)} %param.13), kind=kOutput, calls=%fused_computation.56 | convolution fusion | flops 14495514624 | bytes 82575360 | tf_op jit(solution)/shard_map/bsn,dn->bsd/dot_general | solution.py:87
  566.3 16.6 %bitcast_convert_fusion = bf16[16,128,384]{2,1,0:T(8,128)(2,1)} fusion(bf16[16,384,3,128]{1,3,2,0:T(8,128)(2,1)} %bitcast.184, f32[16,3,384]{2,1,0:T(4,128)S(1)} %fusion.5, f32[16,3,384]{2,1,0:T(4,128)S(1)} %get-tuple-element.22, f32[16,384,384,3]{2,1,3,0:T(8,128)} %get-tuple-element.23, pred[16,384,384]{1,2,0:T(8,128)(4,1)S(1)} %copy-done.7), kind=kOutput, calls=%fused_computation.51 | convolution fusion | flops 1848115200 | bytes 37109760 | tf_op jit(solution)/shard_map/bhgqk,bqhgd->bkhd/dot_general | solution.py:75
  582.9 60.5 %add_convert_fusion = bf16[16,384,3072]{2,1,0:T(8,128)(2,1)} fusion(f32[16,384,3072]{2,1,0:T(8,128)} %fusion.32, f32[16,384,3072]{2,1,0:T(8,128)} %fusion.65, bf16[16,128,384]{2,1,0:T(8,128)(2,1)} %bitcast_convert_fusion, bf16[3072,128]{1,0:T(8,128)(2,1)S(1)} %copy-done.18), kind=kOutput, calls=%fused_computation.1 | convolution fusion | flops 4888461312 | bytes 191102976 | tf_op jit(solution)/shard_map/bsn,dn->bsd/dot_general | solution.py:89
  643.4 25.7 %copy.89 = bf16[16,8,48,3072]{3,2,0,1:T(8,128)(2,1)} copy(bf16[16,8,48,3072]{3,2,1,0:T(8,128)(2,1)} %bitcast.161) | data formatting | bytes 75497472 | tf_op jit(solution)/shard_map/reshape | solution.py:96
  669.0 120.0 %all-to-all-done = bf16[16,8,48,3072]{3,2,0,1:T(8,128)(2,1)} async-done(((bf16[16,8,48,3072]{3,2,0,1:T(8,128)(2,1)}), bf16[16,8,48,3072]{3,2,0,1:T(8,128)(2,1)}, u32[]{:S(2)}, u32[]{:S(2)}) %all-to-all-start) | async-done | bytes 37748768 | tf_op jit(solution)/shard_map/all_to_all | solution.py:97
  789.0 7.8 all-to-all-start.1
  796.9 18.3 %convolution_bitcast_fusion.2 = f32[3072,128]{1,0:T(8,128)} fusion(bf16[16,384,3072]{2,1,0:T(8,128)(2,1)} %all-gather.5.cloned.1.call-done, bf16[16,128,384]{2,1,0:T(8,128)(2,1)} %bitcast_convert_fusion), kind=kOutput, calls=%fused_computation.48 | convolution fusion | flops 4831838208 | bytes 40894464 | tf_op jit(solution)/shard_map/bsd,bsn->dn/dot_general | solution.py:86
  815.2 17.6 %convolution_bitcast_fusion.3 = f32[3072,128]{1,0:T(8,128)} fusion(bf16[16,384,3072]{2,1,0:T(8,128)(2,1)} %all-gather.5.cloned.1.call-done, bf16[16,384,128]{2,1,0:T(8,128)(2,1)S(1)} %copy-done.11), kind=kOutput, calls=%fused_computation.49 | convolution fusion | flops 4831838208 | bytes 40894464 | tf_op jit(solution)/shard_map/bsd,bsn->dn/dot_general | solution.py:85
  832.8 25.0 %convolution_bitcast_fusion = f32[3072,384]{1,0:T(8,128)} fusion(bf16[16,384,3072]{2,1,0:T(8,128)(2,1)} %all-gather.5.cloned.1.call-done, bf16[16,384,384]{2,1,0:T(8,128)(2,1)S(1)} %bitcast.168), kind=kOutput, calls=%fused_computation.42 | convolution fusion | flops 14495514624 | bytes 47185920 | tf_op jit(solution)/shard_map/bsd,bsn->dn/dot_general | solution.py:84
  857.8 21.9 %convolution_bitcast_fusion.1 = f32[384,3072]{1,0:T(8,128)} fusion(bf16[16,384,384]{1,2,0:T(8,128)(2,1)} %bitcast.182, bf16[16,384,3072]{2,1,0:T(8,128)(2,1)} %all-gather.7.cloned.1.call-done), kind=kOutput, calls=%fused_computation.43 | convolution fusion | flops 14495514624 | bytes 47185920 | tf_op jit(solution)/shard_map/bsn,bsd->nd/dot_general | solution.py:116
  879.7 15.9 %reduce_sum.68 = bf16[16,48,3072]{2,1,0:T(8,128)(2,1)} reduce(bf16[16,8,48,3072]{3,2,0,1:T(8,128)(2,1)} %all-to-all-done, bf16[]{:T(256)} %constant.23.clone.1), dimensions={1}, to_apply=%region_3.4 | reduce | flops 16515072 | bytes 42467328 | tf_op jit(solution)/shard_map/reduce_sum | solution.py:98
  895.5 8.0 add.52
  903.6 302.3 %all-to-all-done.1 = bf16[16,8,48,3072]{3,2,0,1:T(8,128)(2,1)} async-done(((bf16[16,8,48,3072]{3,2,0,1:T(8,128)(2,1)}), bf16[16,8,48,3072]{3,2,0,1:T(8,128)(2,1)}, u32[]{:S(2)}, u32[]{:S(2)}) %all-to-all-start.1) | async-done | bytes 37748768 | tf_op jit(solution)/shard_map/all_to_all | solution.py:97
  1205.8 16.9 %convert_reduce_fusion = f32[16,48,3072]{2,1,0:T(8,128)} fusion(bf16[16,8,48,3072]{3,2,0,1:T(8,128)(2,1)} %all-to-all-done.1), kind=kLoop, calls=%fused_computation | loop fusion | flops 35389440 | bytes 47185920 | tf_op jit(solution)/shard_map/reduce_sum | solution.py:98
  1222.7 6.6 fusion.21
  1229.3 23.6 %psum.7 = f32[3072]{0:T(1024)} all-reduce(f32[3072]{0:T(1024)S(1)} %get-tuple-element.7), channel_id=1, replica_groups=mesh['dp'=2,'tp'=8] {'tp'}, use_global_device_ids=true, to_apply=%region_8.9 | all-reduce | flops 3072 | bytes 24576 | tf_op jit(solution)/shard_map/psum | solution.py:121
  1253.0 10.7 fusion.18
  (75 shorter events, 0.3 us)
Async XLA Ops:
  7.2 312.2 %copy-start = (bf16[384,3072]{1,0:T(8,128)(2,1)S(1)}, bf16[384,3072]{1,0:T(8,128)(2,1)}, u32[]{:S(2)}) copy-start(bf16[384,3072]{1,0:T(8,128)(2,1)} %param.16) | copy-start | bytes 7077892
  7.2 4.2 copy-start.28
  7.2 184.6 %all-gather.5.cloned.1.call-start = ((), (), s32[]{:S(2)}) async-start(), calls=%async_computation.2 | async-start | bytes 42467328 | tf_op jit(solution)/shard_map/all_gather | solution.py:106
  7.3 4.7 copy-start.3
  11.4 0.6 copy-start.23
  11.4 0.6 copy-start.21
  16.1 0.9 copy-start.26
  16.1 25.7 %copy-start.27 = (s32[16,48]{1,0:T(8,128)S(1)}, s32[16,48]{1,0:T(8,128)}, u32[]{:S(2)}) copy-start(s32[16,48]{1,0:T(8,128)} %param.11) | copy-start | bytes 9220
  16.1 363.9 %all-gather.7.cloned.1.call-start = ((), (), s32[]{:S(2)}) async-start(), calls=%async_computation.3 | async-start | bytes 42467328 | tf_op jit(solution)/shard_map/all_gather | solution.py:115
  17.0 174.9 %copy-start.15 = (bf16[3072,128]{1,0:T(8,128)(2,1)S(1)}, bf16[3072,128]{1,0:T(8,128)(2,1)}, u32[]{:S(2)}) copy-start(bf16[3072,128]{1,0:T(8,128)(2,1)} %param.14) | copy-start | bytes 2359300
  41.7 204.9 %copy-start.19 = (f32[384,16]{0,1:T(8,128)}, f32[384,16]{0,1:T(8,128)S(1)}, u32[]{:S(2)}) copy-start(f32[384,16]{0,1:T(8,128)S(1)} %reshape.199) | copy-start | bytes 73732
  63.9 182.8 %copy-start.29 = (f32[64]{0:T(128)}, f32[64]{0:T(128)S(1)}, u32[]{:S(2)}) copy-start(f32[64]{0:T(128)S(1)} %multiply_power_fusion) | copy-start | bytes 772
  246.6 8.0 copy-start.8
  246.6 8.0 copy-start.14
  256.2 2.0 copy-start.5
  256.8 16.1 %copy-start.4 = (bf16[16,384,3,64,2]{1,0,4,3,2:T(8,128)(2,1)}, bf16[16,384,3,64,2]{1,0,4,3,2:T(8,128)(2,1)S(1)}, u32[]{:S(2)}) copy-start(bf16[16,384,3,64,2]{1,0,4,3,2:T(8,128)(2,1)S(1)} %pad_maximum_fusion) | copy-start | bytes 14155780
  272.9 13.6 %copy-start.17 = (bf16[3072,128]{1,0:T(8,128)(2,1)S(1)}, bf16[3072,128]{1,0:T(8,128)(2,1)}, u32[]{:S(2)}) copy-start(bf16[3072,128]{1,0:T(8,128)(2,1)} %param.15) | copy-start | bytes 2359300
  303.2 16.3 %copy-start.31 = (bf16[16,384,128]{2,1,0:T(8,128)(2,1)}, bf16[16,384,128]{2,1,0:T(8,128)(2,1)S(1)}, u32[]{:S(2)}) copy-start(bf16[16,384,128]{2,1,0:T(8,128)(2,1)S(1)} %convolution_convert_fusion.2) | copy-start | bytes 4718596
  371.8 417.2 %all-to-all-start = ((bf16[16,8,48,3072]{3,2,0,1:T(8,128)(2,1)}), bf16[16,8,48,3072]{3,2,0,1:T(8,128)(2,1)}, u32[]{:S(2)}, u32[]{:S(2)}) async-start(bf16[16,8,48,3072]{3,2,0,1:T(8,128)(2,1)} %copy.75), calls=%async_computation | async-start | bytes 75497472 | tf_op jit(solution)/shard_map/all_to_all | solution.py:97
  380.1 20.6 %copy-start.6 = (pred[16,384,384]{1,2,0:T(8,128)(4,1)S(1)}, pred[16,384,384]{1,2,0:T(8,128)(4,1)}, u32[]{:S(2)}) copy-start(pred[16,384,384]{1,2,0:T(8,128)(4,1)} %compare_and_fusion) | copy-start | bytes 7077892
  380.1 20.6 %copy-start.32 = (bf16[16,384,128]{2,1,0:T(8,128)(2,1)S(1)}, bf16[16,384,128]{2,1,0:T(8,128)(2,1)}, u32[]{:S(2)}) copy-start(bf16[16,384,128]{2,1,0:T(8,128)(2,1)} %copy-done.31) | copy-start | bytes 4718596
  426.4 25.8 %copy-start.12 = (bf16[16,384,1,64,2]{1,0,4,3,2:T(8,128)(2,1)S(1)}, bf16[16,384,1,64,2]{1,0,4,3,2:T(8,128)(2,1)}, u32[]{:S(2)}) copy-start(bf16[16,384,1,64,2]{1,0,4,3,2:T(8,128)(2,1)} %pad_maximum_fusion.2) | copy-start | bytes 4718596
  447.2 5.1 copy-start.2
  457.7 9.3 copy-start.9
  457.7 9.3 copy-start.13
  490.8 3.7 copy-start.20
  490.8 3.7 copy-start.30
  494.6 11.3 copy-start.16
  504.7 1.1 copy-start.10
  532.8 33.5 %copy-start.7 = (pred[16,384,384]{1,2,0:T(8,128)(4,1)S(1)}, pred[16,384,384]{1,2,0:T(8,128)(4,1)}, u32[]{:S(2)}) copy-start(pred[16,384,384]{1,2,0:T(8,128)(4,1)} %compare_and_fusion) | copy-start | bytes 7077892
  566.3 16.6 %copy-start.18 = (bf16[3072,128]{1,0:T(8,128)(2,1)S(1)}, bf16[3072,128]{1,0:T(8,128)(2,1)}, u32[]{:S(2)}) copy-start(bf16[3072,128]{1,0:T(8,128)(2,1)} %param.15) | copy-start | bytes 2359300
  789.0 416.8 %all-to-all-start.1 = ((bf16[16,8,48,3072]{3,2,0,1:T(8,128)(2,1)}), bf16[16,8,48,3072]{3,2,0,1:T(8,128)(2,1)}, u32[]{:S(2)}, u32[]{:S(2)}) async-start(bf16[16,8,48,3072]{3,2,0,1:T(8,128)(2,1)} %copy.89), calls=%async_computation.1 | async-start | bytes 75497472 | tf_op jit(solution)/shard_map/all_to_all | solution.py:97
  796.8 18.4 %copy-start.11 = (bf16[16,384,128]{2,1,0:T(8,128)(2,1)S(1)}, bf16[16,384,128]{2,1,0:T(8,128)(2,1)}, u32[]{:S(2)}) copy-start(bf16[16,384,128]{2,1,0:T(8,128)(2,1)} %copy-done.10) | copy-start | bytes 4718596
  796.8 36.0 %slice-start = ((s8[4718592]{0:T(1024)(128)(4,1)}), s8[524288]{0:T(1024)(128)(4,1)S(1)}, s32[]{:S(2)}) async-start(s8[4718592]{0:T(1024)(128)(4,1)} %bitcast.167), calls=%async_computation.4 | async-start | bytes 1048576
  815.2 17.6 %slice-start.1 = ((s8[4718592]{0:T(1024)(128)(4,1)}), s8[4194304]{0:T(1024)(128)(4,1)S(1)}, s32[]{:S(2)}) async-start(s8[4718592]{0:T(1024)(128)(4,1)} %bitcast.167), calls=%async_computation.5 | async-start | bytes 8388608
  903.5 319.1 %copy-start.22 = (f32[3072]{0:T(1024)S(1)}, f32[3072]{0:T(1024)}, u32[]{:S(2)}) copy-start(f32[3072]{0:T(1024)} %copy-done.21) | copy-start | bytes 36868
  903.6 319.1 %copy-start.24 = (f32[16,48]{1,0:T(8,128)S(1)}, f32[16,48]{1,0:T(8,128)}, u32[]{:S(2)}) copy-start(f32[16,48]{1,0:T(8,128)} %copy-done.23) | copy-start | bytes 9220
  1222.7 30.3 %copy-start.25 = (f32[16,48]{1,0:T(8,128)S(1)}, f32[16,48]{1,0:T(8,128)}, u32[]{:S(2)}) copy-start(f32[16,48]{1,0:T(8,128)} %get-tuple-element.20) | copy-start | bytes 9220
  1253.0 10.7 copy-start.1
Sparse Core Ops, SparseCore 0:
  16.3 175.5 all-gather.4
  193.4 171.0 all-gather.6
where the time goes:
time: 1280 us; the launch traced here: 1270 us
  waiting for transfers between devices  541 us (42%)
  matrix products  400 us (31%)
  other arithmetic  134 us (10%)
  local copies, waits for them, and re-layouts  95.1 us (7%)
  blocking collectives  70.2 us (5%)
  starting transfers between devices  16.1 us (1%)
  between operations  14.8 us (1%)
    all_to_all x2, waiting for transfers between devices, sum_scatter_rows(): received = lax.all_to_all(pieces, 'tp', 1, 1, tiled=True)  422 us
    all_gather x1, waiting for transfers between devices, device_step(): normed_full = lax.all_gather(normed, 'tp', axis=1, tiled=True)  118 us
    dot_general x1, matrix products, attention_backward(): jnp.einsum('bsn,dn->bsd', grad_value, w_value, preferred_element_type=jnp...  60.5 us
    reshape x2, local copies, waits for them, and re-layouts, sum_scatter_rows(): partial.astype(jnp.bfloat16)  51.4 us
    another operation x5, other arithmetic  37.4 us
    dot_general x1, matrix products, attention_backward(): jnp.einsum('bsn,dn->bsd', grad_query, w_query, preferred_element_type=jnp...  33.5 us
    reduce_sum x2, other arithmetic, sum_scatter_rows(): return jnp.sum(received, axis=1, dtype=jnp.float32)  32.7 us
    dot_general x1, matrix products, attention_backward(): jnp.einsum('bsn,dn->bsd', grad_key, w_key, preferred_element_type=jnp.flo...  26.9 us
  transfers between devices with their start and end apart: 4, of which 3 were waited for; matrix products, arithmetic and copies ran while one was open for 46% of the time, Pallas kernels for 0%

commit v1 on v0

v1 whole, which is shorter than its diff:
```python
import functools

import jax
import jax.numpy as jnp
from jax import lax
from jax.experimental import pallas as pl
from jax.experimental.pallas import tpu as pltpu
from jax.sharding import PartitionSpec as P


HEAD_DIM = 128
NORM_EPS = 1e-5
ROPE_BASE = 10000.0
SCALE = HEAD_DIM ** -0.5
LOG2E = 1.4426950408889634
F32 = jnp.float32
BF16 = jnp.bfloat16
NN = (((1,), (0,)), ((), ()))
NT = (((1,), (1,)), ((), ()))
TN = (((0,), (0,)), ((), ()))
VMEM_LIMIT = 63000 * 1024
GROUPS = (1, 3, 0, 2)
SLOT = {g: s for s, g in enumerate(GROUPS)}
ANY = pl.BlockSpec(memory_space=pl.ANY)


def dot(a, b, dims):
    return lax.dot_general(a, b, dims, preferred_element_type=F32)


def cost(flops, size):
    return pl.CostEstimate(flops=int(flops), bytes_accessed=int(size), transcendentals=0)


def swap_pairs(x):
    lane = lax.broadcasted_iota(jnp.int32, x.shape, 1)
    return jnp.where(lane % 2 == 0, pltpu.roll(x, HEAD_DIM - 1, 1), pltpu.roll(x, 1, 1))


def place_kernel(normalize, x_ref, gain_ref, *refs):
    x = x_ref[...]
    if normalize:
        xf = x.astype(F32)
        inv = lax.rsqrt(jnp.mean(xf * xf, axis=-1, keepdims=True) + NORM_EPS)
        x = (xf * inv * gain_ref[...]).astype(BF16)
    refs[-1][...] = x


def place(x, gain, buf, at, axis, normalize=False):
    rows, width = x.shape
    steps = 4
    tile = rows // steps
    shape = (4 * rows, width) if axis == 0 else (rows, 4 * width)
    where = (lambda m: (at * steps + m, 0)) if axis == 0 else (lambda m: (m, at))
    ops, specs, alias = (x, gain), [pl.BlockSpec((tile, width), lambda m: (m, 0)), pl.BlockSpec(gain.shape, lambda m: (0, 0))], {}
    if buf is not None:
        ops, specs, alias = ops + (buf,), specs + [ANY], {2: 0}
    return pl.pallas_call(
        functools.partial(place_kernel, normalize), grid=(steps,), in_specs=specs, out_specs=pl.BlockSpec((tile, width), where),
        out_shape=jax.ShapeDtypeStruct(shape, BF16), input_output_aliases=alias,
        cost_estimate=cost(1000 * rows * width, 4 * rows * width), name="place")(*ops)


def proj_kernel(turned, x_ref, w_ref, cos_ref, sin_ref, o_ref):
    chunk = x_ref.shape[0] // 4
    for m in range(4):
        rows = slice(m * chunk, (m + 1) * chunk)
        acc = dot(x_ref[rows], w_ref[...], NN)
        for h in range(acc.shape[1] // HEAD_DIM):
            cols = slice(h * HEAD_DIM, (h + 1) * HEAD_DIM)
            part = acc[:, cols]
            if h < turned:
                part = part * cos_ref[rows] + swap_pairs(part) * sin_ref[rows]
            o_ref[rows, cols] = part.astype(BF16)


def project(x, w, cos, sin, first, count, turned):
    rows, width = x.shape
    tile = 2 * HEAD_DIM
    whole = lambda a: pl.BlockSpec(a.shape, lambda n: (0, 0))
    return pl.pallas_call(
        functools.partial(proj_kernel, turned), grid=(count,),
        in_specs=[whole(x), pl.BlockSpec((width, tile), lambda n: (0, first + n)), whole(cos), whole(sin)],
        out_specs=pl.BlockSpec((rows, tile), lambda n: (0, n)),
        out_shape=jax.ShapeDtypeStruct((rows, count * tile), BF16),
        compiler_params=pltpu.CompilerParams(vmem_limit_bytes=VMEM_LIMIT),
        cost_estimate=cost(2 * rows * width * count * tile, 2 * rows * width), name="project")(x, w, cos, sin)


def token_rows(ref, b):
    x = ref[:, b] if len(ref.shape) == 4 else ref[b]
    return x.reshape(-1, x.shape[-1])


def by_head(x):
    return jnp.concatenate([x[:, h * HEAD_DIM:(h + 1) * HEAD_DIM] for h in range(x.shape[1] // HEAD_DIM)], axis=0)


def allowed_block(qi_ref, ki_ref, b):
    kidx = ki_ref[...]
    return (kidx <= qi_ref[b, :, 0:1]) & (kidx >= qi_ref[b, :, 1:2])


def probs(q, k, ok):
    s = dot(q, k, NT).reshape(-1, ok.shape[0], ok.shape[1])
    s = jnp.where(ok[None], s, -1e30)
    e = jnp.exp2((s - jnp.max(s, axis=-1, keepdims=True)) * (SCALE * LOG2E))
    return e * (1.0 / jnp.sum(e, axis=-1, keepdims=True))


def keys_values(kr_ref, kv_ref, b):
    kv = jnp.concatenate([token_rows(kr_ref, b), token_rows(kv_ref, b)], axis=0)
    return kv[:, :HEAD_DIM], kv[:, HEAD_DIM:]


def attn_fwd_kernel(q_ref, kv_ref, kr_ref, qi_ref, ki_ref, *refs):
    o_ref = refs[-1]
    shape = (o_ref.shape[0], o_ref.shape[2], HEAD_DIM)
    for b in range(q_ref.shape[1]):
        ok = allowed_block(qi_ref, ki_ref, b)
        k, v = keys_values(kr_ref, kv_ref, b)
        p = probs(by_head(token_rows(q_ref, b)), k, ok).astype(BF16).reshape(-1, k.shape[0])
        o = dot(p, v, NN).astype(BF16)
        toks = ok.shape[0]
        for h in range(o.shape[0] // toks):
            o_ref[:, b, :, h * HEAD_DIM:(h + 1) * HEAD_DIM] = o[h * toks:(h + 1) * toks].reshape(shape)


def attn_bwd_kernel(n_alias, q_ref, kv_ref, kr_ref, do0_ref, do1_ref, do2_ref, do3_ref, qi_ref, ki_ref, cos_ref, sin_ref, cosr_ref, sinr_ref, *refs):
    dq_ref, dkv_ref, dkr_ref = refs[n_alias:]
    shape = (dq_ref.shape[0], dq_ref.shape[2], HEAD_DIM)
    for b in range(q_ref.shape[1]):
        ok = allowed_block(qi_ref, ki_ref, b)
        toks = ok.shape[0]
        q = by_head(token_rows(q_ref, b))
        do = by_head(jnp.concatenate([token_rows(d, b) for d in (do0_ref, do1_ref, do2_ref, do3_ref)], axis=0))
        k, v = keys_values(kr_ref, kv_ref, b)
        p = probs(q, k, ok)
        dp = dot(do, v, NT).reshape(p.shape)
        p_low = p.astype(BF16).reshape(-1, k.shape[0])
        dv = dot(p_low, do, TN)
        ds = (p * (dp - jnp.sum(p * dp, axis=-1, keepdims=True))).astype(BF16).reshape(p_low.shape)
        dq = dot(ds, k, NN) * SCALE
        dk = dot(ds, q, TN) * SCALE
        cos, sin = token_rows(cos_ref, b), token_rows(sin_ref, b)
        for h in range(dq.shape[0] // toks):
            part = dq[h * toks:(h + 1) * toks]
            dq_ref[:, b, :, h * HEAD_DIM:(h + 1) * HEAD_DIM] = (part * cos - swap_pairs(part) * sin).astype(BF16).reshape(shape)
        dk_r, dk_l = dk[:toks], dk[toks:]
        dkv_ref[:, b, :, :HEAD_DIM] = (dk_l * cos - swap_pairs(dk_l) * sin).reshape(shape)
        dkv_ref[:, b, :, HEAD_DIM:] = dv[toks:].reshape(shape)
        dkr_ref[:, b, :, :HEAD_DIM] = (dk_r * token_rows(cosr_ref, b) - swap_pairs(dk_r) * token_rows(sinr_ref, b)).astype(BF16).reshape(shape)
        dkr_ref[:, b, :, HEAD_DIM:] = dv[:toks].astype(BF16).reshape(shape)


ROWS_PER_STEP = 2


def block_at(pieces, span, width, col):
    return pl.BlockSpec((pieces, ROWS_PER_STEP, span, width), lambda b: (0, b, 0, col))


def attn_specs(group, q_cols, pieces, span):
    toks = pieces * span
    s, t = SLOT[group], SLOT[group ^ 2]
    kv_cols = 2 * HEAD_DIM
    return ([block_at(pieces, span, q_cols, s), block_at(pieces, span, kv_cols, s % 2), block_at(pieces, span, kv_cols, t % 2)],
            [pl.BlockSpec((ROWS_PER_STEP, toks, 2), lambda b: (b, 0, 0)), pl.BlockSpec((1, 2 * toks), lambda b: (0, 0))])


def attn_forward(group, q, kv, kvr, qinfo, kinfo, buf):
    pieces, rows, span, q_all = q.shape
    q_cols, toks = q_all // 4, pieces * span
    big, info = attn_specs(group, q_cols, pieces, span)
    ops, specs, alias = (q, kv, kvr, qinfo, kinfo), big + info, {}
    if buf is not None:
        ops, specs, alias = ops + (buf,), specs + [ANY], {5: 0}
    return pl.pallas_call(
        attn_fwd_kernel, grid=(rows // ROWS_PER_STEP,), in_specs=specs, out_specs=block_at(pieces, span, q_cols, SLOT[group]),
        out_shape=jax.ShapeDtypeStruct(q.shape, BF16), input_output_aliases=alias,
        compiler_params=pltpu.CompilerParams(vmem_limit_bytes=VMEM_LIMIT),
        cost_estimate=cost(8 * rows * toks * toks * q_cols, 8 * rows * toks * q_cols), name="attn_fwd")(*ops)


def attn_backward(group, q, kv, kvr, dos, qinfo, kinfo, tabs, bufs):
    pieces, rows, span, q_all = q.shape
    q_cols, toks, s = q_all // 4, pieces * span, SLOT[group]
    kv_cols = 2 * HEAD_DIM
    big, info = attn_specs(group, q_cols, pieces, span)
    do_spec = pl.BlockSpec((ROWS_PER_STEP, span, q_cols), lambda b: (b, 0, s))
    ops = (q, kv, kvr, *dos, qinfo, kinfo, *tabs)
    specs, alias = big + [do_spec] * 4 + info + [block_at(pieces, span, HEAD_DIM, 0)] * 4, {}
    n_alias = 0
    for i, buf in enumerate(bufs):
        if buf is not None:
            alias[len(ops)] = i
            ops, specs, n_alias = ops + (buf,), specs + [ANY], n_alias + 1
    half = (pieces, rows, span, 2 * kv_cols)
    return pl.pallas_call(
        functools.partial(attn_bwd_kernel, n_alias), grid=(rows // ROWS_PER_STEP,), in_specs=specs,
        out_specs=[block_at(pieces, span, q_cols, s), block_at(pieces, span, kv_cols, s % 2), block_at(pieces, span, kv_cols, s % 2)],
        out_shape=[jax.ShapeDtypeStruct(q.shape, BF16), jax.ShapeDtypeStruct(half, F32), jax.ShapeDtypeStruct(half, BF16)],
        input_output_aliases=alias, compiler_params=pltpu.CompilerParams(vmem_limit_bytes=VMEM_LIMIT),
        cost_estimate=cost(20 * rows * toks * toks * q_cols, 20 * rows * toks * q_cols), name="attn_bwd")(*ops)


def grad_in_kernel(dq_ref, da_ref, db_ref, wq_ref, wkv_ref, first_ref, second_ref):
    half = da_ref.shape[1]
    out = dot(dq_ref[...], wq_ref[...], NT) + dot(da_ref[...], wkv_ref[:, :half], NT) + dot(db_ref[...], wkv_ref[:, half:], NT)
    rows = first_ref.shape[0]
    first_ref[...] = out[:rows].astype(first_ref.dtype)
    second_ref[...] = out[rows:].astype(second_ref.dtype)


def grad_in(dq, da, db, wq, wkv, pair_at, types):
    rows, tile = dq.shape[0] // 2, 2 * HEAD_DIM
    half = lambda a: pl.BlockSpec((rows, a.shape[1]), lambda n: (pair_at, 0))
    row = lambda a: pl.BlockSpec((tile, a.shape[1]), lambda n: (n, 0))
    out = pl.BlockSpec((rows // 2, tile), lambda n: (0, n))
    width = wq.shape[0]
    return pl.pallas_call(
        grad_in_kernel, grid=(width // tile,), in_specs=[half(dq), half(da), half(db), row(wq), row(wkv)], out_specs=[out, out],
        out_shape=[jax.ShapeDtypeStruct((rows // 2, width), t) for t in types],
        compiler_params=pltpu.CompilerParams(vmem_limit_bytes=VMEM_LIMIT),
        cost_estimate=cost(2 * rows * width * (wq.shape[1] + wkv.shape[1]), 4 * rows * width), name="grad_in")(dq, da, db, wq, wkv)


def head_out_kernel(h_ref, w_ref, first_ref, second_ref):
    out = dot(h_ref[...], w_ref[...], NN)
    rows = first_ref.shape[0]
    first_ref[...] = out[:rows].astype(first_ref.dtype)
    second_ref[...] = out[rows:].astype(second_ref.dtype)


def head_out(heads, w, pair_at, types):
    rows, inner, width, tile = heads.shape[0] // 2, heads.shape[1], w.shape[1], 4 * HEAD_DIM
    out = pl.BlockSpec((rows // 2, tile), lambda n: (0, n))
    return pl.pallas_call(
        head_out_kernel, grid=(width // tile,),
        in_specs=[pl.BlockSpec((rows, inner), lambda n: (pair_at, 0)), pl.BlockSpec((inner, tile), lambda n: (0, n))], out_specs=[out, out],
        out_shape=[jax.ShapeDtypeStruct((rows // 2, width), t) for t in types],
        compiler_params=pltpu.CompilerParams(vmem_limit_bytes=VMEM_LIMIT),
        cost_estimate=cost(2 * rows * width * inner, 4 * rows * width), name="head_out")(heads, w)


def residual_kernel(x_ref, a_ref, b_ref, *refs):
    total = a_ref[...].astype(F32) + b_ref[...].astype(F32)
    refs[-1][...] = (x_ref[...].astype(F32) + total.astype(BF16).astype(F32)).astype(BF16)


def norm_back_kernel(x_ref, g_ref, a_ref, b_ref, gain_ref, *refs):
    gh_ref, part_ref = refs[-2:]
    tile, width = x_ref.shape
    chunk = 2 * HEAD_DIM
    cuts = [slice(c, c + chunk) for c in range(0, width, chunk)]

    @pl.when(pl.program_id(0) == 0)
    def _():
        part_ref[...] = jnp.zeros_like(part_ref)

    def load(cols):
        return x_ref[:, cols].astype(F32), a_ref[:, cols].astype(F32) + b_ref[:, cols].astype(F32)

    square, cross = jnp.zeros((tile, chunk), F32), jnp.zeros((tile, chunk), F32)
    for cols in cuts:
        x, gn = load(cols)
        square += x * x
        cross += gn * gain_ref[:, cols] * x
    inv = lax.rsqrt(jnp.sum(square, axis=-1, keepdims=True) / width + NORM_EPS)
    slope = inv * inv * inv * (jnp.sum(cross, axis=-1, keepdims=True) / width)
    for cols in cuts:
        x, gn = load(cols)
        scaled = gn * inv
        gh_ref[:, cols] = (g_ref[:, cols].astype(F32) + (scaled * gain_ref[:, cols] - x * slope)).astype(BF16)
        part_ref[:, cols] += jnp.sum((scaled * x).reshape(-1, 8, chunk), axis=0)


def half_rows_call(kernel, half, arrays, gain, buf, out_shape, with_part):
    rows, width = arrays[-1].shape
    steps = 4
    tile = rows // steps
    mine = pl.BlockSpec((tile, width), lambda m, h: (m, 0))
    full = pl.BlockSpec((tile, width), lambda m, h: (h[0] * steps + m, 0))
    specs = [full if a.shape[0] == out_shape[0] else mine for a in arrays]
    ops, alias = tuple(arrays), {}
    if gain is not None:
        ops, specs = ops + (gain,), specs + [pl.BlockSpec(gain.shape, lambda m, h: (0, 0))]
    if buf is not None:
        alias = {1 + len(ops): 0}
        ops, specs = ops + (buf,), specs + [ANY]
    outs, out_specs = [jax.ShapeDtypeStruct(out_shape, BF16)], [full]
    if with_part:
        outs.append(jax.ShapeDtypeStruct((8, width), F32))
        out_specs.append(pl.BlockSpec((8, width), lambda m, h: (0, 0)))

    def body(h_ref, *refs):
        kernel(*refs)

    return pl.pallas_call(
        body, grid_spec=pltpu.PrefetchScalarGridSpec(num_scalar_prefetch=1, grid=(steps,), in_specs=specs, out_specs=out_specs),
        out_shape=outs, input_output_aliases=alias, cost_estimate=cost(1000 * rows * width, 10 * rows * width))(half, *ops)


def solution(mesh):
    tp = mesh.shape['tp']
    chips = tp // 2
    mirror = [2 * (chips - 1 - i // 2) + i % 2 for i in range(tp)]
    mates = [[(i, i ^ r) for i in range(tp)] for r in range(4)]
    far = [[(mirror[i] ^ r, i) for i in range(tp)] for r in range(4)]
    pair = list(enumerate(mirror))
    later = [(i, j) for i, j in pair if i < j]
    earlier = [(i, j) for i, j in pair if i > j]

    def send(x, perm):
        return lax.ppermute(x, 'tp', perm)

    def device_step(hidden, positions, doc_ids, norm_gain, w_query, w_key, w_value, w_out, grad_out):
        last = []

        def run(fn, *args):
            if last:
                *args, _ = lax.optimization_barrier((*args, last[0]))
            out = fn(*args)
            last[:] = [jax.tree.leaves(out)[0]]
            return out

        def after(x):
            return lax.optimization_barrier((x, last[0]))[0]

        me = lax.axis_index('tp')
        core = me % 2
        all_rows, span, width = hidden.shape
        rows = all_rows // 2
        toks = 4 * span
        q_cols = w_query.shape[1]
        split = lambda x: (lax.dynamic_slice_in_dim(x, core * rows, rows), lax.dynamic_slice_in_dim(x, (1 - core) * rows, rows))
        four = lambda x: x.reshape(4, rows, span, x.shape[-1])
        flat = lambda x: x.reshape(-1, x.shape[-1])

        hid_mine, hid_other = split(hidden)
        hid2 = send(hid_mine, mates[2])
        hid1 = send(hid_other, mates[1])
        w_kv = jnp.concatenate([w_key, w_value], axis=1)
        wkv2 = send(w_kv, pair)
        wkv1 = send(w_kv, mates[1])
        wq1 = send(w_query, mates[1])
        pos_mine, pos_other = split(positions)
        by_piece = (pos_mine, pos_other, pos_mine, pos_other)
        pos_loc = [pos_mine] + [send(by_piece[p], mates[p]) for p in (1, 2, 3)]
        pos_rem = [send(by_piece[p], far[p]) for p in range(4)]
        wq2 = send(w_query, pair)
        hid3 = send(hid_other, mates[3])
        wo1 = send(w_out, mates[1])
        wo2 = send(w_out, pair)
        g_mine, g_other = split(grad_out)
        grd1 = send(g_other, mates[1])
        grd2 = send(g_mine, mates[2])
        grd3 = send(g_other, mates[3])

        gain_row = norm_gain.astype(F32)[None]

        def put(x, buf, at, axis, normalize=False):
            if buf is None:
                return run(lambda x_: place(x_, gain_row, None, at, axis, normalize), x)
            return run(lambda x_, b: place(x_, gain_row, b, at, axis, normalize), x, buf)

        wq_all = put(w_query, None, SLOT[0], 1)
        wkv_all = put(w_kv, None, SLOT[0], 1)
        wo_all = put(w_out, None, SLOT[0], 0)
        normed = put(flat(hid_mine), None, 0, 0, True)
        grads = put(flat(g_mine), None, 0, 0)
        normed = put(flat(hid1), normed, 1, 0, True)
        wkv_all = put(wkv1, wkv_all, SLOT[1], 1)
        wq_all = put(wq1, wq_all, SLOT[1], 1)
        wo_all = put(wo1, wo_all, SLOT[1], 0)
        grads = put(flat(grd1), grads, 1, 0)
        wkv3 = send(after(wkv2), mates[1])
        wkv_all = put(wkv2, wkv_all, SLOT[2], 1)
        wkv_all = put(wkv3, wkv_all, SLOT[3], 1)
        normed = put(flat(hid2), normed, 2, 0, True)

        pos_loc, pos_rem = jnp.stack(pos_loc), jnp.stack(pos_rem)
        pos_loc, pos_rem = after((pos_loc, pos_rem))
        idx_of = lambda dev: (jnp.stack([dev ^ p for p in range(4)])[:, None] * span + jnp.arange(span)).astype(jnp.int32)
        q_idx, r_idx = idx_of(me), idx_of(2 * (chips - 1 - me // 2) + core)
        q_full = jnp.broadcast_to(q_idx[:, None, :], pos_loc.shape)
        qinfo = jnp.stack([q_full, q_full - pos_loc], axis=-1)
        qinfo = jnp.moveaxis(qinfo, 1, 0).reshape(rows, toks, 2)
        kinfo = jnp.concatenate([r_idx.reshape(1, toks), q_idx.reshape(1, toks)], axis=1)
        inv_freq = ROPE_BASE ** (-jnp.arange(0, HEAD_DIM, 2, dtype=F32) / HEAD_DIM)
        lane_freq = jnp.repeat(inv_freq, 2)
        lane_sign = jnp.where(jnp.arange(HEAD_DIM) % 2 == 0, -1.0, 1.0).astype(F32)

        def tables(pos):
            ang = pos.astype(F32)[..., None] * lane_freq
            return jnp.cos(ang), jnp.sin(ang) * lane_sign

        cos_l, sin_l = tables(pos_loc)
        cos_r, sin_r = tables(pos_rem)
        cos2, sin2 = flat(cos_l), flat(sin_l)
        cos2, sin2, qinfo, kinfo, cos_r, sin_r = lax.optimization_barrier((cos2, sin2, qinfo, kinfo, cos_r, sin_r))
        last[:] = [cos2]
        tabs = (four(cos2), four(sin2), cos_r, sin_r)

        wq3 = send(after(wq2), mates[1])
        wq_all = put(wq2, wq_all, SLOT[2], 1)
        wq_all = put(wq3, wq_all, SLOT[3], 1)
        normed = put(flat(hid3), normed, 3, 0, True)

        kvs, kv_in = [], []
        for i in range(2):
            kv = four(run(lambda x, w: project(x, w, cos2, sin2, 2 * i, 2, 1), normed, wkv_all))
            kvs.append(kv)
            kv_in.append(send(kv, later))
        q_all = four(run(lambda x, w: project(x, w, cos2, sin2, 0, 2 * q_cols // HEAD_DIM, 2), normed, wq_all))
        wo3 = send(after(wo2), mates[1])
        wo_all = put(wo2, wo_all, SLOT[2], 0)
        wo_all = put(wo3, wo_all, SLOT[3], 0)
        head_grad = lambda g, w: dot(g, w, NT).astype(BF16).reshape(rows, span, -1)
        dos = [run(head_grad, flat(g), wo_all) for g in (g_mine, grd1, grd2)]
        grads = put(flat(grd2), grads, 2, 0)
        heads = None
        for g in GROUPS:
            local, far_in = kvs[SLOT[g] // 2], kv_in[SLOT[g ^ 2] // 2]
            if heads is None:
                heads = run(lambda q, kv, kr: attn_forward(g, q, kv, kr, qinfo, kinfo, None), q_all, local, far_in)
            else:
                heads = run(lambda q, kv, kr, h: attn_forward(g, q, kv, kr, qinfo, kinfo, h), q_all, local, far_in, heads)
        heads_flat = flat(heads)
        att = [None] * 4
        out2, out3 = run(lambda h, w: head_out(h, w, 1, (BF16, BF16)), heads_flat, wo_all)
        att[2], att[3] = send(out2, mates[2]), send(out3, mates[3])
        own_out, out1 = run(lambda h, w: head_out(h, w, 0, (F32, BF16)), heads_flat, wo_all)
        att[1] = send(out1, mates[1])

        dos.append(run(head_grad, flat(grd3), wo_all))
        dq, dkv, dkr, dkv_in = None, [None, None], [None, None], [None, None]
        for g in GROUPS:
            i = SLOT[g] // 2
            bufs = [b for b in (dq, dkv[i], dkr[i]) if b is not None]
            given = tuple(b is not None for b in (dq, dkv[i], dkr[i]))

            def fn(q, kv, kr, d0, d1, d2, d3, *rest):
                it = iter(rest)
                return attn_backward(g, q, kv, kr, (d0, d1, d2, d3), qinfo, kinfo, tabs, [next(it) if ok else None for ok in given])

            dq, dkv[i], dkr[i] = run(fn, q_all, kvs[i], kv_in[SLOT[g ^ 2] // 2], *dos, *bufs)
            if SLOT[g] % 2 == 1:
                dkv_in[i] = send(dkr[i], earlier)

        def add_far(mine, theirs):
            swapped = jnp.concatenate([theirs[..., 2 * HEAD_DIM:], theirs[..., :2 * HEAD_DIM]], axis=-1)
            return flat((mine + swapped.astype(F32)).astype(BF16))

        grads = put(flat(grd3), grads, 3, 0)
        cut = lambda x, s, n: x[:, s * q_cols:(s + n) * q_cols]
        so13 = send(run(lambda h, g: dot(cut(h, 0, 2), g, TN).astype(BF16), heads_flat, grads), mates[1])
        dq_flat = flat(dq)
        low = lambda x: x.astype(BF16)
        spq13 = send(run(lambda d, n: low(dot(n, cut(d, 0, 2), TN)), dq_flat, normed), mates[1])
        dkv_a = run(add_far, dkv[0], dkv_in[0])
        spk13 = send(run(lambda d, n: low(dot(n, d, TN)), dkv_a, normed), mates[1])
        so1, so3 = run(lambda e: (e[:q_cols], e[q_cols:]), so13)
        so2 = send(run(lambda h, gg, e: (dot(cut(h, 3, 1), gg, TN) + e.astype(F32)).astype(BF16), heads_flat, grads, so3), pair)
        mine_half, other_half = core.astype(jnp.int32)[None], (1 - core).astype(jnp.int32)[None]
        flat_shape = (all_rows * span, width)
        hid_flat, g_flat = flat(hidden), flat(grad_out)
        dkv_b = run(add_far, dkv[1], dkv_in[1])
        both = run(lambda d, a, b, wq, wk: grad_in(d, a, b, wq, wk, 1, (BF16, BF16)), dq_flat, dkv_a, dkv_b, wq_all, wkv_all)
        gn2, gn3 = send(both[0], mates[2]), send(both[1], mates[3])
        spq2 = send(run(lambda d, n, e: low(dot(n, cut(d, 3, 1), TN) + e[:, q_cols:].astype(F32)), dq_flat, normed, spq13), pair)
        kv_half = 2 * HEAD_DIM
        spk2 = send(run(lambda d, n, e: low(dot(n, d[:, kv_half:], TN) + e[:, kv_half:].astype(F32)), dkv_b, normed, spk13), pair)
        own_in, gn1 = run(lambda d, a, b, wq, wk: grad_in(d, a, b, wq, wk, 0, (F32, BF16)), dq_flat, dkv_a, dkv_b, wq_all, wkv_all)
        gn1 = send(gn1, mates[1])
        attn_out = run(lambda x, a, b: half_rows_call(residual_kernel, mine_half, (x, a, b), None, None, flat_shape, False)[0], hid_flat, own_out, flat(att[2]))
        attn_out = run(lambda x, a, b, o: half_rows_call(residual_kernel, other_half, (x, a, b), None, o, flat_shape, False)[0], hid_flat, flat(att[1]), flat(att[3]), attn_out)
        back_call = lambda h, arrays, buf: half_rows_call(norm_back_kernel, h, arrays, gain_row, buf, flat_shape, True)
        grad_hidden, part_a = run(lambda x, g, a, b: back_call(mine_half, (x, g, a, b), None), hid_flat, g_flat, own_in, gn2)
        dwo = run(lambda h, g, a, b: dot(cut(h, 2, 1), g, TN) + a.astype(F32) + b.astype(F32), heads_flat, grads, so1, so2)
        own_q = after(run(lambda d, n, e: dot(n, cut(d, 2, 1), TN) + e[:, :q_cols].astype(F32), dq_flat, normed, spq13))
        own_kv = after(run(lambda d, n, e: dot(n, d[:, :kv_half], TN) + e[:, :kv_half].astype(F32), dkv_b, normed, spk13))
        grad_hidden, part_b = run(lambda x, g, a, b, o: back_call(other_half, (x, g, a, b), o), hid_flat, g_flat, gn1, gn3, grad_hidden)
        gain_sum = jnp.sum(part_a + part_b, axis=0).reshape(-1, HEAD_DIM)
        for perm in (mates[1], mates[2], pair):
            gain_sum = gain_sum + send(gain_sum, perm)
        dwq = own_q + spq2.astype(F32)
        dwk = own_kv[:, :HEAD_DIM] + spk2[:, :HEAD_DIM].astype(F32)
        dwv = own_kv[:, HEAD_DIM:] + spk2[:, HEAD_DIM:].astype(F32)
        return attn_out.reshape(hidden.shape), grad_hidden.reshape(hidden.shape), gain_sum.reshape(-1), dwq, dwk, dwv, dwo

    row_spec = P('dp', 'tp', None)
    tok_spec = P('dp', 'tp')
    col_spec = P(None, 'tp')
    return jax.shard_map(
        device_step, mesh=mesh,
        in_specs=(row_spec, tok_spec, tok_spec, P(), col_spec, col_spec, col_spec, P('tp', None), row_spec),
        out_specs=(row_spec, row_spec, P('dp'), P('dp', 'tp'), P('dp', 'tp'), P('dp', 'tp'), P(('dp', 'tp'), None)),
        check_vma=False)
```

time: 1280 us -> 777 us (0.61)
  Pallas kernels: 0 us -> 298 us
  matrix products: 400 us -> 106 us
  waiting for transfers between devices: 541 us -> 282 us
  other arithmetic: 134 us -> 28 us
  local copies, waits for them, and re-layouts: 95.1 us -> 15.1 us
  blocking collectives: 70.2 us -> 0 us
  starting transfers between devices: 16.1 us -> 34 us
  between operations: 14.8 us -> 1.37 us
    all_to_all x2 -> x0, waiting for transfers between devices: 422 us -> none  [sum_scatter_rows(): received = lax.all_to_all(pieces, 'tp', 1, 1, tiled=True)]
    pallas_call x0 -> x39, Pallas kernels: none -> 298 us  [the longest x20 80.5 us: place(): pl.pallas_call(functools.partial(place_kernel, normalize), grid=(steps,),...]
    dot_general x18 -> x13, matrix products: 400 us -> 106 us  [dot(): return lax.dot_general(a, b, dims, preferred_element_type=F32)]
    ppermute x0 -> x41, waiting for transfers between devices: none -> 282 us  [send(): return lax.ppermute(x, 'tp', perm)]
    all_gather x2 -> x0, waiting for transfers between devices: 118 us -> none  [the longest x1 118 us: device_step(): normed_full = lax.all_gather(normed, 'tp', axis=1, tiled=True)]
    reduce_sum x5 -> x1, other arithmetic: 56.4 us -> 0.93 us  [device_step(): gain_sum = jnp.sum(part_a + part_b, axis=0).reshape(-1, HEAD_DIM)]
    reshape x3 -> x0, local copies, waits for them, and re-layouts: 55.1 us -> none  [the longest x2 51.4 us: sum_scatter_rows(): partial.astype(jnp.bfloat16)]
    all_gather x2 -> x0, blocking collectives: 46.6 us -> none  [the longest x1 24.6 us: device_step(): pos_full = lax.all_gather(positions, 'tp', axis=1, tiled=True)]
  transfers between devices with their start and end apart: 4 -> 41, of which waited for: 3 -> 16; matrix products, arithmetic and copies ran while one was open for 46% -> 16% of each run, Pallas kernels for 0% -> 31%
where the time goes in v1:
time: 777 us; the launch traced here: 765 us
  Pallas kernels  298 us (38%)
  waiting for transfers between devices  282 us (36%)
  matrix products  106 us (14%)
  starting transfers between devices  34 us (4%)
  other arithmetic  28 us (4%)
  local copies, waits for them, and re-layouts  15.1 us (2%)
    ppermute x41, waiting for transfers between devices, send(): return lax.ppermute(x, 'tp', perm)  282 us
    dot_general x13, matrix products, dot(): return lax.dot_general(a, b, dims, preferred_element_type=F32)  106 us
    pallas_call x20, Pallas kernels, place(): pl.pallas_call(functools.partial(place_kernel, normalize), grid=(steps,),...  80.5 us
    pallas_call x4, Pallas kernels, attn_backward(): pl.pallas_call(functools.partial(attn_bwd_kernel, n_alias), grid=(rows //...  54.1 us
    pallas_call x3, Pallas kernels, project(): pl.pallas_call(functools.partial(proj_kernel, turned), grid=(count,), in_...  45.5 us
    pallas_call x2, Pallas kernels, grad_in(): pl.pallas_call(grad_in_kernel, grid=(width // tile,), in_specs=[half(dq),...  37.5 us
    ppermute x41, starting transfers between devices, send(): return lax.ppermute(x, 'tp', perm)  34 us
    pallas_call x4, Pallas kernels, attn_forward(): pl.pallas_call(attn_fwd_kernel, grid=(rows // ROWS_PER_STEP,), in_specs=s...  30 us
  transfers between devices with their start and end apart: 41, of which 16 were waited for; matrix products, arithmetic and copies ran while one was open for 16% of the time, Pallas kernels for 31%

profile of v1, /device:TPU:112, one launch (start us, length us, event | category | flops | bytes accessed | tf_op | source)
XLA Modules:
  0.0 764.7 jit_solution(17433957462241897994)
XLA Ops:
  4.8 4.4 constant_dynamic-slice_fusion.4
  13.0 3.9 collective-permute-start.3
  17.4 4.0 place.20.refs_0_
  25.1 4.0 place.22.refs_0_
  29.2 4.4 place.23.refs_0_
  33.7 3.9 place.24.refs_0_
  37.6 4.4 place.25.refs_0_
  45.7 3.9 place.27.refs_0_
  49.6 3.9 place.28.refs_0_
  53.5 4.0 place.29.refs_0_
  63.3 19.1 %collective-permute-done.15 = s32[8,48]{1,0:T(8,128)S(1)} collective-permute-done((s32[8,48]{1,0:T(8,128)S(1)}, s32[8,48]{1,0:T(8,128)S(1)}, u32[]{:S(2)}, u32[]{:S(2)}) %collective-permute-start.15) | collective-permute-done | bytes 1568 | tf_op jit(solution)/shard_map/ppermute | solution.py:315
  88.4 27.4 %collective-permute-done.14 = s32[8,48]{1,0:T(8,128)S(1)} collective-permute-done((s32[8,48]{1,0:T(8,128)S(1)}, s32[8,48]{1,0:T(8,128)S(1)}, u32[]{:S(2)}, u32[]{:S(2)}) %collective-permute-start.14) | collective-permute-done | bytes 1568 | tf_op jit(solution)/shard_map/ppermute | solution.py:315
  121.5 3.7 place.31.w_ref.wkv_ref
  125.2 4.5 place.32.refs_0_
  131.0 4.4 fusion.9
  135.4 4.3 fusion.8
  140.4 4.1 place.33.refs_0_
  144.6 4.1 place.34.w_ref.wq_ref
  148.7 44.8 %collective-permute-done = bf16[8,48,3072]{2,1,0:T(8,128)(2,1)S(1)} collective-permute-done((bf16[8,48,3072]{2,1,0:T(8,128)(2,1)}, bf16[8,48,3072]{2,1,0:T(8,128)(2,1)S(1)}, u32[]{:S(2)}, u32[]{:S(2)}) %collective-permute-start) | collective-permute-done | bytes 2359328 | tf_op jit(solution)/shard_map/ppermute | solution.py:315
  194.9 4.4 place.35.x_ref
  199.3 11.0 %project.3 = bf16[1536,512]{1,0:T(8,128)(2,1)} custom-call(bf16[1536,3072]{1,0:T(8,128)(2,1)} %place.35.x_ref, bf16[3072,1024]{1,0:T(8,128)(2,1)} %place.31.w_ref.wkv_ref, f32[1536,128]{1,0:T(8,128)} %get-tuple-element.225.cos_ref, f32[1536,128]{1,0:T(8,128)} %get-tuple-element.235.sin_ref), custom_call_target="tpu_custom_call" | custom-call | flops 4831838208 | bytes 9437184 | tf_op jit(solution)/shard_map/project/pallas_call | solution.py:81
  210.4 11.0 %project.4 = bf16[1536,512]{1,0:T(8,128)(2,1)} custom-call(bf16[1536,3072]{1,0:T(8,128)(2,1)} %place.35.x_ref, bf16[3072,1024]{1,0:T(8,128)(2,1)} %place.31.w_ref.wkv_ref, f32[1536,128]{1,0:T(8,128)} %get-tuple-element.225.cos_ref, f32[1536,128]{1,0:T(8,128)} %get-tuple-element.235.sin_ref), custom_call_target="tpu_custom_call" | custom-call | flops 4831838208 | bytes 9437184 | tf_op jit(solution)/shard_map/project/pallas_call | solution.py:81
  221.3 23.5 %project.5 = bf16[1536,1536]{1,0:T(8,128)(2,1)} custom-call(bf16[1536,3072]{1,0:T(8,128)(2,1)} %place.35.x_ref, bf16[3072,1536]{1,0:T(8,128)(2,1)} %place.34.w_ref.wq_ref, f32[1536,128]{1,0:T(8,128)} %get-tuple-element.225.cos_ref, f32[1536,128]{1,0:T(8,128)} %get-tuple-element.235.sin_ref), custom_call_target="tpu_custom_call" | custom-call | flops 14495514624 | bytes 9437184 | tf_op jit(solution)/shard_map/project/pallas_call | solution.py:81
  253.0 4.4 place.36.refs_0_
  257.4 3.9 place.37.w_ref
  261.3 9.4 %convolution_convert_fusion.6 = bf16[384,1536]{1,0:T(8,128)(2,1)} fusion(bf16[384,3072]{1,0:T(8,128)(2,1)} %bitcast.153, bf16[1536,3072]{1,0:T(8,128)(2,1)} %place.37.w_ref), kind=kOutput, calls=%fused_computation.16 | convolution fusion | flops 3624468480 | bytes 12976128 | tf_op jit(solution)/shard_map/dot_general | solution.py:28
  270.8 6.8 convolution_convert_fusion.5
  277.5 72.3 %collective-permute-done.20 = bf16[8,48,3072]{2,1,0:T(8,128)(2,1)} collective-permute-done((bf16[8,48,3072]{2,1,0:T(8,128)(2,1)}, bf16[8,48,3072]{2,1,0:T(8,128)(2,1)}, u32[]{:S(2)}, u32[]{:S(2)}) %collective-permute-start.20) | collective-permute-done | bytes 2359328 | tf_op jit(solution)/shard_map/ppermute | solution.py:315
  349.8 6.7 convolution_convert_fusion.4
  356.6 3.9 place.38.refs_0_
  360.5 7.5 attn_fwd.4.refs_0_
  368.0 7.6 attn_fwd.5.refs_0_
  375.6 7.5 attn_fwd.6.refs_0_
  383.1 7.4 attn_fwd.7
  390.5 11.8 %head_out.2 = (bf16[384,3072]{1,0:T(8,128)(2,1)}, bf16[384,3072]{1,0:T(8,128)(2,1)}) custom-call(bf16[1536,1536]{1,0:T(8,128)(2,1)} %bitcast.93, bf16[1536,3072]{1,0:T(8,128)(2,1)} %place.37.w_ref), custom_call_target="tpu_custom_call" | custom-call | flops 7247757312 | bytes 9437184 | tf_op jit(solution)/shard_map/head_out/pallas_call | solution.py:238
  402.3 12.2 %head_out.3 = (f32[384,3072]{1,0:T(8,128)}, bf16[384,3072]{1,0:T(8,128)(2,1)}) custom-call(bf16[1536,1536]{1,0:T(8,128)(2,1)} %bitcast.94, bf16[1536,3072]{1,0:T(8,128)(2,1)} %place.37.w_ref), custom_call_target="tpu_custom_call" | custom-call | flops 7247757312 | bytes 9437184 | tf_op jit(solution)/shard_map/head_out/pallas_call | solution.py:238
  414.6 9.3 %convolution_convert_fusion.3 = bf16[384,1536]{1,0:T(8,128)(2,1)} fusion(bf16[384,3072]{1,0:T(8,128)(2,1)} %bitcast.37.x_ref, bf16[1536,3072]{1,0:T(8,128)(2,1)} %place.37.w_ref), kind=kOutput, calls=%fused_computation.13 | convolution fusion | flops 3624468480 | bytes 12976128 | tf_op jit(solution)/shard_map/dot_general | solution.py:28
  423.9 13.5 %attn_bwd.4 = (bf16[4,8,48,1536]{3,2,1,0:T(8,128)(2,1)}, f32[4,8,48,512]{3,2,1,0:T(8,128)}, bf16[4,8,48,512]{3,2,1,0:T(8,128)(2,1)}) custom-call(bf16[4,8,48,1536]{3,2,1,0:T(8,128)(2,1)} %bitcast.83, bf16[4,8,48,512]{3,2,1,0:T(8,128)(2,1)} %bitcast.119, bf16[4,8,48,512]{3,2,1,0:T(8,128)(2,1)} %collective-permute-done.19.kr_ref, ...), custom_call_target="tpu_custom_call" | custom-call | flops 2264924160 | bytes 11796480 | tf_op jit(solution)/shard_map/attn_bwd/pallas_call | solution.py:199
  437.4 13.7 %attn_bwd.5 = (bf16[4,8,48,1536]{3,2,1,0:T(8,128)(2,1)}, f32[4,8,48,512]{3,2,1,0:T(8,128)}, bf16[4,8,48,512]{3,2,1,0:T(8,128)(2,1)}) custom-call(bf16[4,8,48,1536]{3,2,1,0:T(8,128)(2,1)} %bitcast.84, bf16[4,8,48,512]{3,2,1,0:T(8,128)(2,1)} %bitcast.120, ...), custom_call_target="tpu_custom_call", output_to_operand_aliasing={{0}: (13, {}), {1}: (14, {}), {2}: (15, {})} | custom-call | flops 2264924160 | bytes 11796480 | tf_op jit(solution)/shard_map/attn_bwd/pallas_call | solution.py:199
  451.2 13.4 %attn_bwd.6 = (bf16[4,8,48,1536]{3,2,1,0:T(8,128)(2,1)}, f32[4,8,48,512]{3,2,1,0:T(8,128)}, bf16[4,8,48,512]{3,2,1,0:T(8,128)(2,1)}) custom-call(bf16[4,8,48,1536]{3,2,1,0:T(8,128)(2,1)} %bitcast.85, bf16[4,8,48,512]{3,2,1,0:T(8,128)(2,1)} %bitcast.125, bf16[4,8,48,512]{3,2,1,0:T(8,128)(2,1)} %collective-permute-done.18.kr_ref, ...), custom_call_target="tpu_custom_call", output_to_operand_aliasing={{0}: (13, {})} | custom-call | flops 2264924160 | bytes 11796480 | tf_op jit(solution)/shard_map/attn_bwd/pallas_call | solution.py:199
  464.6 13.4 %attn_bwd.7 = (bf16[4,8,48,1536]{3,2,1,0:T(8,128)(2,1)}, f32[4,8,48,512]{3,2,1,0:T(8,128)}, bf16[4,8,48,512]{3,2,1,0:T(8,128)(2,1)}) custom-call(bf16[4,8,48,1536]{3,2,1,0:T(8,128)(2,1)} %bitcast.86, bf16[4,8,48,512]{3,2,1,0:T(8,128)(2,1)} %bitcast.126, ...), custom_call_target="tpu_custom_call", output_to_operand_aliasing={{0}: (13, {}), {1}: (14, {}), {2}: (15, {})} | custom-call | flops 2264924160 | bytes 11796480 | tf_op jit(solution)/shard_map/attn_bwd/pallas_call | solution.py:199
  478.1 4.0 place.39
  482.1 12.4 %convolution_convert_fusion.1 = bf16[768,3072]{1,0:T(8,128)(2,1)} fusion(bf16[1536,3072]{1,0:T(8,128)(2,1)} %place.39, bf16[1536,1536]{1,0:T(8,128)(2,1)} %bitcast.95), kind=kOutput, calls=%fused_computation.1 | convolution fusion | flops 7250116608 | bytes 16515072 | tf_op jit(solution)/shard_map/dot_general | solution.py:28
  498.4 13.4 %convolution_convert_fusion = bf16[3072,768]{1,0:T(8,128)(2,1)} fusion(bf16[1536,3072]{1,0:T(8,128)(2,1)} %place.35.x_ref, bf16[1536,1536]{1,0:T(8,128)(2,1)S(1)} %bitcast.116), kind=kOutput, calls=%fused_computation | convolution fusion | flops 7250116608 | bytes 16515072 | tf_op jit(solution)/shard_map/dot_general | solution.py:28
  511.8 24.5 %collective-permute-done.27 = bf16[4,8,48,512]{3,2,1,0:T(8,128)(2,1)S(1)} collective-permute-done((bf16[4,8,48,512]{3,2,1,0:T(8,128)(2,1)S(1)}, bf16[4,8,48,512]{3,2,1,0:T(8,128)(2,1)S(1)}, u32[]{:S(2)}, u32[]{:S(2)}) %collective-permute-start.27) | collective-permute-done | bytes 1572896 | tf_op jit(solution)/shard_map/ppermute | solution.py:315
  537.1 6.6 convolution_convert_fusion.2
  545.4 6.7 add_convert_fusion.1
  552.0 31.6 %collective-permute-done.28 = bf16[4,8,48,512]{3,2,1,0:T(8,128)(2,1)S(1)} collective-permute-done((bf16[4,8,48,512]{3,2,1,0:T(8,128)(2,1)S(1)}, bf16[4,8,48,512]{3,2,1,0:T(8,128)(2,1)S(1)}, u32[]{:S(2)}, u32[]{:S(2)}) %collective-permute-start.28) | collective-permute-done | bytes 1572896 | tf_op jit(solution)/shard_map/ppermute | solution.py:315
  585.5 18.6 %grad_in.2 = (bf16[384,3072]{1,0:T(8,128)(2,1)}, bf16[384,3072]{1,0:T(8,128)(2,1)}) custom-call(bf16[1536,1536]{1,0:T(8,128)(2,1)} %bitcast.110, bf16[1536,512]{1,0:T(8,128)(2,1)} %bitcast.184, bf16[1536,512]{1,0:T(8,128)(2,1)} %bitcast.179, bf16[3072,1536]{1,0:T(8,128)(2,1)} %place.34.w_ref.wq_ref, bf16[3072,1024]{1,0:T(8,128)(2,1)} %place.31.w_ref.wkv_ref), custom_call_target="tpu_custom_call" | custom-call | flops 12079595520 | bytes 9437184 | tf_op jit(solution)/shard_map/grad_in/pallas_call | solution.py:221
  604.3 9.5 %add_convert_fusion = bf16[3072,384]{1,0:T(8,128)(2,1)} fusion(bf16[1536,3072]{1,0:T(8,128)(2,1)} %place.35.x_ref, bf16[3072,768]{1,0:T(8,128)(2,1)} %collective-permute-done.31, bf16[1536,1536]{1,0:T(8,128)(2,1)} %bitcast.111), kind=kOutput, calls=%fused_computation.5 | convolution fusion | flops 3627417600 | bytes 15335424 | tf_op jit(solution)/shard_map/dot_general | solution.py:28
  613.9 5.1 fusion
  619.0 18.8 %grad_in.3 = (f32[384,3072]{1,0:T(8,128)}, bf16[384,3072]{1,0:T(8,128)(2,1)}) custom-call(bf16[1536,1536]{1,0:T(8,128)(2,1)} %bitcast.112, bf16[1536,512]{1,0:T(8,128)(2,1)} %bitcast.185, bf16[1536,512]{1,0:T(8,128)(2,1)} %bitcast.180, bf16[3072,1536]{1,0:T(8,128)(2,1)} %place.34.w_ref.wq_ref, bf16[3072,1024]{1,0:T(8,128)(2,1)} %place.31.w_ref.wkv_ref), custom_call_target="tpu_custom_call" | custom-call | flops 12079595520 | bytes 9437184 | tf_op jit(solution)/shard_map/grad_in/pallas_call | solution.py:221
  641.1 5.7 shard_map.135.refs_3_
  647.0 5.3 shard_map.136
  652.2 6.0 collective-permute-done.34.refs_3_
  658.2 7.8 %shard_map.137 = (bf16[768,3072]{1,0:T(8,128)(2,1)}, f32[8,3072]{1,0:T(8,128)}) custom-call(s32[1]{0:T(128)} %bitcast.36.h_ref, bf16[768,3072]{1,0:T(8,128)(2,1)} %bitcast.91, bf16[768,3072]{1,0:T(8,128)(2,1)} %bitcast.106, f32[384,3072]{1,0:T(8,128)} %get-tuple-element.374.refs_2_, bf16[384,3072]{1,0:T(8,128)(2,1)} %collective-permute-done.34.refs_3_, ...), custom_call_target="tpu_custom_call" | custom-call | flops 1179648000 | bytes 11796480 | tf_op jit(solution)/shard_map/pallas_call | solution.py:299
  669.5 7.2 fusion.4
  676.6 5.0 convert_add_fusion.2
  681.7 8.7 %convert_add_fusion.1 = f32[3072,384]{1,0:T(8,128)} fusion(bf16[1536,3072]{1,0:T(8,128)(2,1)S(1)} %bitcast.78, bf16[3072,768]{1,0:T(8,128)(2,1)} %collective-permute-done.31, bf16[1536,1536]{1,0:T(8,128)(2,1)} %bitcast.113), kind=kOutput, calls=%fused_computation.3 | convolution fusion | flops 3626237952 | bytes 17694720 | tf_op jit(solution)/shard_map/dot_general | solution.py:28
  690.4 4.5 convolution_add_fusion
  694.9 17.0 %collective-permute-done.33.refs_3_ = bf16[384,3072]{1,0:T(8,128)(2,1)} collective-permute-done((bf16[384,3072]{1,0:T(8,128)(2,1)}, bf16[384,3072]{1,0:T(8,128)(2,1)}, u32[]{:S(2)}, u32[]{:S(2)}) %collective-permute-start.33) | collective-permute-done | bytes 2359328 | tf_op jit(solution)/shard_map/ppermute | solution.py:315
  711.9 7.8 %shard_map.138 = (bf16[768,3072]{1,0:T(8,128)(2,1)}, f32[8,3072]{1,0:T(8,128)}) custom-call(s32[1]{0:T(128)} %bitcast.h_ref, bf16[768,3072]{1,0:T(8,128)(2,1)} %bitcast.92, bf16[768,3072]{1,0:T(8,128)(2,1)} %bitcast.107, bf16[384,3072]{1,0:T(8,128)(2,1)} %collective-permute-done.32.refs_2_, ...), custom_call_target="tpu_custom_call", output_to_operand_aliasing={{0}: (6, {})} | custom-call | flops 1179648000 | bytes 11796480 | tf_op jit(solution)/shard_map/pallas_call | solution.py:299
  722.1 31.2 %collective-permute-done.39 = bf16[3072,384]{1,0:T(8,128)(2,1)} collective-permute-done((bf16[3072,384]{1,0:T(8,128)(2,1)}, bf16[3072,384]{1,0:T(8,128)(2,1)}, u32[]{:S(2)}, u32[]{:S(2)}) %collective-permute-start.39) | collective-permute-done | bytes 2359328 | tf_op jit(solution)/shard_map/ppermute | solution.py:315
  753.3 5.7 convert_add_fusion
  (174 shorter events, 68.3 us)
Async XLA Ops:
  4.8 8.2 %collective-permute-start.7 = (bf16[3072,256]{1,0:T(8,128)(2,1)}, bf16[3072,256]{1,0:T(8,128)(2,1)}, u32[]{:S(2)}, u32[]{:S(2)}) collective-permute-start(bf16[3072,256]{1,0:T(8,128)(2,1)} %constant_dynamic-update-slice_fusion.x_ref), channel_id=1, source_target_pairs={{0,1},{1,0},{2,3},{3,2},{4,5},{5,4},{6,7},{7,6},{8,9},{9,8},{10,11... | collective-permute-start | bytes 4718600 | tf_op jit(solution)/shard_map/ppermute | solution.py:315
  9.2 19.9 %copy-start.4 = (bf16[8,48,3072]{2,1,0:T(8,128)(2,1)}, bf16[8,48,3072]{2,1,0:T(8,128)(2,1)S(1)}, u32[]{:S(2)}) copy-start(bf16[8,48,3072]{2,1,0:T(8,128)(2,1)S(1)} %get-tuple-element.403) | copy-start | bytes 7077892
  9.2 7.7 %copy-start.13 = (bf16[3072]{0:T(1024)(128)(2,1)S(1)}, bf16[3072]{0:T(1024)(128)(2,1)}, u32[]{:S(2)}) copy-start(bf16[3072]{0:T(1024)(128)(2,1)} %param.11) | copy-start | bytes 18436
  9.2 19.9 %collective-permute-start.2 = (bf16[8,48,3072]{2,1,0:T(8,128)(2,1)}, bf16[8,48,3072]{2,1,0:T(8,128)(2,1)}, u32[]{:S(2)}, u32[]{:S(2)}) collective-permute-start(bf16[8,48,3072]{2,1,0:T(8,128)(2,1)} %get-tuple-element.404), channel_id=1, source_target_pairs={{0,1},{1,0},{2,3},{3,2},{4,5},{5,4},{6,7},{7,6},{8,9},{9,8},{10,11... | collective-permute-start | bytes 7077896 | tf_op jit(solution)/shard_map/ppermute | solution.py:315
  9.7 36.0 %collective-permute-start.6 = (bf16[3072,384]{1,0:T(8,128)(2,1)}, bf16[3072,384]{1,0:T(8,128)(2,1)}, u32[]{:S(2)}, u32[]{:S(2)}) collective-permute-start(bf16[3072,384]{1,0:T(8,128)(2,1)} %x_ref.1), channel_id=1, source_target_pairs={{0,1},{1,0},{2,3},{3,2},{4,5},{5,4},{6,7},{7,6},{8,9},{9,8},{10,11... | collective-permute-start | bytes 7077896 | tf_op jit(solution)/shard_map/ppermute | solution.py:315
  9.7 39.9 %collective-permute-start.5 = (bf16[384,3072]{1,0:T(8,128)(2,1)}, bf16[384,3072]{1,0:T(8,128)(2,1)}, u32[]{:S(2)}, u32[]{:S(2)}) collective-permute-start(bf16[384,3072]{1,0:T(8,128)(2,1)} %x_ref.2), channel_id=1, source_target_pairs={{0,1},{1,0},{2,3},{3,2},{4,5},{5,4},{6,7},{7,6},{8,9},{9,8},{10,11... | collective-permute-start | bytes 7077896 | tf_op jit(solution)/shard_map/ppermute | solution.py:315
  12.9 40.6 %collective-permute-start.4 = (bf16[8,48,3072]{2,1,0:T(8,128)(2,1)}, bf16[8,48,3072]{2,1,0:T(8,128)(2,1)}, u32[]{:S(2)}, u32[]{:S(2)}) collective-permute-start(bf16[8,48,3072]{2,1,0:T(8,128)(2,1)} %get-tuple-element.401), channel_id=1, source_target_pairs={{0,1},{1,0},{2,3},{3,2},{4,5},{5,4},{6,7},{7,6},{8,9},{9,8},{10,11... | collective-permute-start | bytes 7077896 | tf_op jit(solution)/shard_map/ppermute | solution.py:315
  13.0 44.5 %collective-permute-start.3 = (bf16[3072,256]{1,0:T(8,128)(2,1)}, bf16[3072,256]{1,0:T(8,128)(2,1)}, u32[]{:S(2)}, u32[]{:S(2)}) collective-permute-start(bf16[3072,256]{1,0:T(8,128)(2,1)} %constant_dynamic-update-slice_fusion.x_ref), channel_id=1, source_target_pairs={{0,6},{1,7},{2,4},{3,5},{4,2},{5,3},{6,0},{7,1},{8,14},{9,15},{10,... | collective-permute-start | bytes 4718600 | tf_op jit(solution)/shard_map/ppermute | solution.py:315
  29.1 96.1 %collective-permute-start.1 = (bf16[8,48,3072]{2,1,0:T(8,128)(2,1)S(1)}, bf16[8,48,3072]{2,1,0:T(8,128)(2,1)}, u32[]{:S(2)}, u32[]{:S(2)}) collective-permute-start(bf16[8,48,3072]{2,1,0:T(8,128)(2,1)S(1)} %get-tuple-element.403), channel_id=1, source_target_pairs={{0,2},{1,3},{2,0},{3,1},{4,6},{5,7},{6,4},{7,5},{8,10},{9,11},{10,... | collective-permute-start | bytes 7077896 | tf_op jit(solution)/shard_map/ppermute | solution.py:315
  57.5 64.1 %collective-permute-start.8 = (bf16[3072,256]{1,0:T(8,128)(2,1)}, bf16[3072,256]{1,0:T(8,128)(2,1)}, u32[]{:S(2)}, u32[]{:S(2)}) collective-permute-start(bf16[3072,256]{1,0:T(8,128)(2,1)} %collective-permute-done.3.x_ref), channel_id=1, source_target_pairs={{0,1},{1,0},{2,3},{3,2},{4,5},{5,4},{6,7},{7,6},{8,9},{9,8},{10,11... | collective-permute-start | bytes 4718600 | tf_op jit(solution)/shard_map/ppermute | solution.py:315
  57.6 24.8 %collective-permute-start.15 = (s32[8,48]{1,0:T(8,128)S(1)}, s32[8,48]{1,0:T(8,128)S(1)}, u32[]{:S(2)}, u32[]{:S(2)}) collective-permute-start(s32[8,48]{1,0:T(8,128)S(1)} %get-tuple-element.415), channel_id=1, source_target_pairs={{4,0},{5,1},{6,2},{7,3},{0,4},{1,5},{2,6},{3,7},{12,8},{13,9},{14,... | collective-permute-start | bytes 4616 | tf_op jit(solution)/shard_map/ppermute | solution.py:315
  59.0 23.6 %collective-permute-start.13 = (s32[8,48]{1,0:T(8,128)S(1)}, s32[8,48]{1,0:T(8,128)S(1)}, u32[]{:S(2)}, u32[]{:S(2)}) collective-permute-start(s32[8,48]{1,0:T(8,128)S(1)} %get-tuple-element.415), channel_id=1, source_target_pairs={{6,0},{7,1},{4,2},{5,3},{2,4},{3,5},{0,6},{1,7},{14,8},{15,9},{12,... | collective-permute-start | bytes 4616 | tf_op jit(solution)/shard_map/ppermute | solution.py:315
  62.2 77.5 %collective-permute-start.9 = (bf16[3072,384]{1,0:T(8,128)(2,1)}, bf16[3072,384]{1,0:T(8,128)(2,1)}, u32[]{:S(2)}, u32[]{:S(2)}) collective-permute-start(bf16[3072,384]{1,0:T(8,128)(2,1)} %x_ref.1), channel_id=1, source_target_pairs={{0,6},{1,7},{2,4},{3,5},{4,2},{5,3},{6,0},{7,1},{8,14},{9,15},{10,... | collective-permute-start | bytes 7077896 | tf_op jit(solution)/shard_map/ppermute | solution.py:315
  82.4 3.6 collective-permute-start.11
  82.6 4.6 collective-permute-start.16
  86.0 29.8 %collective-permute-start.14 = (s32[8,48]{1,0:T(8,128)S(1)}, s32[8,48]{1,0:T(8,128)S(1)}, u32[]{:S(2)}, u32[]{:S(2)}) collective-permute-start(s32[8,48]{1,0:T(8,128)S(1)} %get-tuple-element.416), channel_id=1, source_target_pairs={{7,0},{6,1},{5,2},{4,3},{3,4},{2,5},{1,6},{0,7},{15,8},{14,9},{13,... | collective-permute-start | bytes 4616 | tf_op jit(solution)/shard_map/ppermute | solution.py:315
  87.2 29.8 %collective-permute-start.12 = (s32[8,48]{1,0:T(8,128)S(1)}, s32[8,48]{1,0:T(8,128)S(1)}, u32[]{:S(2)}, u32[]{:S(2)}) collective-permute-start(s32[8,48]{1,0:T(8,128)S(1)} %get-tuple-element.416), channel_id=1, source_target_pairs={{0,3},{1,2},{2,1},{3,0},{4,7},{5,6},{6,5},{7,4},{8,11},{9,10},{10,... | collective-permute-start | bytes 4616 | tf_op jit(solution)/shard_map/ppermute | solution.py:315
  115.8 2.1 collective-permute-start.10
  139.7 4.9 collective-permute-start.17
  140.1 53.4 %collective-permute-start = (bf16[8,48,3072]{2,1,0:T(8,128)(2,1)}, bf16[8,48,3072]{2,1,0:T(8,128)(2,1)S(1)}, u32[]{:S(2)}, u32[]{:S(2)}) collective-permute-start(bf16[8,48,3072]{2,1,0:T(8,128)(2,1)} %get-tuple-element.404), channel_id=1, source_target_pairs={{0,3},{1,2},{2,1},{3,0},{4,7},{5,6},{6,5},{7,4},{8,11},{9,10},{10,... | collective-permute-start | bytes 7077896 | tf_op jit(solution)/shard_map/ppermute | solution.py:315
  140.1 104.8 %collective-permute-start.21 = (bf16[384,3072]{1,0:T(8,128)(2,1)}, bf16[384,3072]{1,0:T(8,128)(2,1)}, u32[]{:S(2)}, u32[]{:S(2)}) collective-permute-start(bf16[384,3072]{1,0:T(8,128)(2,1)} %x_ref.2), channel_id=1, source_target_pairs={{0,6},{1,7},{2,4},{3,5},{4,2},{5,3},{6,0},{7,1},{8,14},{9,15},{10,... | collective-permute-start | bytes 7077896 | tf_op jit(solution)/shard_map/ppermute | solution.py:315
  221.3 29.2 %copy-start.1 = (bf16[1536,512]{1,0:T(8,128)(2,1)S(1)}, bf16[1536,512]{1,0:T(8,128)(2,1)}, u32[]{:S(2)}) copy-start(bf16[1536,512]{1,0:T(8,128)(2,1)} %project.3) | copy-start | bytes 4718596
  244.8 12.6 %collective-permute-start.22 = (bf16[384,3072]{1,0:T(8,128)(2,1)}, bf16[384,3072]{1,0:T(8,128)(2,1)}, u32[]{:S(2)}, u32[]{:S(2)}) collective-permute-start(bf16[384,3072]{1,0:T(8,128)(2,1)} %collective-permute-done.21.x_ref), channel_id=1, source_target_pairs={{0,1},{1,0},{2,3},{3,2},{4,5},{5,4},{6,7},{7,6},{8,9},{9,8},{10,11... | collective-permute-start | bytes 7077896 | tf_op jit(solution)/shard_map/ppermute | solution.py:315
  245.4 169.2 %collective-permute-start.26 = (bf16[8,48,3072]{2,1,0:T(8,128)(2,1)}, bf16[8,48,3072]{2,1,0:T(8,128)(2,1)}, u32[]{:S(2)}, u32[]{:S(2)}) collective-permute-start(bf16[8,48,3072]{2,1,0:T(8,128)(2,1)} %get-tuple-element.401), channel_id=1, source_target_pairs={{0,3},{1,2},{2,1},{3,0},{4,7},{5,6},{6,5},{7,4},{8,11},{9,10},{10,... | collective-permute-start | bytes 7077896 | tf_op jit(solution)/shard_map/ppermute | solution.py:315
  245.4 104.4 %collective-permute-start.20 = (bf16[8,48,3072]{2,1,0:T(8,128)(2,1)}, bf16[8,48,3072]{2,1,0:T(8,128)(2,1)}, u32[]{:S(2)}, u32[]{:S(2)}) collective-permute-start(bf16[8,48,3072]{2,1,0:T(8,128)(2,1)} %get-tuple-element.402), channel_id=1, source_target_pairs={{0,2},{1,3},{2,0},{3,1},{4,6},{5,7},{6,4},{7,5},{8,10},{9,11},{10,... | collective-permute-start | bytes 7077896 | tf_op jit(solution)/shard_map/ppermute | solution.py:315
  247.1 128.5 %collective-permute-start.18 = (bf16[4,8,48,512]{3,2,1,0:T(8,128)(2,1)}, bf16[4,8,48,512]{3,2,1,0:T(8,128)(2,1)}, u32[]{:S(2)}, u32[]{:S(2)}) collective-permute-start(bf16[4,8,48,512]{3,2,1,0:T(8,128)(2,1)} %bitcast.122), channel_id=1, source_target_pairs={{0,6},{1,7},{2,4},{3,5},{8,14},{9,15},{10,12},{11,13}} | collective-permute-start | bytes 4718600 | tf_op jit(solution)/shard_map/ppermute | solution.py:315
  250.5 110.0 %collective-permute-start.19 = (bf16[4,8,48,512]{3,2,1,0:T(8,128)(2,1)S(1)}, bf16[4,8,48,512]{3,2,1,0:T(8,128)(2,1)}, u32[]{:S(2)}, u32[]{:S(2)}) collective-permute-start(bf16[4,8,48,512]{3,2,1,0:T(8,128)(2,1)S(1)} %bitcast.121), channel_id=1, source_target_pairs={{0,6},{1,7},{2,4},{3,5},{8,14},{9,15},{10,12},{11,13}} | collective-permute-start | bytes 4718600 | tf_op jit(solution)/shard_map/ppermute | solution.py:315
  261.3 9.4 %copy-start = (bf16[1536,3072]{1,0:T(8,128)(2,1)S(1)}, bf16[1536,3072]{1,0:T(8,128)(2,1)}, u32[]{:S(2)}) copy-start(bf16[1536,3072]{1,0:T(8,128)(2,1)} %place.37.w_ref) | copy-start | bytes 28311556
  478.1 20.3 %slice-start.14 = ((s8[4718592]{0:T(1024)(128)(4,1)}), s8[524288]{0:T(1024)(128)(4,1)S(1)}, s32[]{:S(2)}) async-start(s8[4718592]{0:T(1024)(128)(4,1)} %bitcast.114), calls=%async_computation.14 | async-start | bytes 1048576
  482.1 14.6 %copy-start.7 = (bf16[4,8,48,512]{3,2,1,0:T(8,128)(2,1)S(1)}, bf16[4,8,48,512]{3,2,1,0:T(8,128)(2,1)}, u32[]{:S(2)}) copy-start(bf16[4,8,48,512]{3,2,1,0:T(8,128)(2,1)} %get-tuple-element.326) | copy-start | bytes 4718596
  482.1 16.3 %slice-start.15 = ((s8[4718592]{0:T(1024)(128)(4,1)}), s8[4194304]{0:T(1024)(128)(4,1)S(1)}, s32[]{:S(2)}) async-start(s8[4718592]{0:T(1024)(128)(4,1)} %bitcast.114), calls=%async_computation.15 | async-start | bytes 8388608
  482.1 55.0 %slice-start = ((s8[9437184]{0:T(1024)(128)(4,1)}), s8[4194304]{0:T(1024)(128)(4,1)S(1)}, s32[]{:S(2)}) async-start(s8[9437184]{0:T(1024)(128)(4,1)} %bitcast.73), calls=%async_computation | async-start | bytes 8388608
  494.5 49.2 %collective-permute-start.29 = (bf16[768,3072]{1,0:T(8,128)(2,1)}, bf16[768,3072]{1,0:T(8,128)(2,1)S(1)}, u32[]{:S(2)}, u32[]{:S(2)}) collective-permute-start(bf16[768,3072]{1,0:T(8,128)(2,1)} %convolution_convert_fusion.1), channel_id=1, source_target_pairs={{0,1},{1,0},{2,3},{3,2},{4,5},{5,4},{6,7},{7,6},{8,9},{9,8},{10,11... | collective-permute-start | bytes 14155784 | tf_op jit(solution)/shard_map/ppermute | solution.py:315
  494.5 143.4 %collective-permute-start.25 = (bf16[384,3072]{1,0:T(8,128)(2,1)}, bf16[384,3072]{1,0:T(8,128)(2,1)}, u32[]{:S(2)}, u32[]{:S(2)}) collective-permute-start(bf16[384,3072]{1,0:T(8,128)(2,1)} %get-tuple-element.272), channel_id=1, source_target_pairs={{0,2},{1,3},{2,0},{3,1},{4,6},{5,7},{6,4},{7,5},{8,10},{9,11},{10,... | collective-permute-start | bytes 7077896 | tf_op jit(solution)/shard_map/ppermute | solution.py:315
  494.5 152.3 %collective-permute-start.24 = (bf16[384,3072]{1,0:T(8,128)(2,1)}, bf16[384,3072]{1,0:T(8,128)(2,1)}, u32[]{:S(2)}, u32[]{:S(2)}) collective-permute-start(bf16[384,3072]{1,0:T(8,128)(2,1)} %get-tuple-element.276), channel_id=1, source_target_pairs={{0,3},{1,2},{2,1},{3,0},{4,7},{5,6},{6,5},{7,4},{8,11},{9,10},{10,... | collective-permute-start | bytes 7077896 | tf_op jit(solution)/shard_map/ppermute | solution.py:315
  496.3 150.5 %collective-permute-start.23 = (bf16[384,3072]{1,0:T(8,128)(2,1)}, bf16[384,3072]{1,0:T(8,128)(2,1)}, u32[]{:S(2)}, u32[]{:S(2)}) collective-permute-start(bf16[384,3072]{1,0:T(8,128)(2,1)} %get-tuple-element.275), channel_id=1, source_target_pairs={{0,1},{1,0},{2,3},{3,2},{4,5},{5,4},{6,7},{7,6},{8,9},{9,8},{10,11... | collective-permute-start | bytes 7077896 | tf_op jit(solution)/shard_map/ppermute | solution.py:315
  496.6 39.6 %collective-permute-start.27 = (bf16[4,8,48,512]{3,2,1,0:T(8,128)(2,1)S(1)}, bf16[4,8,48,512]{3,2,1,0:T(8,128)(2,1)S(1)}, u32[]{:S(2)}, u32[]{:S(2)}) collective-permute-start(bf16[4,8,48,512]{3,2,1,0:T(8,128)(2,1)S(1)} %copy-done.7), channel_id=1, source_target_pairs={{4,2},{5,3},{6,0},{7,1},{12,10},{13,11},{14,8},{15,9}} | collective-permute-start | bytes 4718600 | tf_op jit(solution)/shard_map/ppermute | solution.py:315
  498.4 38.7 %slice-start.1 = ((s8[9437184]{0:T(1024)(128)(4,1)}), s8[4194304]{0:T(1024)(128)(4,1)S(1)}, s32[]{:S(2)}) async-start(s8[9437184]{0:T(1024)(128)(4,1)} %bitcast.73), calls=%async_computation.1 | async-start | bytes 8388608
  498.4 38.7 %slice-start.2 = ((s8[9437184]{0:T(1024)(128)(4,1)}), s8[1048576]{0:T(1024)(128)(4,1)S(1)}, s32[]{:S(2)}) async-start(s8[9437184]{0:T(1024)(128)(4,1)} %bitcast.73), calls=%async_computation.2 | async-start | bytes 2097152
  511.8 24.6 %copy-start.3 = (f32[4,8,48,512]{3,2,1,0:T(8,128)S(1)}, f32[4,8,48,512]{3,2,1,0:T(8,128)}, u32[]{:S(2)}) copy-start(f32[4,8,48,512]{3,2,1,0:T(8,128)} %get-tuple-element.333) | copy-start | bytes 9437188
  536.3 67.8 %collective-permute-start.31 = (bf16[3072,768]{1,0:T(8,128)(2,1)}, bf16[3072,768]{1,0:T(8,128)(2,1)}, u32[]{:S(2)}, u32[]{:S(2)}) collective-permute-start(bf16[3072,768]{1,0:T(8,128)(2,1)} %convolution_convert_fusion), channel_id=1, source_target_pairs={{0,1},{1,0},{2,3},{3,2},{4,5},{5,4},{6,7},{7,6},{8,9},{9,8},{10,11... | collective-permute-start | bytes 14155784 | tf_op jit(solution)/shard_map/ppermute | solution.py:315
  536.4 8.9 %slice-start.9 = ((s8[9437184]{0:T(1024)(128)(4,1)}), s8[4194304]{0:T(1024)(128)(4,1)S(1)}, s32[]{:S(2)}) async-start(s8[9437184]{0:T(1024)(128)(4,1)} %bitcast.87), calls=%async_computation.9 | async-start | bytes 8388608
  537.1 8.3 %slice-start.10 = ((s8[9437184]{0:T(1024)(128)(4,1)}), s8[4194304]{0:T(1024)(128)(4,1)S(1)}, s32[]{:S(2)}) async-start(s8[9437184]{0:T(1024)(128)(4,1)} %bitcast.87), calls=%async_computation.10 | async-start | bytes 8388608
  537.1 8.3 %slice-start.11 = ((s8[9437184]{0:T(1024)(128)(4,1)}), s8[1048576]{0:T(1024)(128)(4,1)S(1)}, s32[]{:S(2)}) async-start(s8[9437184]{0:T(1024)(128)(4,1)} %bitcast.87), calls=%async_computation.11 | async-start | bytes 2097152
  543.7 39.9 %collective-permute-start.28 = (bf16[4,8,48,512]{3,2,1,0:T(8,128)(2,1)S(1)}, bf16[4,8,48,512]{3,2,1,0:T(8,128)(2,1)S(1)}, u32[]{:S(2)}, u32[]{:S(2)}) collective-permute-start(bf16[4,8,48,512]{3,2,1,0:T(8,128)(2,1)S(1)} %copy-done.6), channel_id=1, source_target_pairs={{4,2},{5,3},{6,0},{7,1},{12,10},{13,11},{14,8},{15,9}} | collective-permute-start | bytes 4718600 | tf_op jit(solution)/shard_map/ppermute | solution.py:315
  552.0 31.7 %copy-start.2 = (f32[4,8,48,512]{3,2,1,0:T(8,128)S(1)}, f32[4,8,48,512]{3,2,1,0:T(8,128)}, u32[]{:S(2)}) copy-start(f32[4,8,48,512]{3,2,1,0:T(8,128)} %get-tuple-element.343) | copy-start | bytes 9437188
  583.6 30.2 %collective-permute-start.30 = (bf16[3072,512]{1,0:T(8,128)(2,1)}, bf16[3072,512]{1,0:T(8,128)(2,1)}, u32[]{:S(2)}, u32[]{:S(2)}) collective-permute-start(bf16[3072,512]{1,0:T(8,128)(2,1)} %convolution_convert_fusion.2), channel_id=1, source_target_pairs={{0,1},{1,0},{2,3},{3,2},{4,5},{5,4},{6,7},{7,6},{8,9},{9,8},{10,11... | collective-permute-start | bytes 9437192 | tf_op jit(solution)/shard_map/ppermute | solution.py:315
  604.1 9.7 %slice-start.3 = ((s8[9437184]{0:T(1024)(128)(4,1)}), s8[4194304]{0:T(1024)(128)(4,1)S(1)}, s32[]{:S(2)}) async-start(s8[9437184]{0:T(1024)(128)(4,1)} %bitcast.75), calls=%async_computation.3 | async-start | bytes 8388608
  604.1 9.7 %slice-start.4 = ((s8[9437184]{0:T(1024)(128)(4,1)}), s8[4194304]{0:T(1024)(128)(4,1)S(1)}, s32[]{:S(2)}) async-start(s8[9437184]{0:T(1024)(128)(4,1)} %bitcast.75), calls=%async_computation.4 | async-start | bytes 8388608
  604.1 9.7 %slice-start.5 = ((s8[9437184]{0:T(1024)(128)(4,1)}), s8[1048576]{0:T(1024)(128)(4,1)S(1)}, s32[]{:S(2)}) async-start(s8[9437184]{0:T(1024)(128)(4,1)} %bitcast.75), calls=%async_computation.5 | async-start | bytes 2097152
  604.1 9.7 %copy-start.8 = (bf16[4,8,48,512]{3,2,1,0:T(8,128)(2,1)S(1)}, bf16[4,8,48,512]{3,2,1,0:T(8,128)(2,1)}, u32[]{:S(2)}) copy-start(bf16[4,8,48,512]{3,2,1,0:T(8,128)(2,1)} %add_convert_fusion.2) | copy-start | bytes 4718596
  604.2 54.0 %collective-permute-start.34 = (bf16[384,3072]{1,0:T(8,128)(2,1)}, bf16[384,3072]{1,0:T(8,128)(2,1)}, u32[]{:S(2)}, u32[]{:S(2)}) collective-permute-start(bf16[384,3072]{1,0:T(8,128)(2,1)} %get-tuple-element.350), channel_id=1, source_target_pairs={{0,2},{1,3},{2,0},{3,1},{4,6},{5,7},{6,4},{7,5},{8,10},{9,11},{10,... | collective-permute-start | bytes 7077896 | tf_op jit(solution)/shard_map/ppermute | solution.py:315
  613.8 55.6 %collective-permute-start.35 = (bf16[384,3072]{1,0:T(8,128)(2,1)}, bf16[384,3072]{1,0:T(8,128)(2,1)}, u32[]{:S(2)}, u32[]{:S(2)}) collective-permute-start(bf16[384,3072]{1,0:T(8,128)(2,1)} %add_convert_fusion.1), channel_id=1, source_target_pairs={{0,6},{1,7},{2,4},{3,5},{4,2},{5,3},{6,0},{7,1},{8,14},{9,15},{10,... | collective-permute-start | bytes 7077896 | tf_op jit(solution)/shard_map/ppermute | solution.py:315
  637.9 121.4 %collective-permute-start.40 = (bf16[3072,256]{1,0:T(8,128)(2,1)}, bf16[3072,256]{1,0:T(8,128)(2,1)}, u32[]{:S(2)}, u32[]{:S(2)}) collective-permute-start(bf16[3072,256]{1,0:T(8,128)(2,1)} %fusion), channel_id=1, source_target_pairs={{0,6},{1,7},{2,4},{3,5},{4,2},{5,3},{6,0},{7,1},{8,14},{9,15},{10,... | collective-permute-start | bytes 4718600 | tf_op jit(solution)/shard_map/ppermute | solution.py:315
  646.8 106.4 %collective-permute-start.39 = (bf16[3072,384]{1,0:T(8,128)(2,1)}, bf16[3072,384]{1,0:T(8,128)(2,1)}, u32[]{:S(2)}, u32[]{:S(2)}) collective-permute-start(bf16[3072,384]{1,0:T(8,128)(2,1)} %add_convert_fusion), channel_id=1, source_target_pairs={{0,6},{1,7},{2,4},{3,5},{4,2},{5,3},{6,0},{7,1},{8,14},{9,15},{10,... | collective-permute-start | bytes 7077896 | tf_op jit(solution)/shard_map/ppermute | solution.py:315
  646.9 48.0 %collective-permute-start.32 = (bf16[384,3072]{1,0:T(8,128)(2,1)}, bf16[384,3072]{1,0:T(8,128)(2,1)}, u32[]{:S(2)}, u32[]{:S(2)}) collective-permute-start(bf16[384,3072]{1,0:T(8,128)(2,1)} %get-tuple-element.370), channel_id=1, source_target_pairs={{0,1},{1,0},{2,3},{3,2},{4,5},{5,4},{6,7},{7,6},{8,9},{9,8},{10,11... | collective-permute-start | bytes 7077896 | tf_op jit(solution)/shard_map/ppermute | solution.py:315
  658.2 53.7 %collective-permute-start.33 = (bf16[384,3072]{1,0:T(8,128)(2,1)}, bf16[384,3072]{1,0:T(8,128)(2,1)}, u32[]{:S(2)}, u32[]{:S(2)}) collective-permute-start(bf16[384,3072]{1,0:T(8,128)(2,1)} %get-tuple-element.371), channel_id=1, source_target_pairs={{0,3},{1,2},{2,1},{3,0},{4,7},{5,6},{6,5},{7,4},{8,11},{9,10},{10,... | collective-permute-start | bytes 7077896 | tf_op jit(solution)/shard_map/ppermute | solution.py:315
  669.5 12.2 %slice-start.6 = ((s8[9437184]{0:T(1024)(128)(4,1)}), s8[4194304]{0:T(1024)(128)(4,1)S(1)}, s32[]{:S(2)}) async-start(s8[9437184]{0:T(1024)(128)(4,1)} %bitcast.77), calls=%async_computation.6 | async-start | bytes 8388608
  669.5 12.2 %slice-start.7 = ((s8[9437184]{0:T(1024)(128)(4,1)}), s8[4194304]{0:T(1024)(128)(4,1)S(1)}, s32[]{:S(2)}) async-start(s8[9437184]{0:T(1024)(128)(4,1)} %bitcast.77), calls=%async_computation.7 | async-start | bytes 8388608
  681.7 8.7 %copy-start.9 = (bf16[4,8,48,512]{3,2,1,0:T(8,128)(2,1)S(1)}, bf16[4,8,48,512]{3,2,1,0:T(8,128)(2,1)}, u32[]{:S(2)}) copy-start(bf16[4,8,48,512]{3,2,1,0:T(8,128)(2,1)} %add_convert_fusion.2) | copy-start | bytes 4718596
  694.8 24.8 %copy-start.11 = (f32[8,3072]{1,0:T(8,128)S(1)}, f32[8,3072]{1,0:T(8,128)}, u32[]{:S(2)}) copy-start(f32[8,3072]{1,0:T(8,128)} %get-tuple-element.393) | copy-start | bytes 294916
  720.6 1.2 collective-permute-start.36
  721.8 37.1 %collective-permute-start.37 = (f32[24,128]{1,0:T(8,128)S(1)}, f32[24,128]{1,0:T(8,128)S(1)}, u32[]{:S(2)}, u32[]{:S(2)}) collective-permute-start(f32[24,128]{1,0:T(8,128)S(1)} %bitcast_add_fusion), channel_id=1, source_target_pairs={{0,2},{1,3},{2,0},{3,1},{4,6},{5,7},{6,4},{7,5},{8,10},{9,11},{10,... | collective-permute-start | bytes 36872 | tf_op jit(solution)/shard_map/ppermute | solution.py:315
  758.9 5.0 collective-permute-start.38
  (7 other events, 34.6 us)

commit v2 on v1

--- a/solution.py
+++ b/solution.py
@@ -48,7 +48,7 @@
 
 def place(x, gain, buf, at, axis, normalize=False):
     rows, width = x.shape
-    steps = 4
+    steps = 2
     tile = rows // steps
     shape = (4 * rows, width) if axis == 0 else (rows, 4 * width)
     where = (lambda m: (at * steps + m, 0)) if axis == 0 else (lambda m: (m, at))
@@ -61,10 +61,10 @@
         cost_estimate=cost(1000 * rows * width, 4 * rows * width), name="place")(*ops)
 
 
-def proj_kernel(turned, x_ref, w_ref, cos_ref, sin_ref, o_ref):
-    chunk = x_ref.shape[0] // 4
-    for m in range(4):
-        rows = slice(m * chunk, (m + 1) * chunk)
+def proj_kernel(turned, chunk, x_ref, w_ref, cos_ref, sin_ref, *refs):
+    o_ref = refs[-1]
+    for m in range(0, x_ref.shape[0], chunk):
+        rows = slice(m, m + chunk)
         acc = dot(x_ref[rows], w_ref[...], NN)
         for h in range(acc.shape[1] // HEAD_DIM):
             cols = slice(h * HEAD_DIM, (h + 1) * HEAD_DIM)
@@ -74,17 +74,22 @@
             o_ref[rows, cols] = part.astype(BF16)
 
 
-def project(x, w, cos, sin, first, count, turned):
+def project(x, w, cos, sin, first, count, turned, span=None, buf=None):
     rows, width = x.shape
-    tile = 2 * HEAD_DIM
-    whole = lambda a: pl.BlockSpec(a.shape, lambda n: (0, 0))
-    return pl.pallas_call(
-        functools.partial(proj_kernel, turned), grid=(count,),
-        in_specs=[whole(x), pl.BlockSpec((width, tile), lambda n: (0, first + n)), whole(cos), whole(sin)],
-        out_specs=pl.BlockSpec((rows, tile), lambda n: (0, n)),
+    tile, chunk = 2 * HEAD_DIM, rows // 4
+    at, part = span or (0, rows)
+    some = lambda a: pl.BlockSpec((part, a.shape[1]), lambda n: (at, 0))
+    ops, alias = (x, w, cos, sin), {}
+    specs = [some(x), pl.BlockSpec((width, tile), lambda n: (0, first + n)), some(cos), some(sin)]
+    if buf is not None:
+        alias = {len(ops): 0}
+        ops, specs = ops + (buf,), specs + [ANY]
+    return pl.pallas_call(
+        functools.partial(proj_kernel, turned, chunk), grid=(count,), in_specs=specs,
+        out_specs=pl.BlockSpec((part, tile), lambda n: (at, n)), input_output_aliases=alias,
         out_shape=jax.ShapeDtypeStruct((rows, count * tile), BF16),
         compiler_params=pltpu.CompilerParams(vmem_limit_bytes=VMEM_LIMIT),
-        cost_estimate=cost(2 * rows * width * count * tile, 2 * rows * width), name="project")(x, w, cos, sin)
+        cost_estimate=cost(2 * part * width * count * tile, 2 * part * width), name="project")(*ops)
 
 
 def token_rows(ref, b):
@@ -101,9 +106,8 @@
     return (kidx <= qi_ref[b, :, 0:1]) & (kidx >= qi_ref[b, :, 1:2])
 
 
-def probs(q, k, ok):
-    s = dot(q, k, NT).reshape(-1, ok.shape[0], ok.shape[1])
-    s = jnp.where(ok[None], s, -1e30)
+def probs(scores, ok):
+    s = jnp.where(ok[None], scores.reshape(-1, ok.shape[0], ok.shape[1]), -1e30)
     e = jnp.exp2((s - jnp.max(s, axis=-1, keepdims=True)) * (SCALE * LOG2E))
     return e * (1.0 / jnp.sum(e, axis=-1, keepdims=True))
 
@@ -116,12 +120,13 @@
 def attn_fwd_kernel(q_ref, kv_ref, kr_ref, qi_ref, ki_ref, *refs):
     o_ref = refs[-1]
     shape = (o_ref.shape[0], o_ref.shape[2], HEAD_DIM)
-    for b in range(q_ref.shape[1]):
+    batch = range(q_ref.shape[1])
+    kv = [keys_values(kr_ref, kv_ref, b) for b in batch]
+    scores = [dot(by_head(token_rows(q_ref, b)), kv[b][0], NT) for b in batch]
+    for b in batch:
         ok = allowed_block(qi_ref, ki_ref, b)
-        k, v = keys_values(kr_ref, kv_ref, b)
-        p = probs(by_head(token_rows(q_ref, b)), k, ok).astype(BF16).reshape(-1, k.shape[0])
-        o = dot(p, v, NN).astype(BF16)
         toks = ok.shape[0]
+        o = dot(probs(scores[b], ok).astype(BF16).reshape(scores[b].shape), kv[b][1], NN).astype(BF16)
         for h in range(o.shape[0] // toks):
             o_ref[:, b, :, h * HEAD_DIM:(h + 1) * HEAD_DIM] = o[h * toks:(h + 1) * toks].reshape(shape)
 
@@ -129,19 +134,23 @@
 def attn_bwd_kernel(n_alias, q_ref, kv_ref, kr_ref, do0_ref, do1_ref, do2_ref, do3_ref, qi_ref, ki_ref, cos_ref, sin_ref, cosr_ref, sinr_ref, *refs):
     dq_ref, dkv_ref, dkr_ref = refs[n_alias:]
     shape = (dq_ref.shape[0], dq_ref.shape[2], HEAD_DIM)
-    for b in range(q_ref.shape[1]):
-        ok = allowed_block(qi_ref, ki_ref, b)
-        toks = ok.shape[0]
-        q = by_head(token_rows(q_ref, b))
-        do = by_head(jnp.concatenate([token_rows(d, b) for d in (do0_ref, do1_ref, do2_ref, do3_ref)], axis=0))
-        k, v = keys_values(kr_ref, kv_ref, b)
-        p = probs(q, k, ok)
-        dp = dot(do, v, NT).reshape(p.shape)
-        p_low = p.astype(BF16).reshape(-1, k.shape[0])
-        dv = dot(p_low, do, TN)
-        ds = (p * (dp - jnp.sum(p * dp, axis=-1, keepdims=True))).astype(BF16).reshape(p_low.shape)
-        dq = dot(ds, k, NN) * SCALE
-        dk = dot(ds, q, TN) * SCALE
+    batch = range(q_ref.shape[1])
+    kv = [keys_values(kr_ref, kv_ref, b) for b in batch]
+    q = [by_head(token_rows(q_ref, b)) for b in batch]
+    do = [by_head(jnp.concatenate([token_rows(d, b) for d in (do0_ref, do1_ref, do2_ref, do3_ref)], axis=0)) for b in batch]
+    scores = [dot(q[b], kv[b][0], NT) for b in batch]
+    grad_probs = [dot(do[b], kv[b][1], NT) for b in batch]
+    low, ds = [], []
+    for b in batch:
+        p = probs(scores[b], allowed_block(qi_ref, ki_ref, b))
+        dp = grad_probs[b].reshape(p.shape)
+        low.append(p.astype(BF16).reshape(scores[b].shape))
+        ds.append((p * (dp - jnp.sum(p * dp, axis=-1, keepdims=True))).astype(BF16).reshape(scores[b].shape))
+    for b in batch:
+        toks = kv[b][0].shape[0] // 2
+        dv = dot(low[b], do[b], TN)
+        dk = dot(ds[b], q[b], TN) * SCALE
+        dq = dot(ds[b], kv[b][0], NN) * SCALE
         cos, sin = token_rows(cos_ref, b), token_rows(sin_ref, b)
         for h in range(dq.shape[0] // toks):
             part = dq[h * toks:(h + 1) * toks]
@@ -153,30 +162,30 @@
         dkr_ref[:, b, :, HEAD_DIM:] = dv[:toks].astype(BF16).reshape(shape)
 
 
-ROWS_PER_STEP = 2
-
-
-def block_at(pieces, span, width, col):
-    return pl.BlockSpec((pieces, ROWS_PER_STEP, span, width), lambda b: (0, b, 0, col))
-
-
-def attn_specs(group, q_cols, pieces, span):
+FWD_ROWS, BWD_ROWS = 4, 2
+
+
+def block_at(count, pieces, span, width, col):
+    return pl.BlockSpec((pieces, count, span, width), lambda b: (0, b, 0, col))
+
+
+def attn_specs(count, group, q_cols, pieces, span):
     toks = pieces * span
     s, t = SLOT[group], SLOT[group ^ 2]
     kv_cols = 2 * HEAD_DIM
-    return ([block_at(pieces, span, q_cols, s), block_at(pieces, span, kv_cols, s % 2), block_at(pieces, span, kv_cols, t % 2)],
-            [pl.BlockSpec((ROWS_PER_STEP, toks, 2), lambda b: (b, 0, 0)), pl.BlockSpec((1, 2 * toks), lambda b: (0, 0))])
+    return ([block_at(count, pieces, span, q_cols, s), block_at(count, pieces, span, kv_cols, s % 2), block_at(count, pieces, span, kv_cols, t % 2)],
+            [pl.BlockSpec((count, toks, 2), lambda b: (b, 0, 0)), pl.BlockSpec((1, 2 * toks), lambda b: (0, 0))])
 
 
 def attn_forward(group, q, kv, kvr, qinfo, kinfo, buf):
     pieces, rows, span, q_all = q.shape
     q_cols, toks = q_all // 4, pieces * span
-    big, info = attn_specs(group, q_cols, pieces, span)
+    big, info = attn_specs(FWD_ROWS, group, q_cols, pieces, span)
     ops, specs, alias = (q, kv, kvr, qinfo, kinfo), big + info, {}
     if buf is not None:
         ops, specs, alias = ops + (buf,), specs + [ANY], {5: 0}
     return pl.pallas_call(
-        attn_fwd_kernel, grid=(rows // ROWS_PER_STEP,), in_specs=specs, out_specs=block_at(pieces, span, q_cols, SLOT[group]),
+        attn_fwd_kernel, grid=(rows // FWD_ROWS,), in_specs=specs, out_specs=block_at(FWD_ROWS, pieces, span, q_cols, SLOT[group]),
         out_shape=jax.ShapeDtypeStruct(q.shape, BF16), input_output_aliases=alias,
         compiler_params=pltpu.CompilerParams(vmem_limit_bytes=VMEM_LIMIT),
         cost_estimate=cost(8 * rows * toks * toks * q_cols, 8 * rows * toks * q_cols), name="attn_fwd")(*ops)
@@ -186,10 +195,10 @@
     pieces, rows, span, q_all = q.shape
     q_cols, toks, s = q_all // 4, pieces * span, SLOT[group]
     kv_cols = 2 * HEAD_DIM
-    big, info = attn_specs(group, q_cols, pieces, span)
-    do_spec = pl.BlockSpec((ROWS_PER_STEP, span, q_cols), lambda b: (b, 0, s))
+    big, info = attn_specs(BWD_ROWS, group, q_cols, pieces, span)
+    do_spec = pl.BlockSpec((BWD_ROWS, span, q_cols), lambda b: (b, 0, s))
     ops = (q, kv, kvr, *dos, qinfo, kinfo, *tabs)
-    specs, alias = big + [do_spec] * 4 + info + [block_at(pieces, span, HEAD_DIM, 0)] * 4, {}
+    specs, alias = big + [do_spec] * 4 + info + [block_at(BWD_ROWS, pieces, span, HEAD_DIM, 0)] * 4, {}
     n_alias = 0
     for i, buf in enumerate(bufs):
         if buf is not None:
@@ -197,32 +206,32 @@
             ops, specs, n_alias = ops + (buf,), specs + [ANY], n_alias + 1
     half = (pieces, rows, span, 2 * kv_cols)
     return pl.pallas_call(
-        functools.partial(attn_bwd_kernel, n_alias), grid=(rows // ROWS_PER_STEP,), in_specs=specs,
-        out_specs=[block_at(pieces, span, q_cols, s), block_at(pieces, span, kv_cols, s % 2), block_at(pieces, span, kv_cols, s % 2)],
+        functools.partial(attn_bwd_kernel, n_alias), grid=(rows // BWD_ROWS,), in_specs=specs,
+        out_specs=[block_at(BWD_ROWS, pieces, span, q_cols, s), block_at(BWD_ROWS, pieces, span, kv_cols, s % 2), block_at(BWD_ROWS, pieces, span, kv_cols, s % 2)],
         out_shape=[jax.ShapeDtypeStruct(q.shape, BF16), jax.ShapeDtypeStruct(half, F32), jax.ShapeDtypeStruct(half, BF16)],
         input_output_aliases=alias, compiler_params=pltpu.CompilerParams(vmem_limit_bytes=VMEM_LIMIT),
         cost_estimate=cost(20 * rows * toks * toks * q_cols, 20 * rows * toks * q_cols), name="attn_bwd")(*ops)
 
 
-def grad_in_kernel(dq_ref, da_ref, db_ref, wq_ref, wkv_ref, first_ref, second_ref):
+def grad_in_kernel(dq_ref, da_ref, db_ref, wq_ref, wkv_ref, *outs):
     half = da_ref.shape[1]
     out = dot(dq_ref[...], wq_ref[...], NT) + dot(da_ref[...], wkv_ref[:, :half], NT) + dot(db_ref[...], wkv_ref[:, half:], NT)
-    rows = first_ref.shape[0]
-    first_ref[...] = out[:rows].astype(first_ref.dtype)
-    second_ref[...] = out[rows:].astype(second_ref.dtype)
-
-
-def grad_in(dq, da, db, wq, wkv, pair_at, types):
-    rows, tile = dq.shape[0] // 2, 2 * HEAD_DIM
-    half = lambda a: pl.BlockSpec((rows, a.shape[1]), lambda n: (pair_at, 0))
+    rows = out.shape[0] // len(outs)
+    for i, ref in enumerate(outs):
+        ref[...] = out[i * rows:(i + 1) * rows].astype(ref.dtype)
+
+
+def grad_in(dq, da, db, wq, wkv, at, types):
+    count, width = len(types), wq.shape[0]
+    rows, tile = dq.shape[0] // 4, 4 * HEAD_DIM
+    part = lambda a: pl.BlockSpec((count * rows, a.shape[1]), lambda n: (at, 0))
     row = lambda a: pl.BlockSpec((tile, a.shape[1]), lambda n: (n, 0))
-    out = pl.BlockSpec((rows // 2, tile), lambda n: (0, n))
-    width = wq.shape[0]
-    return pl.pallas_call(
-        grad_in_kernel, grid=(width // tile,), in_specs=[half(dq), half(da), half(db), row(wq), row(wkv)], out_specs=[out, out],
-        out_shape=[jax.ShapeDtypeStruct((rows // 2, width), t) for t in types],
+    return pl.pallas_call(
+        grad_in_kernel, grid=(width // tile,), in_specs=[part(dq), part(da), part(db), row(wq), row(wkv)],
+        out_specs=[pl.BlockSpec((rows, tile), lambda n: (0, n))] * count,
+        out_shape=[jax.ShapeDtypeStruct((rows, width), t) for t in types],
         compiler_params=pltpu.CompilerParams(vmem_limit_bytes=VMEM_LIMIT),
-        cost_estimate=cost(2 * rows * width * (wq.shape[1] + wkv.shape[1]), 4 * rows * width), name="grad_in")(dq, da, db, wq, wkv)
+        cost_estimate=cost(2 * count * rows * width * (wq.shape[1] + wkv.shape[1]), 4 * count * rows * width), name="grad_in")(dq, da, db, wq, wkv)
 
 
 def head_out_kernel(h_ref, w_ref, first_ref, second_ref):
@@ -277,7 +286,7 @@
 
 def half_rows_call(kernel, half, arrays, gain, buf, out_shape, with_part):
     rows, width = arrays[-1].shape
-    steps = 4
+    steps = 4 if with_part else 2
     tile = rows // steps
     mine = pl.BlockSpec((tile, width), lambda m, h: (m, 0))
     full = pl.BlockSpec((tile, width), lambda m, h: (h[0] * steps + m, 0))
@@ -331,7 +340,7 @@
         core = me % 2
         all_rows, span, width = hidden.shape
         rows = all_rows // 2
-        toks = 4 * span
+        toks, half = 4 * span, rows * span
         q_cols = w_query.shape[1]
         split = lambda x: (lax.dynamic_slice_in_dim(x, core * rows, rows), lax.dynamic_slice_in_dim(x, (1 - core) * rows, rows))
         four = lambda x: x.reshape(4, rows, span, x.shape[-1])
@@ -402,6 +411,7 @@
         last[:] = [cos2]
         tabs = (four(cos2), four(sin2), cos_r, sin_r)
 
+        early = [run(lambda x, w: project(x, w, cos2, sin2, 2 * i, 2, 1, (0, 3 * half)), normed, wkv_all) for i in range(2)]
         wq3 = send(after(wq2), mates[1])
         wq_all = put(wq2, wq_all, SLOT[2], 1)
         wq_all = put(wq3, wq_all, SLOT[3], 1)
@@ -409,7 +419,7 @@
 
         kvs, kv_in = [], []
         for i in range(2):
-            kv = four(run(lambda x, w: project(x, w, cos2, sin2, 2 * i, 2, 1), normed, wkv_all))
+            kv = four(run(lambda x, w, e: project(x, w, cos2, sin2, 2 * i, 2, 1, (3, half), e), normed, wkv_all, early[i]))
             kvs.append(kv)
             kv_in.append(send(kv, later))
         q_all = four(run(lambda x, w: project(x, w, cos2, sin2, 0, 2 * q_cols // HEAD_DIM, 2), normed, wq_all))
@@ -425,6 +435,8 @@
             if heads is None:
                 heads = run(lambda q, kv, kr: attn_forward(g, q, kv, kr, qinfo, kinfo, None), q_all, local, far_in)
             else:
+                if SLOT[g] == 2:
+                    grads = put(flat(grd3), grads, 3, 0)
                 heads = run(lambda q, kv, kr, h: attn_forward(g, q, kv, kr, qinfo, kinfo, h), q_all, local, far_in, heads)
         heads_flat = flat(heads)
         att = [None] * 4
@@ -452,39 +464,39 @@
             swapped = jnp.concatenate([theirs[..., 2 * HEAD_DIM:], theirs[..., :2 * HEAD_DIM]], axis=-1)
             return flat((mine + swapped.astype(F32)).astype(BF16))
 
-        grads = put(flat(grd3), grads, 3, 0)
         cut = lambda x, s, n: x[:, s * q_cols:(s + n) * q_cols]
-        so13 = send(run(lambda h, g: dot(cut(h, 0, 2), g, TN).astype(BF16), heads_flat, grads), mates[1])
+        low = lambda x: x.astype(BF16)
+        kv_half = 2 * HEAD_DIM
         dq_flat = flat(dq)
-        low = lambda x: x.astype(BF16)
         spq13 = send(run(lambda d, n: low(dot(n, cut(d, 0, 2), TN)), dq_flat, normed), mates[1])
         dkv_a = run(add_far, dkv[0], dkv_in[0])
         spk13 = send(run(lambda d, n: low(dot(n, d, TN)), dkv_a, normed), mates[1])
+        spq2 = send(run(lambda d, n, e: low(dot(n, cut(d, 3, 1), TN) + e[:, q_cols:].astype(F32)), dq_flat, normed, spq13), pair)
+        so13 = send(run(lambda h, g: low(dot(cut(h, 0, 2), g, TN)), heads_flat, grads), mates[1])
+        dkv_b = run(add_far, dkv[1], dkv_in[1])
+        gn = [None] * 4
+        for p in (2, 3):
+            gn[p] = send(run(lambda *x: grad_in(*x, p, (BF16,))[0], dq_flat, dkv_a, dkv_b, wq_all, wkv_all), mates[p])
+        gn2, gn3 = gn[2], gn[3]
         so1, so3 = run(lambda e: (e[:q_cols], e[q_cols:]), so13)
-        so2 = send(run(lambda h, gg, e: (dot(cut(h, 3, 1), gg, TN) + e.astype(F32)).astype(BF16), heads_flat, grads, so3), pair)
+        so2 = send(run(lambda h, gg, e: low(dot(cut(h, 3, 1), gg, TN) + e.astype(F32)), heads_flat, grads, so3), pair)
+        spk2 = send(run(lambda d, n, e: low(dot(n, d[:, kv_half:], TN) + e[:, kv_half:].astype(F32)), dkv_b, normed, spk13), pair)
         mine_half, other_half = core.astype(jnp.int32)[None], (1 - core).astype(jnp.int32)[None]
         flat_shape = (all_rows * span, width)
         hid_flat, g_flat = flat(hidden), flat(grad_out)
-        dkv_b = run(add_far, dkv[1], dkv_in[1])
-        both = run(lambda d, a, b, wq, wk: grad_in(d, a, b, wq, wk, 1, (BF16, BF16)), dq_flat, dkv_a, dkv_b, wq_all, wkv_all)
-        gn2, gn3 = send(both[0], mates[2]), send(both[1], mates[3])
-        spq2 = send(run(lambda d, n, e: low(dot(n, cut(d, 3, 1), TN) + e[:, q_cols:].astype(F32)), dq_flat, normed, spq13), pair)
-        kv_half = 2 * HEAD_DIM
-        spk2 = send(run(lambda d, n, e: low(dot(n, d[:, kv_half:], TN) + e[:, kv_half:].astype(F32)), dkv_b, normed, spk13), pair)
         own_in, gn1 = run(lambda d, a, b, wq, wk: grad_in(d, a, b, wq, wk, 0, (F32, BF16)), dq_flat, dkv_a, dkv_b, wq_all, wkv_all)
         gn1 = send(gn1, mates[1])
         attn_out = run(lambda x, a, b: half_rows_call(residual_kernel, mine_half, (x, a, b), None, None, flat_shape, False)[0], hid_flat, own_out, flat(att[2]))
         attn_out = run(lambda x, a, b, o: half_rows_call(residual_kernel, other_half, (x, a, b), None, o, flat_shape, False)[0], hid_flat, flat(att[1]), flat(att[3]), attn_out)
         back_call = lambda h, arrays, buf: half_rows_call(norm_back_kernel, h, arrays, gain_row, buf, flat_shape, True)
         grad_hidden, part_a = run(lambda x, g, a, b: back_call(mine_half, (x, g, a, b), None), hid_flat, g_flat, own_in, gn2)
-        dwo = run(lambda h, g, a, b: dot(cut(h, 2, 1), g, TN) + a.astype(F32) + b.astype(F32), heads_flat, grads, so1, so2)
-        own_q = after(run(lambda d, n, e: dot(n, cut(d, 2, 1), TN) + e[:, :q_cols].astype(F32), dq_flat, normed, spq13))
+        dwq = run(lambda d, n, e, f: dot(n, cut(d, 2, 1), TN) + (e[:, :q_cols].astype(F32) + f.astype(F32)), dq_flat, normed, spq13, spq2)
         own_kv = after(run(lambda d, n, e: dot(n, d[:, :kv_half], TN) + e[:, :kv_half].astype(F32), dkv_b, normed, spk13))
+        dwo = run(lambda h, g, a, b: dot(cut(h, 2, 1), g, TN) + (a.astype(F32) + b.astype(F32)), heads_flat, grads, so1, so2)
         grad_hidden, part_b = run(lambda x, g, a, b, o: back_call(other_half, (x, g, a, b), o), hid_flat, g_flat, gn1, gn3, grad_hidden)
         gain_sum = jnp.sum(part_a + part_b, axis=0).reshape(-1, HEAD_DIM)
         for perm in (mates[1], mates[2], pair):
             gain_sum = gain_sum + send(gain_sum, perm)
-        dwq = own_q + spq2.astype(F32)
         dwk = own_kv[:, :HEAD_DIM] + spk2[:, :HEAD_DIM].astype(F32)
         dwv = own_kv[:, HEAD_DIM:] + spk2[:, HEAD_DIM:].astype(F32)
         return attn_out.reshape(hidden.shape), grad_hidden.reshape(hidden.shape), gain_sum.reshape(-1), dwq, dwk, dwv, dwo

time: 777 us -> 788 us (1.014)
  waiting for transfers between devices: 282 us -> 320 us
  Pallas kernels: 298 us -> 273 us
  other arithmetic: 28 us -> 17.4 us
    ppermute x41, waiting for transfers between devices: 282 us -> 320 us  [send(): return lax.ppermute(x, 'tp', perm)]
    pallas_call x20, Pallas kernels: 80.5 us -> 58.5 us  [place(): pl.pallas_call(functools.partial(place_kernel, normalize), grid=(steps,),...]
    add x2 -> x0, other arithmetic: 10.7 us -> none  [the longest x1 5.67 us: device_step(): dwq = own_q + spq2.astype(F32)]
    pallas_call x9 -> x12, Pallas kernels: 113 us -> 117 us  [the longest x5 50.7 us: project(): pl.pallas_call(functools.partial(proj_kernel, turned, chunk), grid=(count...]
  transfers between devices with their start and end apart: 41 -> 41, of which waited for: 16 -> 14; matrix products, arithmetic and copies ran while one was open for 16% -> 13% of each run, Pallas kernels for 31% -> 24%
where the time goes in v2:
time: 788 us; the launch traced here: 777 us
  waiting for transfers between devices  320 us (41%)
  Pallas kernels  273 us (35%)
  matrix products  107 us (14%)
  starting transfers between devices  37.2 us (5%)
  local copies, waits for them, and re-layouts  21.2 us (3%)
  other arithmetic  17.4 us (2%)
    ppermute x41, waiting for transfers between devices, send(): return lax.ppermute(x, 'tp', perm)  320 us
    dot_general x13, matrix products, dot(): return lax.dot_general(a, b, dims, preferred_element_type=F32)  107 us
    pallas_call x20, Pallas kernels, place(): pl.pallas_call(functools.partial(place_kernel, normalize), grid=(steps,),...  58.5 us
    pallas_call x5, Pallas kernels, project(): pl.pallas_call(functools.partial(proj_kernel, turned, chunk), grid=(count...  50.7 us
    pallas_call x4, Pallas kernels, attn_backward(): pl.pallas_call(functools.partial(attn_bwd_kernel, n_alias), grid=(rows //...  48 us
    pallas_call x3, Pallas kernels, grad_in(): pl.pallas_call(grad_in_kernel, grid=(width // tile,), in_specs=[part(dq),...  41.4 us
    ppermute x41, starting transfers between devices, send(): return lax.ppermute(x, 'tp', perm)  37.2 us
    pallas_call x4, Pallas kernels, half_rows_call(): pl.pallas_call(body, grid_spec=pltpu.PrefetchScalarGridSpec(num_scalar_pr...  25.6 us
  transfers between devices with their start and end apart: 41, of which 14 were waited for; matrix products, arithmetic and copies ran while one was open for 13% of the time, Pallas kernels for 24%

profile of v2, /device:TPU:112, one launch (start us, length us, event | category | flops | bytes accessed | tf_op | source)
XLA Modules:
  0.0 776.7 jit_solution(5358433961272216536)
XLA Ops:
  4.8 4.4 constant_dynamic-slice_fusion.4
  13.0 3.9 collective-permute-start.3
  17.4 2.9 place.20.refs_0_
  22.8 2.8 place.22.refs_0_
  25.8 3.6 place.23.refs_0_
  32.2 3.6 place.25.refs_0_
  38.2 2.9 place.27.refs_0_
  46.7 5.4 collective-permute-done.3.x_ref
  57.1 21.8 %collective-permute-done.15 = s32[8,48]{1,0:T(8,128)S(1)} collective-permute-done((s32[8,48]{1,0:T(8,128)S(1)}, s32[8,48]{1,0:T(8,128)S(1)}, u32[]{:S(2)}, u32[]{:S(2)}) %collective-permute-start.15) | collective-permute-done | bytes 1568 | tf_op jit(solution)/shard_map/ppermute | solution.py:324
  92.2 3.6 place.32.x_ref.refs_0_
  97.2 4.4 fusion.8
  101.6 4.4 fusion.7
  106.0 8.9 %project.5.refs_0_ = bf16[1536,512]{1,0:T(8,128)(2,1)} custom-call(bf16[1536,3072]{1,0:T(8,128)(2,1)} %place.32.x_ref.refs_0_, bf16[3072,1024]{1,0:T(8,128)(2,1)} %place.31.w_ref.wkv_ref, f32[1536,128]{1,0:T(8,128)} %get-tuple-element.234.cos_ref, f32[1536,128]{1,0:T(8,128)} %get-tuple-element.237.sin_ref), custom_call_target="tpu_custom_call" | custom-call | flops 3623878656 | bytes 7077888 | tf_op jit(solution)/shard_map/project/pallas_call | solution.py:87
  114.9 8.9 %project.6.refs_0_ = bf16[1536,512]{1,0:T(8,128)(2,1)} custom-call(bf16[1536,3072]{1,0:T(8,128)(2,1)} %place.32.x_ref.refs_0_, bf16[3072,1024]{1,0:T(8,128)(2,1)} %place.31.w_ref.wkv_ref, f32[1536,128]{1,0:T(8,128)} %get-tuple-element.234.cos_ref, f32[1536,128]{1,0:T(8,128)} %get-tuple-element.237.sin_ref), custom_call_target="tpu_custom_call" | custom-call | flops 3623878656 | bytes 7077888 | tf_op jit(solution)/shard_map/project/pallas_call | solution.py:87
  123.8 12.9 %collective-permute-done.9.x_ref = bf16[3072,384]{1,0:T(8,128)(2,1)} collective-permute-done((bf16[3072,384]{1,0:T(8,128)(2,1)}, bf16[3072,384]{1,0:T(8,128)(2,1)}, u32[]{:S(2)}, u32[]{:S(2)}) %collective-permute-start.9) | collective-permute-done | bytes 2359328 | tf_op jit(solution)/shard_map/ppermute | solution.py:324
  137.8 3.0 place.33.refs_0_
  141.5 2.9 place.34.w_ref.wq_ref
  144.5 45.3 %collective-permute-done = bf16[8,48,3072]{2,1,0:T(8,128)(2,1)S(1)} collective-permute-done((bf16[8,48,3072]{2,1,0:T(8,128)(2,1)}, bf16[8,48,3072]{2,1,0:T(8,128)(2,1)S(1)}, u32[]{:S(2)}, u32[]{:S(2)}) %collective-permute-start) | collective-permute-done | bytes 2359328 | tf_op jit(solution)/shard_map/ppermute | solution.py:324
  191.1 3.6 place.35.x_ref
  194.7 4.6 project.7
  199.4 4.6 project.8
  204.0 23.6 %project.9 = bf16[1536,1536]{1,0:T(8,128)(2,1)} custom-call(bf16[1536,3072]{1,0:T(8,128)(2,1)} %place.35.x_ref, bf16[3072,1536]{1,0:T(8,128)(2,1)} %place.34.w_ref.wq_ref, f32[1536,128]{1,0:T(8,128)} %get-tuple-element.234.cos_ref, f32[1536,128]{1,0:T(8,128)} %get-tuple-element.237.sin_ref), custom_call_target="tpu_custom_call" | custom-call | flops 14495514624 | bytes 9437184 | tf_op jit(solution)/shard_map/project/pallas_call | solution.py:87
  230.2 4.2 collective-permute-start.18
  237.0 2.8 place.36.refs_0_
  242.6 9.4 %convolution_convert_fusion.6 = bf16[384,1536]{1,0:T(8,128)(2,1)} fusion(bf16[384,3072]{1,0:T(8,128)(2,1)} %bitcast.165, bf16[1536,3072]{1,0:T(8,128)(2,1)} %place.37.w_ref), kind=kOutput, calls=%fused_computation.15 | convolution fusion | flops 3624468480 | bytes 12976128 | tf_op jit(solution)/shard_map/dot_general | solution.py:28
  252.0 6.7 convolution_convert_fusion.5
  258.8 74.2 %collective-permute-done.20 = bf16[8,48,3072]{2,1,0:T(8,128)(2,1)} collective-permute-done((bf16[8,48,3072]{2,1,0:T(8,128)(2,1)}, bf16[8,48,3072]{2,1,0:T(8,128)(2,1)}, u32[]{:S(2)}, u32[]{:S(2)}) %collective-permute-start.20) | collective-permute-done | bytes 2359328 | tf_op jit(solution)/shard_map/ppermute | solution.py:324
  333.0 6.8 convolution_convert_fusion.4
  339.7 2.8 place.38.refs_0_
  342.5 6.1 attn_fwd.4.refs_0_
  348.6 6.3 attn_fwd.5.refs_0_
  354.9 2.9 place.39
  357.8 6.0 attn_fwd.6.refs_0_
  363.8 6.1 attn_fwd.7
  369.9 11.8 %head_out.2 = (bf16[384,3072]{1,0:T(8,128)(2,1)}, bf16[384,3072]{1,0:T(8,128)(2,1)}) custom-call(bf16[1536,1536]{1,0:T(8,128)(2,1)} %bitcast.101, bf16[1536,3072]{1,0:T(8,128)(2,1)} %place.37.w_ref), custom_call_target="tpu_custom_call" | custom-call | flops 7247757312 | bytes 9437184 | tf_op jit(solution)/shard_map/head_out/pallas_call | solution.py:247
  381.7 12.3 %head_out.3 = (f32[384,3072]{1,0:T(8,128)}, bf16[384,3072]{1,0:T(8,128)(2,1)}) custom-call(bf16[1536,1536]{1,0:T(8,128)(2,1)} %bitcast.102, bf16[1536,3072]{1,0:T(8,128)(2,1)} %place.37.w_ref), custom_call_target="tpu_custom_call" | custom-call | flops 7247757312 | bytes 9437184 | tf_op jit(solution)/shard_map/head_out/pallas_call | solution.py:247
  393.9 9.3 %convolution_convert_fusion.3 = bf16[384,1536]{1,0:T(8,128)(2,1)} fusion(bf16[384,3072]{1,0:T(8,128)(2,1)} %bitcast.35.x_ref, bf16[1536,3072]{1,0:T(8,128)(2,1)} %place.37.w_ref), kind=kOutput, calls=%fused_computation.12 | convolution fusion | flops 3624468480 | bytes 12976128 | tf_op jit(solution)/shard_map/dot_general | solution.py:28
  403.2 12.3 %attn_bwd.4 = (bf16[4,8,48,1536]{3,2,1,0:T(8,128)(2,1)}, f32[4,8,48,512]{3,2,1,0:T(8,128)}, bf16[4,8,48,512]{3,2,1,0:T(8,128)(2,1)}) custom-call(bf16[4,8,48,1536]{3,2,1,0:T(8,128)(2,1)} %bitcast.83, bf16[4,8,48,512]{3,2,1,0:T(8,128)(2,1)} %bitcast.126, bf16[4,8,48,512]{3,2,1,0:T(8,128)(2,1)} %collective-permute-done.19.kr_ref, ...), custom_call_target="tpu_custom_call" | custom-call | flops 2264924160 | bytes 11796480 | tf_op jit(solution)/shard_map/attn_bwd/pallas_call | solution.py:208
  415.5 11.9 %attn_bwd.5 = (bf16[4,8,48,1536]{3,2,1,0:T(8,128)(2,1)}, f32[4,8,48,512]{3,2,1,0:T(8,128)}, bf16[4,8,48,512]{3,2,1,0:T(8,128)(2,1)}) custom-call(bf16[4,8,48,1536]{3,2,1,0:T(8,128)(2,1)} %bitcast.84, bf16[4,8,48,512]{3,2,1,0:T(8,128)(2,1)} %bitcast.127, ...), custom_call_target="tpu_custom_call", output_to_operand_aliasing={{0}: (13, {}), {1}: (14, {}), {2}: (15, {})} | custom-call | flops 2264924160 | bytes 11796480 | tf_op jit(solution)/shard_map/attn_bwd/pallas_call | solution.py:208
  427.4 11.9 %attn_bwd.6 = (bf16[4,8,48,1536]{3,2,1,0:T(8,128)(2,1)}, f32[4,8,48,512]{3,2,1,0:T(8,128)}, bf16[4,8,48,512]{3,2,1,0:T(8,128)(2,1)}) custom-call(bf16[4,8,48,1536]{3,2,1,0:T(8,128)(2,1)} %bitcast.85, bf16[4,8,48,512]{3,2,1,0:T(8,128)(2,1)} %bitcast.132, bf16[4,8,48,512]{3,2,1,0:T(8,128)(2,1)} %collective-permute-done.18.kr_ref, ...), custom_call_target="tpu_custom_call", output_to_operand_aliasing={{0}: (13, {})} | custom-call | flops 2264924160 | bytes 11796480 | tf_op jit(solution)/shard_map/attn_bwd/pallas_call | solution.py:208
  439.3 11.9 %attn_bwd.7 = (bf16[4,8,48,1536]{3,2,1,0:T(8,128)(2,1)}, f32[4,8,48,512]{3,2,1,0:T(8,128)}, bf16[4,8,48,512]{3,2,1,0:T(8,128)(2,1)}) custom-call(bf16[4,8,48,1536]{3,2,1,0:T(8,128)(2,1)} %bitcast.86, bf16[4,8,48,512]{3,2,1,0:T(8,128)(2,1)} %bitcast.133, ...), custom_call_target="tpu_custom_call", output_to_operand_aliasing={{0}: (13, {}), {1}: (14, {}), {2}: (15, {})} | custom-call | flops 2264924160 | bytes 11796480 | tf_op jit(solution)/shard_map/attn_bwd/pallas_call | solution.py:208
  451.2 12.6 %convolution_convert_fusion = bf16[3072,768]{1,0:T(8,128)(2,1)} fusion(bf16[1536,3072]{1,0:T(8,128)(2,1)} %place.35.x_ref, bf16[1536,1536]{1,0:T(8,128)(2,1)} %bitcast.95), kind=kOutput, calls=%fused_computation | convolution fusion | flops 7250116608 | bytes 16515072 | tf_op jit(solution)/shard_map/dot_general | solution.py:28
  465.5 38.5 %collective-permute-done.27 = bf16[4,8,48,512]{3,2,1,0:T(8,128)(2,1)S(1)} collective-permute-done((bf16[4,8,48,512]{3,2,1,0:T(8,128)(2,1)S(1)}, bf16[4,8,48,512]{3,2,1,0:T(8,128)(2,1)S(1)}, u32[]{:S(2)}, u32[]{:S(2)}) %collective-permute-start.27) | collective-permute-done | bytes 1572896 | tf_op jit(solution)/shard_map/ppermute | solution.py:324
  504.8 6.5 convolution_convert_fusion.2
  513.5 7.7 add_convert_fusion.1
  521.3 9.2 %convolution_convert_fusion.1 = bf16[768,3072]{1,0:T(8,128)(2,1)} fusion(bf16[1536,3072]{1,0:T(8,128)(2,1)S(1)} %bitcast.88, bf16[1536,1536]{1,0:T(8,128)(2,1)S(1)} %bitcast.107), kind=kOutput, calls=%fused_computation.1 | convolution fusion | flops 7250116608 | bytes 16515072 | tf_op jit(solution)/shard_map/dot_general | solution.py:28
  534.3 36.1 %collective-permute-done.28 = bf16[4,8,48,512]{3,2,1,0:T(8,128)(2,1)S(1)} collective-permute-done((bf16[4,8,48,512]{3,2,1,0:T(8,128)(2,1)S(1)}, bf16[4,8,48,512]{3,2,1,0:T(8,128)(2,1)S(1)}, u32[]{:S(2)}, u32[]{:S(2)}) %collective-permute-start.28) | collective-permute-done | bytes 1572896 | tf_op jit(solution)/shard_map/ppermute | solution.py:324
  572.3 12.1 %grad_in.3 = bf16[384,3072]{1,0:T(8,128)(2,1)} custom-call(bf16[1536,1536]{1,0:T(8,128)(2,1)} %bitcast.97, bf16[1536,512]{1,0:T(8,128)(2,1)} %bitcast.161, bf16[1536,512]{1,0:T(8,128)(2,1)} %bitcast.155, bf16[3072,1536]{1,0:T(8,128)(2,1)} %place.34.w_ref.wq_ref, bf16[3072,1024]{1,0:T(8,128)(2,1)} %place.31.w_ref.wkv_ref), custom_call_target="tpu_custom_call" | custom-call | flops 6039797760 | bytes 4718592 | tf_op jit(solution)/shard_map/grad_in/pallas_call | solution.py:229
  584.4 11.9 %grad_in.4 = bf16[384,3072]{1,0:T(8,128)(2,1)} custom-call(bf16[1536,1536]{1,0:T(8,128)(2,1)} %bitcast.98, bf16[1536,512]{1,0:T(8,128)(2,1)} %bitcast.162, bf16[1536,512]{1,0:T(8,128)(2,1)} %bitcast.156, bf16[3072,1536]{1,0:T(8,128)(2,1)} %place.34.w_ref.wq_ref, bf16[3072,1024]{1,0:T(8,128)(2,1)} %place.31.w_ref.wkv_ref), custom_call_target="tpu_custom_call" | custom-call | flops 6039797760 | bytes 4718592 | tf_op jit(solution)/shard_map/grad_in/pallas_call | solution.py:229
  596.4 4.3 fusion.11
  600.7 9.9 %add_convert_fusion = bf16[384,3072]{1,0:T(8,128)(2,1)} fusion(bf16[384,3072]{1,0:T(8,128)(2,1)S(1)} %get-tuple-element.372, bf16[1536,3072]{1,0:T(8,128)(2,1)} %place.39, bf16[1536,1536]{1,0:T(8,128)(2,1)} %bitcast.103), kind=kOutput, calls=%fused_computation.4 | convolution fusion | flops 3627417600 | bytes 15335424 | tf_op jit(solution)/shard_map/dot_general | solution.py:28
  610.7 5.1 fusion
  615.8 17.3 %grad_in.5 = (f32[384,3072]{1,0:T(8,128)}, bf16[384,3072]{1,0:T(8,128)(2,1)}) custom-call(bf16[1536,1536]{1,0:T(8,128)(2,1)} %bitcast.99, bf16[1536,512]{1,0:T(8,128)(2,1)} %bitcast.163, bf16[1536,512]{1,0:T(8,128)(2,1)} %bitcast.157, bf16[3072,1536]{1,0:T(8,128)(2,1)} %place.34.w_ref.wq_ref, bf16[3072,1024]{1,0:T(8,128)(2,1)} %place.31.w_ref.wkv_ref), custom_call_target="tpu_custom_call" | custom-call | flops 12079595520 | bytes 9437184 | tf_op jit(solution)/shard_map/grad_in/pallas_call | solution.py:229
  635.0 5.2 shard_map.135.refs_3_
  643.4 4.6 shard_map.136
  648.0 39.8 %collective-permute-done.34.refs_3_ = bf16[384,3072]{1,0:T(8,128)(2,1)} collective-permute-done((bf16[384,3072]{1,0:T(8,128)(2,1)}, bf16[384,3072]{1,0:T(8,128)(2,1)}, u32[]{:S(2)}, u32[]{:S(2)}) %collective-permute-start.34) | collective-permute-done | bytes 2359328 | tf_op jit(solution)/shard_map/ppermute | solution.py:324
  687.7 7.9 %shard_map.137 = (bf16[768,3072]{1,0:T(8,128)(2,1)}, f32[8,3072]{1,0:T(8,128)}) custom-call(s32[1]{0:T(128)} %bitcast.37.h_ref, bf16[768,3072]{1,0:T(8,128)(2,1)} %bitcast.93, bf16[768,3072]{1,0:T(8,128)(2,1)} %bitcast.134, f32[384,3072]{1,0:T(8,128)} %get-tuple-element.392.refs_2_, bf16[384,3072]{1,0:T(8,128)(2,1)} %collective-permute-done.34.refs_3_, ...), custom_call_target="tpu_custom_call" | custom-call | flops 1179648000 | bytes 11796480 | tf_op jit(solution)/shard_map/pallas_call | solution.py:308
  695.7 10.8 %add_add_fusion.1 = f32[3072,384]{1,0:T(8,128)} fusion(bf16[3072,384]{1,0:T(8,128)(2,1)} %collective-permute-done.36, bf16[1536,3072]{1,0:T(8,128)(2,1)} %place.35.x_ref, bf16[3072,768]{1,0:T(8,128)(2,1)} %copy-done.16, bf16[1536,1536]{1,0:T(8,128)(2,1)} %bitcast.100), kind=kOutput, calls=%fused_computation.3 | convolution fusion | flops 3628597248 | bytes 20054016 | tf_op jit(solution)/shard_map/dot_general | solution.py:28
  706.7 5.4 convolution_add_fusion
  712.1 37.8 %collective-permute-done.35 = bf16[384,3072]{1,0:T(8,128)(2,1)S(1)} collective-permute-done((bf16[384,3072]{1,0:T(8,128)(2,1)}, bf16[384,3072]{1,0:T(8,128)(2,1)S(1)}, u32[]{:S(2)}, u32[]{:S(2)}) %collective-permute-start.35) | collective-permute-done | bytes 2359328 | tf_op jit(solution)/shard_map/ppermute | solution.py:324
  750.0 7.0 add_add_fusion
  757.0 7.9 %shard_map.138 = (bf16[768,3072]{1,0:T(8,128)(2,1)}, f32[8,3072]{1,0:T(8,128)}) custom-call(s32[1]{0:T(128)} %bitcast.h_ref, bf16[768,3072]{1,0:T(8,128)(2,1)} %bitcast.94, bf16[768,3072]{1,0:T(8,128)(2,1)} %bitcast.135, bf16[384,3072]{1,0:T(8,128)(2,1)} %collective-permute-done.32.refs_2_, ...), custom_call_target="tpu_custom_call", output_to_operand_aliasing={{0}: (6, {})} | custom-call | flops 1179648000 | bytes 11796480 | tf_op jit(solution)/shard_map/pallas_call | solution.py:308
  767.6 3.2 collective-permute-done.38
  771.1 3.3 convert_add_fusion
  (190 shorter events, 73.0 us)
Async XLA Ops:
  4.8 8.2 %collective-permute-start.7 = (bf16[3072,256]{1,0:T(8,128)(2,1)}, bf16[3072,256]{1,0:T(8,128)(2,1)}, u32[]{:S(2)}, u32[]{:S(2)}) collective-permute-start(bf16[3072,256]{1,0:T(8,128)(2,1)} %constant_dynamic-update-slice_fusion.x_ref), channel_id=1, source_target_pairs={{0,1},{1,0},{2,3},{3,2},{4,5},{5,4},{6,7},{7,6},{8,9},{9,8},{10,11... | collective-permute-start | bytes 4718600 | tf_op jit(solution)/shard_map/ppermute | solution.py:324
  9.2 16.5 %copy-start.8 = (bf16[8,48,3072]{2,1,0:T(8,128)(2,1)}, bf16[8,48,3072]{2,1,0:T(8,128)(2,1)S(1)}, u32[]{:S(2)}) copy-start(bf16[8,48,3072]{2,1,0:T(8,128)(2,1)S(1)} %get-tuple-element.421) | copy-start | bytes 7077892
  9.2 16.5 %collective-permute-start.2 = (bf16[8,48,3072]{2,1,0:T(8,128)(2,1)}, bf16[8,48,3072]{2,1,0:T(8,128)(2,1)}, u32[]{:S(2)}, u32[]{:S(2)}) collective-permute-start(bf16[8,48,3072]{2,1,0:T(8,128)(2,1)} %get-tuple-element.422), channel_id=1, source_target_pairs={{0,1},{1,0},{2,3},{3,2},{4,5},{5,4},{6,7},{7,6},{8,9},{9,8},{10,11... | collective-permute-start | bytes 7077896 | tf_op jit(solution)/shard_map/ppermute | solution.py:324
  9.7 28.6 %collective-permute-start.6 = (bf16[3072,384]{1,0:T(8,128)(2,1)}, bf16[3072,384]{1,0:T(8,128)(2,1)}, u32[]{:S(2)}, u32[]{:S(2)}) collective-permute-start(bf16[3072,384]{1,0:T(8,128)(2,1)} %x_ref.1), channel_id=1, source_target_pairs={{0,1},{1,0},{2,3},{3,2},{4,5},{5,4},{6,7},{7,6},{8,9},{9,8},{10,11... | collective-permute-start | bytes 7077896 | tf_op jit(solution)/shard_map/ppermute | solution.py:324
  9.7 31.4 %collective-permute-start.5 = (bf16[384,3072]{1,0:T(8,128)(2,1)}, bf16[384,3072]{1,0:T(8,128)(2,1)}, u32[]{:S(2)}, u32[]{:S(2)}) collective-permute-start(bf16[384,3072]{1,0:T(8,128)(2,1)} %x_ref.2), channel_id=1, source_target_pairs={{0,1},{1,0},{2,3},{3,2},{4,5},{5,4},{6,7},{7,6},{8,9},{9,8},{10,11... | collective-permute-start | bytes 7077896 | tf_op jit(solution)/shard_map/ppermute | solution.py:324
  12.9 31.0 %collective-permute-start.4 = (bf16[8,48,3072]{2,1,0:T(8,128)(2,1)}, bf16[8,48,3072]{2,1,0:T(8,128)(2,1)}, u32[]{:S(2)}, u32[]{:S(2)}) collective-permute-start(bf16[8,48,3072]{2,1,0:T(8,128)(2,1)} %get-tuple-element.419), channel_id=1, source_target_pairs={{0,1},{1,0},{2,3},{3,2},{4,5},{5,4},{6,7},{7,6},{8,9},{9,8},{10,11... | collective-permute-start | bytes 7077896 | tf_op jit(solution)/shard_map/ppermute | solution.py:324
  13.0 39.2 %collective-permute-start.3 = (bf16[3072,256]{1,0:T(8,128)(2,1)}, bf16[3072,256]{1,0:T(8,128)(2,1)}, u32[]{:S(2)}, u32[]{:S(2)}) collective-permute-start(bf16[3072,256]{1,0:T(8,128)(2,1)} %constant_dynamic-update-slice_fusion.x_ref), channel_id=1, source_target_pairs={{0,6},{1,7},{2,4},{3,5},{4,2},{5,3},{6,0},{7,1},{8,14},{9,15},{10,... | collective-permute-start | bytes 4718600 | tf_op jit(solution)/shard_map/ppermute | solution.py:324
  25.7 66.6 %collective-permute-start.1 = (bf16[8,48,3072]{2,1,0:T(8,128)(2,1)S(1)}, bf16[8,48,3072]{2,1,0:T(8,128)(2,1)}, u32[]{:S(2)}, u32[]{:S(2)}) collective-permute-start(bf16[8,48,3072]{2,1,0:T(8,128)(2,1)S(1)} %get-tuple-element.421), channel_id=1, source_target_pairs={{0,2},{1,3},{2,0},{3,1},{4,6},{5,7},{6,4},{7,5},{8,10},{9,11},{10,... | collective-permute-start | bytes 7077896 | tf_op jit(solution)/shard_map/ppermute | solution.py:324
  52.2 37.6 %collective-permute-start.8 = (bf16[3072,256]{1,0:T(8,128)(2,1)}, bf16[3072,256]{1,0:T(8,128)(2,1)}, u32[]{:S(2)}, u32[]{:S(2)}) collective-permute-start(bf16[3072,256]{1,0:T(8,128)(2,1)} %collective-permute-done.3.x_ref), channel_id=1, source_target_pairs={{0,1},{1,0},{2,3},{3,2},{4,5},{5,4},{6,7},{7,6},{8,9},{9,8},{10,11... | collective-permute-start | bytes 4718600 | tf_op jit(solution)/shard_map/ppermute | solution.py:324
  52.2 26.7 %collective-permute-start.15 = (s32[8,48]{1,0:T(8,128)S(1)}, s32[8,48]{1,0:T(8,128)S(1)}, u32[]{:S(2)}, u32[]{:S(2)}) collective-permute-start(s32[8,48]{1,0:T(8,128)S(1)} %get-tuple-element.433), channel_id=1, source_target_pairs={{4,0},{5,1},{6,2},{7,3},{0,4},{1,5},{2,6},{3,7},{12,8},{13,9},{14,... | collective-permute-start | bytes 4616 | tf_op jit(solution)/shard_map/ppermute | solution.py:324
  54.1 25.7 %collective-permute-start.13 = (s32[8,48]{1,0:T(8,128)S(1)}, s32[8,48]{1,0:T(8,128)S(1)}, u32[]{:S(2)}, u32[]{:S(2)}) collective-permute-start(s32[8,48]{1,0:T(8,128)S(1)} %get-tuple-element.433), channel_id=1, source_target_pairs={{6,0},{7,1},{4,2},{5,3},{2,4},{3,5},{0,6},{1,7},{14,8},{15,9},{12,... | collective-permute-start | bytes 4616 | tf_op jit(solution)/shard_map/ppermute | solution.py:324
  55.3 26.2 %collective-permute-start.11 = (s32[8,48]{1,0:T(8,128)S(1)}, s32[8,48]{1,0:T(8,128)S(1)}, u32[]{:S(2)}, u32[]{:S(2)}) collective-permute-start(s32[8,48]{1,0:T(8,128)S(1)} %get-tuple-element.433), channel_id=1, source_target_pairs={{0,2},{1,3},{2,0},{3,1},{4,6},{5,7},{6,4},{7,5},{8,10},{9,11},{10,... | collective-permute-start | bytes 4616 | tf_op jit(solution)/shard_map/ppermute | solution.py:324
  78.9 5.3 collective-permute-start.16
  79.8 4.5 collective-permute-start.14
  81.5 55.2 %collective-permute-start.9 = (bf16[3072,384]{1,0:T(8,128)(2,1)}, bf16[3072,384]{1,0:T(8,128)(2,1)}, u32[]{:S(2)}, u32[]{:S(2)}) collective-permute-start(bf16[3072,384]{1,0:T(8,128)(2,1)} %x_ref.1), channel_id=1, source_target_pairs={{0,6},{1,7},{2,4},{3,5},{4,2},{5,3},{6,0},{7,1},{8,14},{9,15},{10,... | collective-permute-start | bytes 7077896 | tf_op jit(solution)/shard_map/ppermute | solution.py:324
  84.2 3.1 collective-permute-start.12
  84.3 3.0 collective-permute-start.10
  136.7 4.9 collective-permute-start.17
  136.7 53.1 %collective-permute-start = (bf16[8,48,3072]{2,1,0:T(8,128)(2,1)}, bf16[8,48,3072]{2,1,0:T(8,128)(2,1)S(1)}, u32[]{:S(2)}, u32[]{:S(2)}) collective-permute-start(bf16[8,48,3072]{2,1,0:T(8,128)(2,1)} %get-tuple-element.422), channel_id=1, source_target_pairs={{0,3},{1,2},{2,1},{3,0},{4,7},{5,6},{6,5},{7,4},{8,11},{9,10},{10,... | collective-permute-start | bytes 7077896 | tf_op jit(solution)/shard_map/ppermute | solution.py:324
  136.7 91.0 %collective-permute-start.21 = (bf16[384,3072]{1,0:T(8,128)(2,1)}, bf16[384,3072]{1,0:T(8,128)(2,1)}, u32[]{:S(2)}, u32[]{:S(2)}) collective-permute-start(bf16[384,3072]{1,0:T(8,128)(2,1)} %x_ref.2), channel_id=1, source_target_pairs={{0,6},{1,7},{2,4},{3,5},{4,2},{5,3},{6,0},{7,1},{8,14},{9,15},{10,... | collective-permute-start | bytes 7077896 | tf_op jit(solution)/shard_map/ppermute | solution.py:324
  204.0 30.5 %copy-start.1 = (bf16[1536,512]{1,0:T(8,128)(2,1)S(1)}, bf16[1536,512]{1,0:T(8,128)(2,1)}, u32[]{:S(2)}) copy-start(bf16[1536,512]{1,0:T(8,128)(2,1)} %project.7) | copy-start | bytes 4718596
  227.6 12.2 %collective-permute-start.22 = (bf16[384,3072]{1,0:T(8,128)(2,1)}, bf16[384,3072]{1,0:T(8,128)(2,1)}, u32[]{:S(2)}, u32[]{:S(2)}) collective-permute-start(bf16[384,3072]{1,0:T(8,128)(2,1)} %collective-permute-done.21.x_ref), channel_id=1, source_target_pairs={{0,1},{1,0},{2,3},{3,2},{4,5},{5,4},{6,7},{7,6},{8,9},{9,8},{10,11... | collective-permute-start | bytes 7077896 | tf_op jit(solution)/shard_map/ppermute | solution.py:324
  228.5 126.3 %collective-permute-start.23 = (bf16[8,48,3072]{2,1,0:T(8,128)(2,1)}, bf16[8,48,3072]{2,1,0:T(8,128)(2,1)}, u32[]{:S(2)}, u32[]{:S(2)}) collective-permute-start(bf16[8,48,3072]{2,1,0:T(8,128)(2,1)} %get-tuple-element.419), channel_id=1, source_target_pairs={{0,3},{1,2},{2,1},{3,0},{4,7},{5,6},{6,5},{7,4},{8,11},{9,10},{10,... | collective-permute-start | bytes 7077896 | tf_op jit(solution)/shard_map/ppermute | solution.py:324
  228.6 104.3 %collective-permute-start.20 = (bf16[8,48,3072]{2,1,0:T(8,128)(2,1)}, bf16[8,48,3072]{2,1,0:T(8,128)(2,1)}, u32[]{:S(2)}, u32[]{:S(2)}) collective-permute-start(bf16[8,48,3072]{2,1,0:T(8,128)(2,1)} %get-tuple-element.420), channel_id=1, source_target_pairs={{0,2},{1,3},{2,0},{3,1},{4,6},{5,7},{6,4},{7,5},{8,10},{9,11},{10,... | collective-permute-start | bytes 7077896 | tf_op jit(solution)/shard_map/ppermute | solution.py:324
  230.2 127.5 %collective-permute-start.18 = (bf16[4,8,48,512]{3,2,1,0:T(8,128)(2,1)}, bf16[4,8,48,512]{3,2,1,0:T(8,128)(2,1)}, u32[]{:S(2)}, u32[]{:S(2)}) collective-permute-start(bf16[4,8,48,512]{3,2,1,0:T(8,128)(2,1)} %bitcast.129), channel_id=1, source_target_pairs={{0,6},{1,7},{2,4},{3,5},{8,14},{9,15},{10,12},{11,13}} | collective-permute-start | bytes 4718600 | tf_op jit(solution)/shard_map/ppermute | solution.py:324
  234.5 108.1 %collective-permute-start.19 = (bf16[4,8,48,512]{3,2,1,0:T(8,128)(2,1)S(1)}, bf16[4,8,48,512]{3,2,1,0:T(8,128)(2,1)}, u32[]{:S(2)}, u32[]{:S(2)}) collective-permute-start(bf16[4,8,48,512]{3,2,1,0:T(8,128)(2,1)S(1)} %bitcast.128), channel_id=1, source_target_pairs={{0,6},{1,7},{2,4},{3,5},{8,14},{9,15},{10,12},{11,13}} | collective-permute-start | bytes 4718600 | tf_op jit(solution)/shard_map/ppermute | solution.py:324
  439.3 65.5 %slice-start = ((s8[9437184]{0:T(1024)(128)(4,1)}), s8[1048576]{0:T(1024)(128)(4,1)S(1)}, s32[]{:S(2)}) async-start(s8[9437184]{0:T(1024)(128)(4,1)} %bitcast.73), calls=%async_computation | async-start | bytes 2097152
  451.2 12.7 %copy-start.12 = (bf16[4,8,48,512]{3,2,1,0:T(8,128)(2,1)S(1)}, bf16[4,8,48,512]{3,2,1,0:T(8,128)(2,1)}, u32[]{:S(2)}) copy-start(bf16[4,8,48,512]{3,2,1,0:T(8,128)(2,1)} %get-tuple-element.343) | copy-start | bytes 4718596
  451.2 53.5 %slice-start.1 = ((s8[9437184]{0:T(1024)(128)(4,1)}), s8[4194304]{0:T(1024)(128)(4,1)S(1)}, s32[]{:S(2)}) async-start(s8[9437184]{0:T(1024)(128)(4,1)} %bitcast.73), calls=%async_computation.1 | async-start | bytes 8388608
  451.2 53.5 %slice-start.2 = ((s8[9437184]{0:T(1024)(128)(4,1)}), s8[4194304]{0:T(1024)(128)(4,1)S(1)}, s32[]{:S(2)}) async-start(s8[9437184]{0:T(1024)(128)(4,1)} %bitcast.73), calls=%async_computation.2 | async-start | bytes 8388608
  463.9 40.2 %copy-start.6 = (f32[4,8,48,512]{3,2,1,0:T(8,128)S(1)}, f32[4,8,48,512]{3,2,1,0:T(8,128)}, u32[]{:S(2)}) copy-start(f32[4,8,48,512]{3,2,1,0:T(8,128)} %get-tuple-element.346) | copy-start | bytes 9437188
  463.9 47.4 %collective-permute-start.29 = (bf16[3072,768]{1,0:T(8,128)(2,1)}, bf16[3072,768]{1,0:T(8,128)(2,1)S(1)}, u32[]{:S(2)}, u32[]{:S(2)}) collective-permute-start(bf16[3072,768]{1,0:T(8,128)(2,1)} %convolution_convert_fusion), channel_id=1, source_target_pairs={{0,1},{1,0},{2,3},{3,2},{4,5},{5,4},{6,7},{7,6},{8,9},{9,8},{10,11... | collective-permute-start | bytes 14155784 | tf_op jit(solution)/shard_map/ppermute | solution.py:324
  463.9 40.1 %collective-permute-start.27 = (bf16[4,8,48,512]{3,2,1,0:T(8,128)(2,1)S(1)}, bf16[4,8,48,512]{3,2,1,0:T(8,128)(2,1)S(1)}, u32[]{:S(2)}, u32[]{:S(2)}) collective-permute-start(bf16[4,8,48,512]{3,2,1,0:T(8,128)(2,1)S(1)} %copy-done.12), channel_id=1, source_target_pairs={{4,2},{5,3},{6,0},{7,1},{12,10},{13,11},{14,8},{15,9}} | collective-permute-start | bytes 4718600 | tf_op jit(solution)/shard_map/ppermute | solution.py:324
  504.1 17.2 %slice-start.15 = ((s8[4718592]{0:T(1024)(128)(4,1)}), s8[4194304]{0:T(1024)(128)(4,1)S(1)}, s32[]{:S(2)}) async-start(s8[4718592]{0:T(1024)(128)(4,1)} %bitcast.105), calls=%async_computation.15 | async-start | bytes 8388608
  504.8 16.5 %slice-start.9 = ((s8[9437184]{0:T(1024)(128)(4,1)}), s8[4194304]{0:T(1024)(128)(4,1)S(1)}, s32[]{:S(2)}) async-start(s8[9437184]{0:T(1024)(128)(4,1)} %bitcast.87), calls=%async_computation.9 | async-start | bytes 8388608
  504.8 16.5 %slice-start.10 = ((s8[9437184]{0:T(1024)(128)(4,1)}), s8[4194304]{0:T(1024)(128)(4,1)S(1)}, s32[]{:S(2)}) async-start(s8[9437184]{0:T(1024)(128)(4,1)} %bitcast.87), calls=%async_computation.10 | async-start | bytes 8388608
  504.8 16.5 %slice-start.16 = ((s8[4718592]{0:T(1024)(128)(4,1)}), s8[524288]{0:T(1024)(128)(4,1)S(1)}, s32[]{:S(2)}) async-start(s8[4718592]{0:T(1024)(128)(4,1)} %bitcast.105), calls=%async_computation.16 | async-start | bytes 1048576
  530.5 40.1 %copy-start.5 = (f32[4,8,48,512]{3,2,1,0:T(8,128)S(1)}, f32[4,8,48,512]{3,2,1,0:T(8,128)}, u32[]{:S(2)}) copy-start(f32[4,8,48,512]{3,2,1,0:T(8,128)} %get-tuple-element.357) | copy-start | bytes 9437188
  530.5 65.8 %collective-permute-start.31 = (bf16[768,3072]{1,0:T(8,128)(2,1)}, bf16[768,3072]{1,0:T(8,128)(2,1)}, u32[]{:S(2)}, u32[]{:S(2)}) collective-permute-start(bf16[768,3072]{1,0:T(8,128)(2,1)} %convolution_convert_fusion.1), channel_id=1, source_target_pairs={{0,1},{1,0},{2,3},{3,2},{4,5},{5,4},{6,7},{7,6},{8,9},{9,8},{10,11... | collective-permute-start | bytes 14155784 | tf_op jit(solution)/shard_map/ppermute | solution.py:324
  530.5 39.9 %collective-permute-start.28 = (bf16[4,8,48,512]{3,2,1,0:T(8,128)(2,1)S(1)}, bf16[4,8,48,512]{3,2,1,0:T(8,128)(2,1)S(1)}, u32[]{:S(2)}, u32[]{:S(2)}) collective-permute-start(bf16[4,8,48,512]{3,2,1,0:T(8,128)(2,1)S(1)} %copy-done.11), channel_id=1, source_target_pairs={{4,2},{5,3},{6,0},{7,1},{12,10},{13,11},{14,8},{15,9}} | collective-permute-start | bytes 4718600 | tf_op jit(solution)/shard_map/ppermute | solution.py:324
  532.1 101.0 %collective-permute-start.26 = (bf16[384,3072]{1,0:T(8,128)(2,1)}, bf16[384,3072]{1,0:T(8,128)(2,1)}, u32[]{:S(2)}, u32[]{:S(2)}) collective-permute-start(bf16[384,3072]{1,0:T(8,128)(2,1)} %get-tuple-element.289), channel_id=1, source_target_pairs={{0,2},{1,3},{2,0},{3,1},{4,6},{5,7},{6,4},{7,5},{8,10},{9,11},{10,... | collective-permute-start | bytes 7077896 | tf_op jit(solution)/shard_map/ppermute | solution.py:324
  532.2 107.9 %collective-permute-start.25 = (bf16[384,3072]{1,0:T(8,128)(2,1)}, bf16[384,3072]{1,0:T(8,128)(2,1)}, u32[]{:S(2)}, u32[]{:S(2)}) collective-permute-start(bf16[384,3072]{1,0:T(8,128)(2,1)} %get-tuple-element.293), channel_id=1, source_target_pairs={{0,3},{1,2},{2,1},{3,0},{4,7},{5,6},{6,5},{7,4},{8,11},{9,10},{10,... | collective-permute-start | bytes 7077896 | tf_op jit(solution)/shard_map/ppermute | solution.py:324
  533.8 108.7 %collective-permute-start.24 = (bf16[384,3072]{1,0:T(8,128)(2,1)}, bf16[384,3072]{1,0:T(8,128)(2,1)}, u32[]{:S(2)}, u32[]{:S(2)}) collective-permute-start(bf16[384,3072]{1,0:T(8,128)(2,1)} %get-tuple-element.292), channel_id=1, source_target_pairs={{0,1},{1,0},{2,3},{3,2},{4,5},{5,4},{6,7},{7,6},{8,9},{9,8},{10,11... | collective-permute-start | bytes 7077896 | tf_op jit(solution)/shard_map/ppermute | solution.py:324
  570.5 40.2 %collective-permute-start.30 = (bf16[3072,512]{1,0:T(8,128)(2,1)}, bf16[3072,512]{1,0:T(8,128)(2,1)}, u32[]{:S(2)}, u32[]{:S(2)}) collective-permute-start(bf16[3072,512]{1,0:T(8,128)(2,1)} %convolution_convert_fusion.2), channel_id=1, source_target_pairs={{0,1},{1,0},{2,3},{3,2},{4,5},{5,4},{6,7},{7,6},{8,9},{9,8},{10,11... | collective-permute-start | bytes 9437192 | tf_op jit(solution)/shard_map/ppermute | solution.py:324
  596.4 91.4 %collective-permute-start.34 = (bf16[384,3072]{1,0:T(8,128)(2,1)}, bf16[384,3072]{1,0:T(8,128)(2,1)}, u32[]{:S(2)}, u32[]{:S(2)}) collective-permute-start(bf16[384,3072]{1,0:T(8,128)(2,1)} %grad_in.3), channel_id=1, source_target_pairs={{0,2},{1,3},{2,0},{3,1},{4,6},{5,7},{6,4},{7,5},{8,10},{9,11},{10,... | collective-permute-start | bytes 7077896 | tf_op jit(solution)/shard_map/ppermute | solution.py:324
  596.4 14.2 %slice-start.3 = ((s8[9437184]{0:T(1024)(128)(4,1)}), s8[4194304]{0:T(1024)(128)(4,1)S(1)}, s32[]{:S(2)}) async-start(s8[9437184]{0:T(1024)(128)(4,1)} %bitcast.75), calls=%async_computation.3 | async-start | bytes 8388608
  596.4 14.2 %slice-start.4 = ((s8[9437184]{0:T(1024)(128)(4,1)}), s8[4194304]{0:T(1024)(128)(4,1)S(1)}, s32[]{:S(2)}) async-start(s8[9437184]{0:T(1024)(128)(4,1)} %bitcast.75), calls=%async_computation.4 | async-start | bytes 8388608
  610.6 85.0 %collective-permute-start.36 = (bf16[3072,384]{1,0:T(8,128)(2,1)}, bf16[3072,384]{1,0:T(8,128)(2,1)}, u32[]{:S(2)}, u32[]{:S(2)}) collective-permute-start(bf16[3072,384]{1,0:T(8,128)(2,1)} %add_convert_fusion.1), channel_id=1, source_target_pairs={{0,6},{1,7},{2,4},{3,5},{4,2},{5,3},{6,0},{7,1},{8,14},{9,15},{10,... | collective-permute-start | bytes 7077896 | tf_op jit(solution)/shard_map/ppermute | solution.py:324
  633.1 123.9 %collective-permute-start.33 = (bf16[384,3072]{1,0:T(8,128)(2,1)}, bf16[384,3072]{1,0:T(8,128)(2,1)}, u32[]{:S(2)}, u32[]{:S(2)}) collective-permute-start(bf16[384,3072]{1,0:T(8,128)(2,1)} %grad_in.4), channel_id=1, source_target_pairs={{0,3},{1,2},{2,1},{3,0},{4,7},{5,6},{6,5},{7,4},{8,11},{9,10},{10,... | collective-permute-start | bytes 7077896 | tf_op jit(solution)/shard_map/ppermute | solution.py:324
  640.1 130.9 %collective-permute-start.40 = (bf16[3072,256]{1,0:T(8,128)(2,1)}, bf16[3072,256]{1,0:T(8,128)(2,1)}, u32[]{:S(2)}, u32[]{:S(2)}) collective-permute-start(bf16[3072,256]{1,0:T(8,128)(2,1)} %fusion), channel_id=1, source_target_pairs={{0,6},{1,7},{2,4},{3,5},{4,2},{5,3},{6,0},{7,1},{8,14},{9,15},{10,... | collective-permute-start | bytes 4718600 | tf_op jit(solution)/shard_map/ppermute | solution.py:324
  642.5 107.5 %collective-permute-start.35 = (bf16[384,3072]{1,0:T(8,128)(2,1)}, bf16[384,3072]{1,0:T(8,128)(2,1)S(1)}, u32[]{:S(2)}, u32[]{:S(2)}) collective-permute-start(bf16[384,3072]{1,0:T(8,128)(2,1)} %add_convert_fusion), channel_id=1, source_target_pairs={{0,6},{1,7},{2,4},{3,5},{4,2},{5,3},{6,0},{7,1},{8,14},{9,15},{10,... | collective-permute-start | bytes 7077896 | tf_op jit(solution)/shard_map/ppermute | solution.py:324
  687.7 18.9 %slice-start.6 = ((s8[9437184]{0:T(1024)(128)(4,1)}), s8[1048576]{0:T(1024)(128)(4,1)S(1)}, s32[]{:S(2)}) async-start(s8[9437184]{0:T(1024)(128)(4,1)} %bitcast.77), calls=%async_computation.6 | async-start | bytes 2097152
  695.7 11.0 %slice-start.7 = ((s8[9437184]{0:T(1024)(128)(4,1)}), s8[4194304]{0:T(1024)(128)(4,1)S(1)}, s32[]{:S(2)}) async-start(s8[9437184]{0:T(1024)(128)(4,1)} %bitcast.77), calls=%async_computation.7 | async-start | bytes 8388608
  695.7 11.0 %slice-start.8 = ((s8[9437184]{0:T(1024)(128)(4,1)}), s8[4194304]{0:T(1024)(128)(4,1)S(1)}, s32[]{:S(2)}) async-start(s8[9437184]{0:T(1024)(128)(4,1)} %bitcast.77), calls=%async_computation.8 | async-start | bytes 8388608
  695.7 11.0 %copy-start.3 = (bf16[4,8,48,512]{3,2,1,0:T(8,128)(2,1)S(1)}, bf16[4,8,48,512]{3,2,1,0:T(8,128)(2,1)}, u32[]{:S(2)}) copy-start(bf16[4,8,48,512]{3,2,1,0:T(8,128)(2,1)} %add_convert_fusion.2) | copy-start | bytes 4718596
  706.5 43.5 %slice-start.12 = ((s8[9437184]{0:T(1024)(128)(4,1)}), s8[4194304]{0:T(1024)(128)(4,1)S(1)}, s32[]{:S(2)}) async-start(s8[9437184]{0:T(1024)(128)(4,1)} %bitcast.89), calls=%async_computation.12 | async-start | bytes 8388608
  706.5 43.5 %slice-start.13 = ((s8[9437184]{0:T(1024)(128)(4,1)}), s8[4194304]{0:T(1024)(128)(4,1)S(1)}, s32[]{:S(2)}) async-start(s8[9437184]{0:T(1024)(128)(4,1)} %bitcast.89), calls=%async_computation.13 | async-start | bytes 8388608
  706.5 43.5 %slice-start.14 = ((s8[9437184]{0:T(1024)(128)(4,1)}), s8[1048576]{0:T(1024)(128)(4,1)S(1)}, s32[]{:S(2)}) async-start(s8[9437184]{0:T(1024)(128)(4,1)} %bitcast.89), calls=%async_computation.14 | async-start | bytes 2097152
  706.5 43.4 %copy-start.7 = (bf16[384,3072]{1,0:T(8,128)(2,1)S(1)}, bf16[384,3072]{1,0:T(8,128)(2,1)}, u32[]{:S(2)}) copy-start(bf16[384,3072]{1,0:T(8,128)(2,1)} %get-tuple-element.404) | copy-start | bytes 7077892
  706.6 50.4 %collective-permute-start.32 = (bf16[384,3072]{1,0:T(8,128)(2,1)S(1)}, bf16[384,3072]{1,0:T(8,128)(2,1)}, u32[]{:S(2)}, u32[]{:S(2)}) collective-permute-start(bf16[384,3072]{1,0:T(8,128)(2,1)S(1)} %copy-done.17), channel_id=1, source_target_pairs={{0,1},{1,0},{2,3},{3,2},{4,5},{5,4},{6,7},{7,6},{8,9},{9,8},{10,11... | collective-permute-start | bytes 7077896 | tf_op jit(solution)/shard_map/ppermute | solution.py:324
  757.0 14.1 %copy-start.9 = (f32[3072,256]{1,0:T(8,128)S(1)}, f32[3072,256]{1,0:T(8,128)}, u32[]{:S(2)}) copy-start(f32[3072,256]{1,0:T(8,128)} %convolution_add_fusion) | copy-start | bytes 9437188
  765.8 1.2 collective-permute-start.37
  767.1 3.7 collective-permute-start.38
  770.8 4.9 collective-permute-start.39
  (14 other events, 104.3 us)

commit v3 on v2

--- a/solution.py
+++ b/solution.py
@@ -207,8 +207,8 @@
     half = (pieces, rows, span, 2 * kv_cols)
     return pl.pallas_call(
         functools.partial(attn_bwd_kernel, n_alias), grid=(rows // BWD_ROWS,), in_specs=specs,
-        out_specs=[block_at(BWD_ROWS, pieces, span, q_cols, s), block_at(BWD_ROWS, pieces, span, kv_cols, s % 2), block_at(BWD_ROWS, pieces, span, kv_cols, s % 2)],
-        out_shape=[jax.ShapeDtypeStruct(q.shape, BF16), jax.ShapeDtypeStruct(half, F32), jax.ShapeDtypeStruct(half, BF16)],
+        out_specs=[block_at(BWD_ROWS, pieces, span, q_cols, s), block_at(BWD_ROWS, pieces, span, kv_cols, s % 2), block_at(BWD_ROWS, pieces, span, kv_cols, 0)],
+        out_shape=[jax.ShapeDtypeStruct(q.shape, BF16), jax.ShapeDtypeStruct(half, F32), jax.ShapeDtypeStruct((pieces, rows, span, kv_cols), BF16)],
         input_output_aliases=alias, compiler_params=pltpu.CompilerParams(vmem_limit_bytes=VMEM_LIMIT),
         cost_estimate=cost(20 * rows * toks * toks * q_cols, 20 * rows * toks * q_cols), name="attn_bwd")(*ops)
 
@@ -250,6 +250,48 @@
         out_shape=[jax.ShapeDtypeStruct((rows // 2, width), t) for t in types],
         compiler_params=pltpu.CompilerParams(vmem_limit_bytes=VMEM_LIMIT),
         cost_estimate=cost(2 * rows * width * inner, 4 * rows * width), name="head_out")(heads, w)
+
+
+def head_out_own_kernel(half_ref, h_ref, w_ref, x_ref, far_ref, own_ref, second_ref):
+    out = dot(h_ref[...], w_ref[...], NN)
+    rows = second_ref.shape[0]
+    total = (out[:rows] + far_ref[...].astype(F32)).astype(BF16)
+    own_ref[...] = (x_ref[...].astype(F32) + total.astype(F32)).astype(BF16)
+    second_ref[...] = out[rows:].astype(BF16)
+
+
+def head_out_own(half, heads, w, hid, far):
+    rows, inner, width, tile = heads.shape[0] // 2, heads.shape[1], w.shape[1], 4 * HEAD_DIM
+    part = rows // 2
+    own = pl.BlockSpec((part, tile), lambda n, h: (h[0], n))
+    plain = pl.BlockSpec((part, tile), lambda n, h: (0, n))
+    return pl.pallas_call(
+        head_out_own_kernel,
+        grid_spec=pltpu.PrefetchScalarGridSpec(
+            num_scalar_prefetch=1, grid=(width // tile,),
+            in_specs=[pl.BlockSpec((rows, inner), lambda n, h: (0, 0)), pl.BlockSpec((inner, tile), lambda n, h: (0, n)), own, plain],
+            out_specs=[own, plain]),
+        out_shape=[jax.ShapeDtypeStruct(hid.shape, BF16), jax.ShapeDtypeStruct((part, width), BF16)],
+        compiler_params=pltpu.CompilerParams(vmem_limit_bytes=VMEM_LIMIT),
+        cost_estimate=cost(2 * rows * width * inner, 4 * rows * width), name="head_out")(half, heads, w, hid, far)
+
+
+def grad_out_kernel(h_ref, g_ref, mate_ref, own_ref, far_ref):
+    out = dot(h_ref[...], g_ref[...], TN) + mate_ref[...].astype(F32)
+    rows = own_ref.shape[0]
+    own_ref[...] = out[:rows]
+    far_ref[...] = out[rows:].astype(BF16)
+
+
+def grad_out_rest(heads, grads, mate):
+    toks, width, cols, tile = heads.shape[0], grads.shape[1], heads.shape[1] // 2, 8 * HEAD_DIM
+    col = lambda rows: pl.BlockSpec((rows, tile), lambda n: (0, n))
+    return pl.pallas_call(
+        grad_out_kernel, grid=(width // tile,),
+        in_specs=[pl.BlockSpec((toks, cols), lambda n: (0, 1)), col(toks), col(cols)], out_specs=[col(cols // 2), col(cols // 2)],
+        out_shape=[jax.ShapeDtypeStruct((cols // 2, width), F32), jax.ShapeDtypeStruct((cols // 2, width), BF16)],
+        compiler_params=pltpu.CompilerParams(vmem_limit_bytes=VMEM_LIMIT),
+        cost_estimate=cost(2 * toks * cols * width, 4 * toks * width), name="grad_out")(heads, grads, mate)
 
 
 def residual_kernel(x_ref, a_ref, b_ref, *refs):
@@ -436,69 +478,66 @@
                 heads = run(lambda q, kv, kr: attn_forward(g, q, kv, kr, qinfo, kinfo, None), q_all, local, far_in)
             else:
                 if SLOT[g] == 2:
+                    dos.append(run(head_grad, flat(grd3), wo_all))
                     grads = put(flat(grd3), grads, 3, 0)
                 heads = run(lambda q, kv, kr, h: attn_forward(g, q, kv, kr, qinfo, kinfo, h), q_all, local, far_in, heads)
         heads_flat = flat(heads)
         att = [None] * 4
         out2, out3 = run(lambda h, w: head_out(h, w, 1, (BF16, BF16)), heads_flat, wo_all)
         att[2], att[3] = send(out2, mates[2]), send(out3, mates[3])
-        own_out, out1 = run(lambda h, w: head_out(h, w, 0, (F32, BF16)), heads_flat, wo_all)
-        att[1] = send(out1, mates[1])
-
-        dos.append(run(head_grad, flat(grd3), wo_all))
-        dq, dkv, dkr, dkv_in = None, [None, None], [None, None], [None, None]
+
+        dq, dkv, dkv_in = None, [None, None], [None] * 4
         for g in GROUPS:
             i = SLOT[g] // 2
-            bufs = [b for b in (dq, dkv[i], dkr[i]) if b is not None]
-            given = tuple(b is not None for b in (dq, dkv[i], dkr[i]))
+            bufs = [b for b in (dq, dkv[i]) if b is not None]
+            given = tuple(b is not None for b in (dq, dkv[i]))
 
             def fn(q, kv, kr, d0, d1, d2, d3, *rest):
                 it = iter(rest)
                 return attn_backward(g, q, kv, kr, (d0, d1, d2, d3), qinfo, kinfo, tabs, [next(it) if ok else None for ok in given])
 
-            dq, dkv[i], dkr[i] = run(fn, q_all, kvs[i], kv_in[SLOT[g ^ 2] // 2], *dos, *bufs)
-            if SLOT[g] % 2 == 1:
-                dkv_in[i] = send(dkr[i], earlier)
-
-        def add_far(mine, theirs):
-            swapped = jnp.concatenate([theirs[..., 2 * HEAD_DIM:], theirs[..., :2 * HEAD_DIM]], axis=-1)
-            return flat((mine + swapped.astype(F32)).astype(BF16))
+            dq, dkv[i], dkr = run(fn, q_all, kvs[i], kv_in[SLOT[g ^ 2] // 2], *dos, *bufs)
+            dkv_in[g ^ 2] = send(dkr, earlier)
+
+        def add_far(mine, *theirs):
+            return flat((mine + jnp.concatenate(theirs, axis=-1).astype(F32)).astype(BF16))
 
         cut = lambda x, s, n: x[:, s * q_cols:(s + n) * q_cols]
         low = lambda x: x.astype(BF16)
         kv_half = 2 * HEAD_DIM
+        mine_half, other_half = core.astype(jnp.int32)[None], (1 - core).astype(jnp.int32)[None]
+        flat_shape = (all_rows * span, width)
+        hid_flat, g_flat = flat(hidden), flat(grad_out)
         dq_flat = flat(dq)
         spq13 = send(run(lambda d, n: low(dot(n, cut(d, 0, 2), TN)), dq_flat, normed), mates[1])
-        dkv_a = run(add_far, dkv[0], dkv_in[0])
+        dkv_a = run(add_far, dkv[0], *[dkv_in[g] for g in GROUPS[:2]])
         spk13 = send(run(lambda d, n: low(dot(n, d, TN)), dkv_a, normed), mates[1])
         spq2 = send(run(lambda d, n, e: low(dot(n, cut(d, 3, 1), TN) + e[:, q_cols:].astype(F32)), dq_flat, normed, spq13), pair)
-        so13 = send(run(lambda h, g: low(dot(cut(h, 0, 2), g, TN)), heads_flat, grads), mates[1])
-        dkv_b = run(add_far, dkv[1], dkv_in[1])
+        dkv_b = run(add_far, dkv[1], *[dkv_in[g] for g in GROUPS[2:]])
         gn = [None] * 4
         for p in (2, 3):
             gn[p] = send(run(lambda *x: grad_in(*x, p, (BF16,))[0], dq_flat, dkv_a, dkv_b, wq_all, wkv_all), mates[p])
         gn2, gn3 = gn[2], gn[3]
-        so1, so3 = run(lambda e: (e[:q_cols], e[q_cols:]), so13)
-        so2 = send(run(lambda h, gg, e: low(dot(cut(h, 3, 1), gg, TN) + e.astype(F32)), heads_flat, grads, so3), pair)
         spk2 = send(run(lambda d, n, e: low(dot(n, d[:, kv_half:], TN) + e[:, kv_half:].astype(F32)), dkv_b, normed, spk13), pair)
-        mine_half, other_half = core.astype(jnp.int32)[None], (1 - core).astype(jnp.int32)[None]
-        flat_shape = (all_rows * span, width)
-        hid_flat, g_flat = flat(hidden), flat(grad_out)
+        so13 = send(run(lambda h, g: low(dot(cut(h, 0, 2), g, TN)), heads_flat, grads), mates[1])
+        attn_out, out1 = run(lambda h, w, x, f: head_out_own(mine_half, h, w, x, f), heads_flat, wo_all, hid_flat, flat(att[2]))
+        att[1] = send(out1, mates[1])
+        own_wo, so2 = run(grad_out_rest, heads_flat, grads, so13)
+        so2 = send(so2, pair)
         own_in, gn1 = run(lambda d, a, b, wq, wk: grad_in(d, a, b, wq, wk, 0, (F32, BF16)), dq_flat, dkv_a, dkv_b, wq_all, wkv_all)
         gn1 = send(gn1, mates[1])
-        attn_out = run(lambda x, a, b: half_rows_call(residual_kernel, mine_half, (x, a, b), None, None, flat_shape, False)[0], hid_flat, own_out, flat(att[2]))
         attn_out = run(lambda x, a, b, o: half_rows_call(residual_kernel, other_half, (x, a, b), None, o, flat_shape, False)[0], hid_flat, flat(att[1]), flat(att[3]), attn_out)
         back_call = lambda h, arrays, buf: half_rows_call(norm_back_kernel, h, arrays, gain_row, buf, flat_shape, True)
         grad_hidden, part_a = run(lambda x, g, a, b: back_call(mine_half, (x, g, a, b), None), hid_flat, g_flat, own_in, gn2)
         dwq = run(lambda d, n, e, f: dot(n, cut(d, 2, 1), TN) + (e[:, :q_cols].astype(F32) + f.astype(F32)), dq_flat, normed, spq13, spq2)
         own_kv = after(run(lambda d, n, e: dot(n, d[:, :kv_half], TN) + e[:, :kv_half].astype(F32), dkv_b, normed, spk13))
-        dwo = run(lambda h, g, a, b: dot(cut(h, 2, 1), g, TN) + (a.astype(F32) + b.astype(F32)), heads_flat, grads, so1, so2)
+        add_cols = lambda cols: (lambda a, b: a[:, cols] + b[:, cols].astype(F32))
+        dwk, dwv = run(lambda a, b: (add_cols(slice(0, HEAD_DIM))(a, b), add_cols(slice(HEAD_DIM, kv_half))(a, b)), own_kv, spk2)
         grad_hidden, part_b = run(lambda x, g, a, b, o: back_call(other_half, (x, g, a, b), o), hid_flat, g_flat, gn1, gn3, grad_hidden)
         gain_sum = jnp.sum(part_a + part_b, axis=0).reshape(-1, HEAD_DIM)
         for perm in (mates[1], mates[2], pair):
             gain_sum = gain_sum + send(gain_sum, perm)
-        dwk = own_kv[:, :HEAD_DIM] + spk2[:, :HEAD_DIM].astype(F32)
-        dwv = own_kv[:, HEAD_DIM:] + spk2[:, HEAD_DIM:].astype(F32)
+        dwo = run(lambda a, b: a + b.astype(F32), own_wo, so2)
         return attn_out.reshape(hidden.shape), grad_hidden.reshape(hidden.shape), gain_sum.reshape(-1), dwq, dwk, dwv, dwo
 
     row_spec = P('dp', 'tp', None)

time: 788 us -> 807 us (1.024)
  waiting for transfers between devices: 320 us -> 342 us
  matrix products: 107 us -> 95.7 us
    pallas_call x0 -> x2, Pallas kernels: none -> 25.8 us  [the longest x1 12.9 us: grad_out_rest(): pl.pallas_call(grad_out_kernel, grid=(width // tile,), in_specs=[pl.Block...]
    ppermute x41 -> x43, waiting for transfers between devices: 320 us -> 342 us  [send(): return lax.ppermute(x, 'tp', perm)]
    pallas_call x2 -> x1, Pallas kernels: 24.1 us -> 11.8 us  [head_out(): pl.pallas_call(head_out_kernel, grid=(width // tile,), in_specs=[pl.Block...]
    dot_general x13 -> x11, matrix products: 107 us -> 95.7 us  [dot(): return lax.dot_general(a, b, dims, preferred_element_type=F32)]
    pallas_call x4 -> x3, Pallas kernels: 25.6 us -> 20.2 us  [half_rows_call(): pl.pallas_call(body, grid_spec=pltpu.PrefetchScalarGridSpec(num_scalar_pr...]
    ppermute x41 -> x43, starting transfers between devices: 37.2 us -> 38 us  [send(): return lax.ppermute(x, 'tp', perm)]
  transfers between devices with their start and end apart: 41 -> 43, of which waited for: 14 -> 18; matrix products, arithmetic and copies ran while one was open for 13% -> 12% of each run, Pallas kernels for 24% -> 26%
where the time goes in v3:
time: 807 us; the launch traced here: 797 us
  waiting for transfers between devices  342 us (42%)
  Pallas kernels  281 us (35%)
  matrix products  95.7 us (12%)
  starting transfers between devices  38 us (5%)
  other arithmetic  23.5 us (3%)
  local copies, waits for them, and re-layouts  15.8 us (2%)
    ppermute x43, waiting for transfers between devices, send(): return lax.ppermute(x, 'tp', perm)  342 us
    dot_general x11, matrix products, dot(): return lax.dot_general(a, b, dims, preferred_element_type=F32)  95.7 us
    pallas_call x20, Pallas kernels, place(): pl.pallas_call(functools.partial(place_kernel, normalize), grid=(steps,),...  58.2 us
    pallas_call x5, Pallas kernels, project(): pl.pallas_call(functools.partial(proj_kernel, turned, chunk), grid=(count...  50.8 us
    pallas_call x4, Pallas kernels, attn_backward(): pl.pallas_call(functools.partial(attn_bwd_kernel, n_alias), grid=(rows //...  47.8 us
    pallas_call x3, Pallas kernels, grad_in(): pl.pallas_call(grad_in_kernel, grid=(width // tile,), in_specs=[part(dq),...  41.5 us
    ppermute x43, starting transfers between devices, send(): return lax.ppermute(x, 'tp', perm)  38 us
    pallas_call x4, Pallas kernels, attn_forward(): pl.pallas_call(attn_fwd_kernel, grid=(rows // FWD_ROWS,), in_specs=specs,...  24.4 us
  transfers between devices with their start and end apart: 43, of which 18 were waited for; matrix products, arithmetic and copies ran while one was open for 12% of the time, Pallas kernels for 26%

profile of v3, /device:TPU:112, one launch (start us, length us, event | category | flops | bytes accessed | tf_op | source)
XLA Modules:
  0.0 796.6 jit_solution(10281003420190582595)
XLA Ops:
  4.8 4.4 constant_dynamic-slice_fusion.4
  13.0 3.9 collective-permute-start.3
  17.5 2.9 place.20.refs_0_
  22.8 2.8 place.22.refs_0_
  25.8 3.6 place.23.refs_0_
  32.1 3.6 place.25.refs_0_
  38.2 2.9 place.27.refs_0_
  41.1 2.8 place.28.refs_0_
  43.9 2.8 place.29.refs_0_
  46.8 5.4 collective-permute-done.3.x_ref
  57.1 21.8 %collective-permute-done.15 = s32[8,48]{1,0:T(8,128)S(1)} collective-permute-done((s32[8,48]{1,0:T(8,128)S(1)}, s32[8,48]{1,0:T(8,128)S(1)}, u32[]{:S(2)}, u32[]{:S(2)}) %collective-permute-start.15) | collective-permute-done | bytes 1568 | tf_op jit(solution)/shard_map/ppermute | solution.py:366
  92.2 3.7 place.32.x_ref.refs_0_
  97.2 4.4 fusion.6
  101.6 4.3 fusion.5
  105.9 8.9 %project.5.refs_0_ = bf16[1536,512]{1,0:T(8,128)(2,1)} custom-call(bf16[1536,3072]{1,0:T(8,128)(2,1)} %place.32.x_ref.refs_0_, bf16[3072,1024]{1,0:T(8,128)(2,1)} %place.31.w_ref.wkv_ref, f32[1536,128]{1,0:T(8,128)} %get-tuple-element.234.cos_ref, f32[1536,128]{1,0:T(8,128)} %get-tuple-element.237.sin_ref), custom_call_target="tpu_custom_call" | custom-call | flops 3623878656 | bytes 7077888 | tf_op jit(solution)/shard_map/project/pallas_call | solution.py:87
  114.8 9.0 %project.6.refs_0_ = bf16[1536,512]{1,0:T(8,128)(2,1)} custom-call(bf16[1536,3072]{1,0:T(8,128)(2,1)} %place.32.x_ref.refs_0_, bf16[3072,1024]{1,0:T(8,128)(2,1)} %place.31.w_ref.wkv_ref, f32[1536,128]{1,0:T(8,128)} %get-tuple-element.234.cos_ref, f32[1536,128]{1,0:T(8,128)} %get-tuple-element.237.sin_ref), custom_call_target="tpu_custom_call" | custom-call | flops 3623878656 | bytes 7077888 | tf_op jit(solution)/shard_map/project/pallas_call | solution.py:87
  123.8 12.8 %collective-permute-done.9.x_ref = bf16[3072,384]{1,0:T(8,128)(2,1)} collective-permute-done((bf16[3072,384]{1,0:T(8,128)(2,1)}, bf16[3072,384]{1,0:T(8,128)(2,1)}, u32[]{:S(2)}, u32[]{:S(2)}) %collective-permute-start.9) | collective-permute-done | bytes 2359328 | tf_op jit(solution)/shard_map/ppermute | solution.py:366
  137.8 3.0 place.33.refs_0_
  141.5 2.8 place.34.w_ref.wq_ref
  144.3 45.4 %collective-permute-done = bf16[8,48,3072]{2,1,0:T(8,128)(2,1)S(1)} collective-permute-done((bf16[8,48,3072]{2,1,0:T(8,128)(2,1)}, bf16[8,48,3072]{2,1,0:T(8,128)(2,1)S(1)}, u32[]{:S(2)}, u32[]{:S(2)}) %collective-permute-start) | collective-permute-done | bytes 2359328 | tf_op jit(solution)/shard_map/ppermute | solution.py:366
  191.1 3.6 place.35.x_ref
  194.7 4.6 project.7
  199.3 4.7 project.8
  204.0 23.6 %project.9 = bf16[1536,1536]{1,0:T(8,128)(2,1)} custom-call(bf16[1536,3072]{1,0:T(8,128)(2,1)} %place.35.x_ref, bf16[3072,1536]{1,0:T(8,128)(2,1)} %place.34.w_ref.wq_ref, f32[1536,128]{1,0:T(8,128)} %get-tuple-element.234.cos_ref, f32[1536,128]{1,0:T(8,128)} %get-tuple-element.237.sin_ref), custom_call_target="tpu_custom_call" | custom-call | flops 14495514624 | bytes 9437184 | tf_op jit(solution)/shard_map/project/pallas_call | solution.py:87
  230.3 4.2 collective-permute-start.18
  242.4 9.4 %convolution_convert_fusion.6 = bf16[384,1536]{1,0:T(8,128)(2,1)} fusion(bf16[384,3072]{1,0:T(8,128)(2,1)} %bitcast.155, bf16[1536,3072]{1,0:T(8,128)(2,1)} %place.37.w_ref), kind=kOutput, calls=%fused_computation.14 | convolution fusion | flops 3624468480 | bytes 12976128 | tf_op jit(solution)/shard_map/dot_general | solution.py:28
  251.9 6.7 convolution_convert_fusion.5
  258.6 74.3 %collective-permute-done.20 = bf16[8,48,3072]{2,1,0:T(8,128)(2,1)} collective-permute-done((bf16[8,48,3072]{2,1,0:T(8,128)(2,1)}, bf16[8,48,3072]{2,1,0:T(8,128)(2,1)}, u32[]{:S(2)}, u32[]{:S(2)}) %collective-permute-start.20) | collective-permute-done | bytes 2359328 | tf_op jit(solution)/shard_map/ppermute | solution.py:366
  333.0 6.7 convolution_convert_fusion.4
  342.5 6.0 attn_fwd.4.refs_0_
  348.5 6.4 attn_fwd.5.refs_0_
  354.9 9.3 %convolution_convert_fusion.3 = bf16[384,1536]{1,0:T(8,128)(2,1)} fusion(bf16[384,3072]{1,0:T(8,128)(2,1)} %bitcast.36.x_ref, bf16[1536,3072]{1,0:T(8,128)(2,1)} %place.37.w_ref), kind=kOutput, calls=%fused_computation.11 | convolution fusion | flops 3624468480 | bytes 12976128 | tf_op jit(solution)/shard_map/dot_general | solution.py:28
  366.9 6.0 attn_fwd.6.refs_0_
  372.9 6.0 attn_fwd.7
  378.9 11.8 %head_out.2 = (bf16[384,3072]{1,0:T(8,128)(2,1)}, bf16[384,3072]{1,0:T(8,128)(2,1)}) custom-call(bf16[1536,1536]{1,0:T(8,128)(2,1)} %bitcast.93, bf16[1536,3072]{1,0:T(8,128)(2,1)} %place.37.w_ref), custom_call_target="tpu_custom_call" | custom-call | flops 7247757312 | bytes 9437184 | tf_op jit(solution)/shard_map/head_out/pallas_call | solution.py:247
  390.7 12.0 %attn_bwd.4 = (bf16[4,8,48,1536]{3,2,1,0:T(8,128)(2,1)}, f32[4,8,48,512]{3,2,1,0:T(8,128)}, bf16[4,8,48,256]{3,2,1,0:T(8,128)(2,1)}) custom-call(bf16[4,8,48,1536]{3,2,1,0:T(8,128)(2,1)} %bitcast.79, bf16[4,8,48,512]{3,2,1,0:T(8,128)(2,1)} %bitcast.117, bf16[4,8,48,512]{3,2,1,0:T(8,128)(2,1)} %collective-permute-done.19.kr_ref, ...), custom_call_target="tpu_custom_call" | custom-call | flops 2264924160 | bytes 11796480 | tf_op jit(solution)/shard_map/attn_bwd/pallas_call | solution.py:208
  402.8 11.9 %attn_bwd.5 = (bf16[4,8,48,1536]{3,2,1,0:T(8,128)(2,1)}, f32[4,8,48,512]{3,2,1,0:T(8,128)}, bf16[4,8,48,256]{3,2,1,0:T(8,128)(2,1)}) custom-call(bf16[4,8,48,1536]{3,2,1,0:T(8,128)(2,1)} %bitcast.80, bf16[4,8,48,512]{3,2,1,0:T(8,128)(2,1)} %bitcast.118, ...), custom_call_target="tpu_custom_call", output_to_operand_aliasing={{0}: (13, {}), {1}: (14, {})} | custom-call | flops 2264924160 | bytes 11796480 | tf_op jit(solution)/shard_map/attn_bwd/pallas_call | solution.py:208
  414.7 11.9 %attn_bwd.6 = (bf16[4,8,48,1536]{3,2,1,0:T(8,128)(2,1)}, f32[4,8,48,512]{3,2,1,0:T(8,128)}, bf16[4,8,48,256]{3,2,1,0:T(8,128)(2,1)}) custom-call(bf16[4,8,48,1536]{3,2,1,0:T(8,128)(2,1)} %bitcast.81, bf16[4,8,48,512]{3,2,1,0:T(8,128)(2,1)} %bitcast.123, bf16[4,8,48,512]{3,2,1,0:T(8,128)(2,1)} %collective-permute-done.18.kr_ref, ...), custom_call_target="tpu_custom_call", output_to_operand_aliasing={{0}: (13, {})} | custom-call | flops 2264924160 | bytes 11796480 | tf_op jit(solution)/shard_map/attn_bwd/pallas_call | solution.py:208
  426.6 11.9 %attn_bwd.7 = (bf16[4,8,48,1536]{3,2,1,0:T(8,128)(2,1)}, f32[4,8,48,512]{3,2,1,0:T(8,128)}, bf16[4,8,48,256]{3,2,1,0:T(8,128)(2,1)}) custom-call(bf16[4,8,48,1536]{3,2,1,0:T(8,128)(2,1)} %bitcast.82, bf16[4,8,48,512]{3,2,1,0:T(8,128)(2,1)} %bitcast.124, ...), custom_call_target="tpu_custom_call", output_to_operand_aliasing={{0}: (13, {}), {1}: (14, {})} | custom-call | flops 2264924160 | bytes 11796480 | tf_op jit(solution)/shard_map/attn_bwd/pallas_call | solution.py:208
  438.6 11.1 %convolution_convert_fusion = bf16[3072,768]{1,0:T(8,128)(2,1)S(1)} fusion(bf16[1536,3072]{1,0:T(8,128)(2,1)} %place.35.x_ref, bf16[1536,1536]{1,0:T(8,128)(2,1)} %bitcast.83), kind=kOutput, calls=%fused_computation | convolution fusion | flops 7250116608 | bytes 16515072 | tf_op jit(solution)/shard_map/dot_general | solution.py:28
  455.1 18.3 %collective-permute-done.28 = bf16[4,8,48,256]{3,2,1,0:T(8,128)(2,1)S(1)} collective-permute-done((bf16[4,8,48,256]{3,2,1,0:T(8,128)(2,1)S(1)}, bf16[4,8,48,256]{3,2,1,0:T(8,128)(2,1)S(1)}, u32[]{:S(2)}, u32[]{:S(2)}) %collective-permute-start.28) | collective-permute-done | bytes 786464 | tf_op jit(solution)/shard_map/ppermute | solution.py:366
  473.3 16.9 %collective-permute-done.29 = bf16[4,8,48,256]{3,2,1,0:T(8,128)(2,1)S(1)} collective-permute-done((bf16[4,8,48,256]{3,2,1,0:T(8,128)(2,1)S(1)}, bf16[4,8,48,256]{3,2,1,0:T(8,128)(2,1)S(1)}, u32[]{:S(2)}, u32[]{:S(2)}) %collective-permute-start.29) | collective-permute-done | bytes 786464 | tf_op jit(solution)/shard_map/ppermute | solution.py:366
  490.8 6.9 convolution_convert_fusion.2
  497.8 8.9 %add_convert_fusion = bf16[3072,384]{1,0:T(8,128)(2,1)} fusion(bf16[1536,3072]{1,0:T(8,128)(2,1)S(1)} %bitcast.72, bf16[3072,768]{1,0:T(8,128)(2,1)S(1)} %collective-permute-done.27, bf16[1536,1536]{1,0:T(8,128)(2,1)} %bitcast.84), kind=kOutput, calls=%fused_computation.4 | convolution fusion | flops 3627417600 | bytes 15335424 | tf_op jit(solution)/shard_map/dot_general | solution.py:28
  507.0 16.3 %collective-permute-done.26 = bf16[4,8,48,256]{3,2,1,0:T(8,128)(2,1)S(1)} collective-permute-done((bf16[4,8,48,256]{3,2,1,0:T(8,128)(2,1)S(1)}, bf16[4,8,48,256]{3,2,1,0:T(8,128)(2,1)S(1)}, u32[]{:S(2)}, u32[]{:S(2)}) %collective-permute-start.26) | collective-permute-done | bytes 786464 | tf_op jit(solution)/shard_map/ppermute | solution.py:366
  525.1 11.9 %grad_in.3 = bf16[384,3072]{1,0:T(8,128)(2,1)} custom-call(bf16[1536,1536]{1,0:T(8,128)(2,1)} %bitcast.85, bf16[1536,512]{1,0:T(8,128)(2,1)} %bitcast.151, bf16[1536,512]{1,0:T(8,128)(2,1)} %bitcast.145, bf16[3072,1536]{1,0:T(8,128)(2,1)} %place.34.w_ref.wq_ref, bf16[3072,1024]{1,0:T(8,128)(2,1)} %place.31.w_ref.wkv_ref), custom_call_target="tpu_custom_call" | custom-call | flops 6039797760 | bytes 4718592 | tf_op jit(solution)/shard_map/grad_in/pallas_call | solution.py:229
  537.1 12.1 %grad_in.4 = bf16[384,3072]{1,0:T(8,128)(2,1)} custom-call(bf16[1536,1536]{1,0:T(8,128)(2,1)} %bitcast.86, bf16[1536,512]{1,0:T(8,128)(2,1)} %bitcast.152, bf16[1536,512]{1,0:T(8,128)(2,1)} %bitcast.146, bf16[3072,1536]{1,0:T(8,128)(2,1)} %place.34.w_ref.wq_ref, bf16[3072,1024]{1,0:T(8,128)(2,1)} %place.31.w_ref.wkv_ref), custom_call_target="tpu_custom_call" | custom-call | flops 6039797760 | bytes 4718592 | tf_op jit(solution)/shard_map/grad_in/pallas_call | solution.py:229
  549.2 8.3 %fusion = bf16[3072,256]{1,0:T(8,128)(2,1)} fusion(bf16[1536,3072]{1,0:T(8,128)(2,1)} %place.35.x_ref, bf16[3072,512]{1,0:T(8,128)(2,1)} %collective-permute-done.30, bf16[1536,512]{1,0:T(8,128)(2,1)S(1)} %bitcast.148), kind=kOutput, calls=%fused_computation.8 | convolution fusion | flops 2418278400 | bytes 13369344 | tf_op jit(solution)/shard_map/dot_general | solution.py:28
  557.5 13.2 %convolution_convert_fusion.1 = bf16[768,3072]{1,0:T(8,128)(2,1)} fusion(bf16[1536,3072]{1,0:T(8,128)(2,1)} %place.39.g_ref, bf16[1536,1536]{1,0:T(8,128)(2,1)S(1)} %bitcast.98), kind=kOutput, calls=%fused_computation.1 | convolution fusion | flops 7250116608 | bytes 16515072 | tf_op jit(solution)/shard_map/dot_general | solution.py:28
  572.5 52.3 %collective-permute-done.24.far_ref = bf16[384,3072]{1,0:T(8,128)(2,1)S(1)} collective-permute-done((bf16[384,3072]{1,0:T(8,128)(2,1)S(1)}, bf16[384,3072]{1,0:T(8,128)(2,1)S(1)}, u32[]{:S(2)}, u32[]{:S(2)}) %collective-permute-start.24) | collective-permute-done | bytes 2359328 | tf_op jit(solution)/shard_map/ppermute | solution.py:366
  626.2 12.9 %head_out.3 = (bf16[768,3072]{1,0:T(8,128)(2,1)}, bf16[384,3072]{1,0:T(8,128)(2,1)}) custom-call(s32[1]{0:T(128)} %bitcast.2.half_ref.h_ref, bf16[1536,1536]{1,0:T(8,128)(2,1)} %bitcast.94, bf16[1536,3072]{1,0:T(8,128)(2,1)} %place.37.w_ref, bf16[768,3072]{1,0:T(8,128)(2,1)} %bitcast.89, bf16[384,3072]{1,0:T(8,128)(2,1)} %copy-done.15), custom_call_target="tpu_custom_call" | custom-call | flops 7247757312 | bytes 9437184 | tf_op jit(solution)/shard_map/head_out/pallas_call | solution.py:268
  639.2 3.2 collective-permute-start.38
  642.4 12.9 %grad_out.1 = (f32[384,3072]{1,0:T(8,128)}, bf16[384,3072]{1,0:T(8,128)(2,1)}) custom-call(bf16[1536,1536]{1,0:T(8,128)(2,1)} %bitcast.95, bf16[1536,3072]{1,0:T(8,128)(2,1)} %place.39.g_ref, bf16[768,3072]{1,0:T(8,128)(2,1)} %collective-permute-done.33.mate_ref), custom_call_target="tpu_custom_call" | custom-call | flops 7247757312 | bytes 18874368 | tf_op jit(solution)/shard_map/grad_out/pallas_call | solution.py:289
  655.3 17.5 %grad_in.5 = (f32[384,3072]{1,0:T(8,128)}, bf16[384,3072]{1,0:T(8,128)(2,1)}) custom-call(bf16[1536,1536]{1,0:T(8,128)(2,1)} %bitcast.87, bf16[1536,512]{1,0:T(8,128)(2,1)} %bitcast.153, bf16[1536,512]{1,0:T(8,128)(2,1)} %bitcast.147, bf16[3072,1536]{1,0:T(8,128)(2,1)} %place.34.w_ref.wq_ref, bf16[3072,1024]{1,0:T(8,128)(2,1)} %place.31.w_ref.wkv_ref), custom_call_target="tpu_custom_call" | custom-call | flops 12079595520 | bytes 9437184 | tf_op jit(solution)/shard_map/grad_in/pallas_call | solution.py:229
  675.2 4.6 shard_map.135
  679.7 46.2 %collective-permute-done.36.refs_3_ = bf16[384,3072]{1,0:T(8,128)(2,1)} collective-permute-done((bf16[384,3072]{1,0:T(8,128)(2,1)}, bf16[384,3072]{1,0:T(8,128)(2,1)}, u32[]{:S(2)}, u32[]{:S(2)}) %collective-permute-start.36) | collective-permute-done | bytes 2359328 | tf_op jit(solution)/shard_map/ppermute | solution.py:366
  726.0 7.9 shard_map.136
  734.1 10.8 %add_add_fusion = f32[3072,384]{1,0:T(8,128)} fusion(bf16[3072,384]{1,0:T(8,128)(2,1)} %collective-permute-done.37, bf16[1536,3072]{1,0:T(8,128)(2,1)} %place.35.x_ref, bf16[3072,768]{1,0:T(8,128)(2,1)} %copy-done.13, bf16[1536,1536]{1,0:T(8,128)(2,1)} %bitcast.88), kind=kOutput, calls=%fused_computation.3 | convolution fusion | flops 3628597248 | bytes 20054016 | tf_op jit(solution)/shard_map/dot_general | solution.py:28
  744.9 4.4 convolution_add_fusion
  749.3 3.3 convert_add_fusion.1
  752.6 23.0 %collective-permute-done.35.refs_3_ = bf16[384,3072]{1,0:T(8,128)(2,1)} collective-permute-done((bf16[384,3072]{1,0:T(8,128)(2,1)S(1)}, bf16[384,3072]{1,0:T(8,128)(2,1)}, u32[]{:S(2)}, u32[]{:S(2)}) %collective-permute-start.35) | collective-permute-done | bytes 2359328 | tf_op jit(solution)/shard_map/ppermute | solution.py:366
  775.6 7.8 shard_map.137
  786.1 3.0 collective-permute-done.42
  789.6 6.2 convert_add_fusion
  (173 shorter events, 73.1 us)
Async XLA Ops:
  4.8 8.2 %collective-permute-start.7 = (bf16[3072,256]{1,0:T(8,128)(2,1)}, bf16[3072,256]{1,0:T(8,128)(2,1)}, u32[]{:S(2)}, u32[]{:S(2)}) collective-permute-start(bf16[3072,256]{1,0:T(8,128)(2,1)} %constant_dynamic-update-slice_fusion.x_ref), channel_id=1, source_target_pairs={{0,1},{1,0},{2,3},{3,2},{4,5},{5,4},{6,7},{7,6},{8,9},{9,8},{10,11... | collective-permute-start | bytes 4718600 | tf_op jit(solution)/shard_map/ppermute | solution.py:366
  9.2 16.5 %copy-start.7 = (bf16[8,48,3072]{2,1,0:T(8,128)(2,1)}, bf16[8,48,3072]{2,1,0:T(8,128)(2,1)S(1)}, u32[]{:S(2)}) copy-start(bf16[8,48,3072]{2,1,0:T(8,128)(2,1)S(1)} %get-tuple-element.419) | copy-start | bytes 7077892
  9.2 16.5 %collective-permute-start.2 = (bf16[8,48,3072]{2,1,0:T(8,128)(2,1)}, bf16[8,48,3072]{2,1,0:T(8,128)(2,1)}, u32[]{:S(2)}, u32[]{:S(2)}) collective-permute-start(bf16[8,48,3072]{2,1,0:T(8,128)(2,1)} %get-tuple-element.420), channel_id=1, source_target_pairs={{0,1},{1,0},{2,3},{3,2},{4,5},{5,4},{6,7},{7,6},{8,9},{9,8},{10,11... | collective-permute-start | bytes 7077896 | tf_op jit(solution)/shard_map/ppermute | solution.py:366
  9.7 28.5 %collective-permute-start.6 = (bf16[3072,384]{1,0:T(8,128)(2,1)}, bf16[3072,384]{1,0:T(8,128)(2,1)}, u32[]{:S(2)}, u32[]{:S(2)}) collective-permute-start(bf16[3072,384]{1,0:T(8,128)(2,1)} %x_ref.1), channel_id=1, source_target_pairs={{0,1},{1,0},{2,3},{3,2},{4,5},{5,4},{6,7},{7,6},{8,9},{9,8},{10,11... | collective-permute-start | bytes 7077896 | tf_op jit(solution)/shard_map/ppermute | solution.py:366
  9.7 31.4 %collective-permute-start.5 = (bf16[384,3072]{1,0:T(8,128)(2,1)}, bf16[384,3072]{1,0:T(8,128)(2,1)}, u32[]{:S(2)}, u32[]{:S(2)}) collective-permute-start(bf16[384,3072]{1,0:T(8,128)(2,1)} %x_ref.2), channel_id=1, source_target_pairs={{0,1},{1,0},{2,3},{3,2},{4,5},{5,4},{6,7},{7,6},{8,9},{9,8},{10,11... | collective-permute-start | bytes 7077896 | tf_op jit(solution)/shard_map/ppermute | solution.py:366
  12.9 31.1 %collective-permute-start.4 = (bf16[8,48,3072]{2,1,0:T(8,128)(2,1)}, bf16[8,48,3072]{2,1,0:T(8,128)(2,1)}, u32[]{:S(2)}, u32[]{:S(2)}) collective-permute-start(bf16[8,48,3072]{2,1,0:T(8,128)(2,1)} %get-tuple-element.417), channel_id=1, source_target_pairs={{0,1},{1,0},{2,3},{3,2},{4,5},{5,4},{6,7},{7,6},{8,9},{9,8},{10,11... | collective-permute-start | bytes 7077896 | tf_op jit(solution)/shard_map/ppermute | solution.py:366
  13.0 39.2 %collective-permute-start.3 = (bf16[3072,256]{1,0:T(8,128)(2,1)}, bf16[3072,256]{1,0:T(8,128)(2,1)}, u32[]{:S(2)}, u32[]{:S(2)}) collective-permute-start(bf16[3072,256]{1,0:T(8,128)(2,1)} %constant_dynamic-update-slice_fusion.x_ref), channel_id=1, source_target_pairs={{0,6},{1,7},{2,4},{3,5},{4,2},{5,3},{6,0},{7,1},{8,14},{9,15},{10,... | collective-permute-start | bytes 4718600 | tf_op jit(solution)/shard_map/ppermute | solution.py:366
  25.6 66.6 %collective-permute-start.1 = (bf16[8,48,3072]{2,1,0:T(8,128)(2,1)S(1)}, bf16[8,48,3072]{2,1,0:T(8,128)(2,1)}, u32[]{:S(2)}, u32[]{:S(2)}) collective-permute-start(bf16[8,48,3072]{2,1,0:T(8,128)(2,1)S(1)} %get-tuple-element.419), channel_id=1, source_target_pairs={{0,2},{1,3},{2,0},{3,1},{4,6},{5,7},{6,4},{7,5},{8,10},{9,11},{10,... | collective-permute-start | bytes 7077896 | tf_op jit(solution)/shard_map/ppermute | solution.py:366
  52.2 37.6 %collective-permute-start.8 = (bf16[3072,256]{1,0:T(8,128)(2,1)}, bf16[3072,256]{1,0:T(8,128)(2,1)}, u32[]{:S(2)}, u32[]{:S(2)}) collective-permute-start(bf16[3072,256]{1,0:T(8,128)(2,1)} %collective-permute-done.3.x_ref), channel_id=1, source_target_pairs={{0,1},{1,0},{2,3},{3,2},{4,5},{5,4},{6,7},{7,6},{8,9},{9,8},{10,11... | collective-permute-start | bytes 4718600 | tf_op jit(solution)/shard_map/ppermute | solution.py:366
  52.2 26.7 %collective-permute-start.15 = (s32[8,48]{1,0:T(8,128)S(1)}, s32[8,48]{1,0:T(8,128)S(1)}, u32[]{:S(2)}, u32[]{:S(2)}) collective-permute-start(s32[8,48]{1,0:T(8,128)S(1)} %get-tuple-element.427), channel_id=1, source_target_pairs={{4,0},{5,1},{6,2},{7,3},{0,4},{1,5},{2,6},{3,7},{12,8},{13,9},{14,... | collective-permute-start | bytes 4616 | tf_op jit(solution)/shard_map/ppermute | solution.py:366
  54.1 25.6 %collective-permute-start.13 = (s32[8,48]{1,0:T(8,128)S(1)}, s32[8,48]{1,0:T(8,128)S(1)}, u32[]{:S(2)}, u32[]{:S(2)}) collective-permute-start(s32[8,48]{1,0:T(8,128)S(1)} %get-tuple-element.427), channel_id=1, source_target_pairs={{6,0},{7,1},{4,2},{5,3},{2,4},{3,5},{0,6},{1,7},{14,8},{15,9},{12,... | collective-permute-start | bytes 4616 | tf_op jit(solution)/shard_map/ppermute | solution.py:366
  55.3 26.2 %collective-permute-start.11 = (s32[8,48]{1,0:T(8,128)S(1)}, s32[8,48]{1,0:T(8,128)S(1)}, u32[]{:S(2)}, u32[]{:S(2)}) collective-permute-start(s32[8,48]{1,0:T(8,128)S(1)} %get-tuple-element.427), channel_id=1, source_target_pairs={{0,2},{1,3},{2,0},{3,1},{4,6},{5,7},{6,4},{7,5},{8,10},{9,11},{10,... | collective-permute-start | bytes 4616 | tf_op jit(solution)/shard_map/ppermute | solution.py:366
  78.8 5.3 collective-permute-start.16
  79.7 4.5 collective-permute-start.14
  81.4 55.2 %collective-permute-start.9 = (bf16[3072,384]{1,0:T(8,128)(2,1)}, bf16[3072,384]{1,0:T(8,128)(2,1)}, u32[]{:S(2)}, u32[]{:S(2)}) collective-permute-start(bf16[3072,384]{1,0:T(8,128)(2,1)} %x_ref.1), channel_id=1, source_target_pairs={{0,6},{1,7},{2,4},{3,5},{4,2},{5,3},{6,0},{7,1},{8,14},{9,15},{10,... | collective-permute-start | bytes 7077896 | tf_op jit(solution)/shard_map/ppermute | solution.py:366
  84.1 3.1 collective-permute-start.12
  84.2 3.0 collective-permute-start.10
  136.6 4.9 collective-permute-start.17
  136.6 53.1 %collective-permute-start = (bf16[8,48,3072]{2,1,0:T(8,128)(2,1)}, bf16[8,48,3072]{2,1,0:T(8,128)(2,1)S(1)}, u32[]{:S(2)}, u32[]{:S(2)}) collective-permute-start(bf16[8,48,3072]{2,1,0:T(8,128)(2,1)} %get-tuple-element.420), channel_id=1, source_target_pairs={{0,3},{1,2},{2,1},{3,0},{4,7},{5,6},{6,5},{7,4},{8,11},{9,10},{10,... | collective-permute-start | bytes 7077896 | tf_op jit(solution)/shard_map/ppermute | solution.py:366
  136.6 91.0 %collective-permute-start.21 = (bf16[384,3072]{1,0:T(8,128)(2,1)}, bf16[384,3072]{1,0:T(8,128)(2,1)}, u32[]{:S(2)}, u32[]{:S(2)}) collective-permute-start(bf16[384,3072]{1,0:T(8,128)(2,1)} %x_ref.2), channel_id=1, source_target_pairs={{0,6},{1,7},{2,4},{3,5},{4,2},{5,3},{6,0},{7,1},{8,14},{9,15},{10,... | collective-permute-start | bytes 7077896 | tf_op jit(solution)/shard_map/ppermute | solution.py:366
  204.0 30.5 %copy-start.1 = (bf16[1536,512]{1,0:T(8,128)(2,1)S(1)}, bf16[1536,512]{1,0:T(8,128)(2,1)}, u32[]{:S(2)}) copy-start(bf16[1536,512]{1,0:T(8,128)(2,1)} %project.7) | copy-start | bytes 4718596
  227.6 12.0 %collective-permute-start.22 = (bf16[384,3072]{1,0:T(8,128)(2,1)}, bf16[384,3072]{1,0:T(8,128)(2,1)}, u32[]{:S(2)}, u32[]{:S(2)}) collective-permute-start(bf16[384,3072]{1,0:T(8,128)(2,1)} %collective-permute-done.21.x_ref), channel_id=1, source_target_pairs={{0,1},{1,0},{2,3},{3,2},{4,5},{5,4},{6,7},{7,6},{8,9},{9,8},{10,11... | collective-permute-start | bytes 7077896 | tf_op jit(solution)/shard_map/ppermute | solution.py:366
  228.5 126.4 %collective-permute-start.23 = (bf16[8,48,3072]{2,1,0:T(8,128)(2,1)}, bf16[8,48,3072]{2,1,0:T(8,128)(2,1)}, u32[]{:S(2)}, u32[]{:S(2)}) collective-permute-start(bf16[8,48,3072]{2,1,0:T(8,128)(2,1)} %get-tuple-element.417), channel_id=1, source_target_pairs={{0,3},{1,2},{2,1},{3,0},{4,7},{5,6},{6,5},{7,4},{8,11},{9,10},{10,... | collective-permute-start | bytes 7077896 | tf_op jit(solution)/shard_map/ppermute | solution.py:366
  228.7 104.3 %collective-permute-start.20 = (bf16[8,48,3072]{2,1,0:T(8,128)(2,1)}, bf16[8,48,3072]{2,1,0:T(8,128)(2,1)}, u32[]{:S(2)}, u32[]{:S(2)}) collective-permute-start(bf16[8,48,3072]{2,1,0:T(8,128)(2,1)} %get-tuple-element.418), channel_id=1, source_target_pairs={{0,2},{1,3},{2,0},{3,1},{4,6},{5,7},{6,4},{7,5},{8,10},{9,11},{10,... | collective-permute-start | bytes 7077896 | tf_op jit(solution)/shard_map/ppermute | solution.py:366
  230.3 136.6 %collective-permute-start.18 = (bf16[4,8,48,512]{3,2,1,0:T(8,128)(2,1)}, bf16[4,8,48,512]{3,2,1,0:T(8,128)(2,1)}, u32[]{:S(2)}, u32[]{:S(2)}) collective-permute-start(bf16[4,8,48,512]{3,2,1,0:T(8,128)(2,1)} %bitcast.120), channel_id=1, source_target_pairs={{0,6},{1,7},{2,4},{3,5},{8,14},{9,15},{10,12},{11,13}} | collective-permute-start | bytes 4718600 | tf_op jit(solution)/shard_map/ppermute | solution.py:366
  234.5 108.0 %collective-permute-start.19 = (bf16[4,8,48,512]{3,2,1,0:T(8,128)(2,1)S(1)}, bf16[4,8,48,512]{3,2,1,0:T(8,128)(2,1)}, u32[]{:S(2)}, u32[]{:S(2)}) collective-permute-start(bf16[4,8,48,512]{3,2,1,0:T(8,128)(2,1)S(1)} %bitcast.119), channel_id=1, source_target_pairs={{0,6},{1,7},{2,4},{3,5},{8,14},{9,15},{10,12},{11,13}} | collective-permute-start | bytes 4718600 | tf_op jit(solution)/shard_map/ppermute | solution.py:366
  242.4 9.5 %copy-start = (bf16[1536,3072]{1,0:T(8,128)(2,1)S(1)}, bf16[1536,3072]{1,0:T(8,128)(2,1)}, u32[]{:S(2)}) copy-start(bf16[1536,3072]{1,0:T(8,128)(2,1)} %place.37.w_ref) | copy-start | bytes 28311556
  426.6 64.2 %slice-start = ((s8[9437184]{0:T(1024)(128)(4,1)}), s8[1048576]{0:T(1024)(128)(4,1)S(1)}, s32[]{:S(2)}) async-start(s8[9437184]{0:T(1024)(128)(4,1)} %bitcast.71), calls=%async_computation | async-start | bytes 2097152
  438.5 11.3 %copy-start.19 = (bf16[4,8,48,256]{3,2,1,0:T(8,128)(2,1)S(1)}, bf16[4,8,48,256]{3,2,1,0:T(8,128)(2,1)}, u32[]{:S(2)}) copy-start(bf16[4,8,48,256]{3,2,1,0:T(8,128)(2,1)} %get-tuple-element.339) | copy-start | bytes 2359300
  438.5 12.6 %copy-start.18 = (bf16[4,8,48,256]{3,2,1,0:T(8,128)(2,1)S(1)}, bf16[4,8,48,256]{3,2,1,0:T(8,128)(2,1)}, u32[]{:S(2)}) copy-start(bf16[4,8,48,256]{3,2,1,0:T(8,128)(2,1)} %get-tuple-element.340) | copy-start | bytes 2359300
  438.5 13.9 %copy-start.17 = (bf16[4,8,48,256]{3,2,1,0:T(8,128)(2,1)S(1)}, bf16[4,8,48,256]{3,2,1,0:T(8,128)(2,1)}, u32[]{:S(2)}) copy-start(bf16[4,8,48,256]{3,2,1,0:T(8,128)(2,1)} %get-tuple-element.333) | copy-start | bytes 2359300
  438.5 15.2 %copy-start.16 = (bf16[4,8,48,256]{3,2,1,0:T(8,128)(2,1)S(1)}, bf16[4,8,48,256]{3,2,1,0:T(8,128)(2,1)}, u32[]{:S(2)}) copy-start(bf16[4,8,48,256]{3,2,1,0:T(8,128)(2,1)} %get-tuple-element.334) | copy-start | bytes 2359300
  438.6 51.6 %copy-start.6 = (f32[4,8,48,512]{3,2,1,0:T(8,128)S(1)}, f32[4,8,48,512]{3,2,1,0:T(8,128)}, u32[]{:S(2)}) copy-start(f32[4,8,48,512]{3,2,1,0:T(8,128)} %get-tuple-element.341) | copy-start | bytes 9437188
  438.6 52.2 %slice-start.1 = ((s8[9437184]{0:T(1024)(128)(4,1)}), s8[4194304]{0:T(1024)(128)(4,1)S(1)}, s32[]{:S(2)}) async-start(s8[9437184]{0:T(1024)(128)(4,1)} %bitcast.71), calls=%async_computation.1 | async-start | bytes 8388608
  438.6 52.2 %slice-start.2 = ((s8[9437184]{0:T(1024)(128)(4,1)}), s8[4194304]{0:T(1024)(128)(4,1)S(1)}, s32[]{:S(2)}) async-start(s8[9437184]{0:T(1024)(128)(4,1)} %bitcast.71), calls=%async_computation.2 | async-start | bytes 8388608
  449.7 48.1 %collective-permute-start.27 = (bf16[3072,768]{1,0:T(8,128)(2,1)S(1)}, bf16[3072,768]{1,0:T(8,128)(2,1)S(1)}, u32[]{:S(2)}, u32[]{:S(2)}) collective-permute-start(bf16[3072,768]{1,0:T(8,128)(2,1)S(1)} %convolution_convert_fusion), channel_id=1, source_target_pairs={{0,1},{1,0},{2,3},{3,2},{4,5},{5,4},{6,7},{7,6},{8,9},{9,8},{10,11... | collective-permute-start | bytes 14155784 | tf_op jit(solution)/shard_map/ppermute | solution.py:366
  449.8 23.6 %collective-permute-start.28 = (bf16[4,8,48,256]{3,2,1,0:T(8,128)(2,1)S(1)}, bf16[4,8,48,256]{3,2,1,0:T(8,128)(2,1)S(1)}, u32[]{:S(2)}, u32[]{:S(2)}) collective-permute-start(bf16[4,8,48,256]{3,2,1,0:T(8,128)(2,1)S(1)} %copy-done.19), channel_id=1, source_target_pairs={{4,2},{5,3},{6,0},{7,1},{12,10},{13,11},{14,8},{15,9}} | collective-permute-start | bytes 2359304 | tf_op jit(solution)/shard_map/ppermute | solution.py:366
  451.1 39.1 %collective-permute-start.29 = (bf16[4,8,48,256]{3,2,1,0:T(8,128)(2,1)S(1)}, bf16[4,8,48,256]{3,2,1,0:T(8,128)(2,1)S(1)}, u32[]{:S(2)}, u32[]{:S(2)}) collective-permute-start(bf16[4,8,48,256]{3,2,1,0:T(8,128)(2,1)S(1)} %copy-done.18), channel_id=1, source_target_pairs={{4,2},{5,3},{6,0},{7,1},{12,10},{13,11},{14,8},{15,9}} | collective-permute-start | bytes 2359304 | tf_op jit(solution)/shard_map/ppermute | solution.py:366
  452.4 54.6 %collective-permute-start.25 = (bf16[4,8,48,256]{3,2,1,0:T(8,128)(2,1)S(1)}, bf16[4,8,48,256]{3,2,1,0:T(8,128)(2,1)S(1)}, u32[]{:S(2)}, u32[]{:S(2)}) collective-permute-start(bf16[4,8,48,256]{3,2,1,0:T(8,128)(2,1)S(1)} %copy-done.17), channel_id=1, source_target_pairs={{4,2},{5,3},{6,0},{7,1},{12,10},{13,11},{14,8},{15,9}} | collective-permute-start | bytes 2359304 | tf_op jit(solution)/shard_map/ppermute | solution.py:366
  453.8 69.6 %collective-permute-start.26 = (bf16[4,8,48,256]{3,2,1,0:T(8,128)(2,1)S(1)}, bf16[4,8,48,256]{3,2,1,0:T(8,128)(2,1)S(1)}, u32[]{:S(2)}, u32[]{:S(2)}) collective-permute-start(bf16[4,8,48,256]{3,2,1,0:T(8,128)(2,1)S(1)} %copy-done.16), channel_id=1, source_target_pairs={{4,2},{5,3},{6,0},{7,1},{12,10},{13,11},{14,8},{15,9}} | collective-permute-start | bytes 2359304 | tf_op jit(solution)/shard_map/ppermute | solution.py:366
  497.8 25.6 %copy-start.5 = (f32[4,8,48,512]{3,2,1,0:T(8,128)S(1)}, f32[4,8,48,512]{3,2,1,0:T(8,128)}, u32[]{:S(2)}) copy-start(f32[4,8,48,512]{3,2,1,0:T(8,128)} %get-tuple-element.349) | copy-start | bytes 9437188
  497.8 51.4 %collective-permute-start.30 = (bf16[3072,512]{1,0:T(8,128)(2,1)}, bf16[3072,512]{1,0:T(8,128)(2,1)}, u32[]{:S(2)}, u32[]{:S(2)}) collective-permute-start(bf16[3072,512]{1,0:T(8,128)(2,1)} %convolution_convert_fusion.2), channel_id=1, source_target_pairs={{0,1},{1,0},{2,3},{3,2},{4,5},{5,4},{6,7},{7,6},{8,9},{9,8},{10,11... | collective-permute-start | bytes 9437192 | tf_op jit(solution)/shard_map/ppermute | solution.py:366
  497.8 8.9 %copy-start.13 = (bf16[3072,768]{1,0:T(8,128)(2,1)}, bf16[3072,768]{1,0:T(8,128)(2,1)S(1)}, u32[]{:S(2)}) copy-start(bf16[3072,768]{1,0:T(8,128)(2,1)S(1)} %collective-permute-done.27) | copy-start | bytes 14155780
  537.1 12.1 %copy-start.2 = (bf16[4,8,48,512]{3,2,1,0:T(8,128)(2,1)S(1)}, bf16[4,8,48,512]{3,2,1,0:T(8,128)(2,1)}, u32[]{:S(2)}) copy-start(bf16[4,8,48,512]{3,2,1,0:T(8,128)(2,1)} %add_convert_fusion.1) | copy-start | bytes 4718596
  537.1 20.4 %slice-start.6 = ((s8[4718592]{0:T(1024)(128)(4,1)}), s8[524288]{0:T(1024)(128)(4,1)S(1)}, s32[]{:S(2)}) async-start(s8[4718592]{0:T(1024)(128)(4,1)} %bitcast.96), calls=%async_computation.6 | async-start | bytes 1048576
  557.5 13.2 %copy-start.14 = (bf16[384,3072]{1,0:T(8,128)(2,1)S(1)}, bf16[384,3072]{1,0:T(8,128)(2,1)}, u32[]{:S(2)}) copy-start(bf16[384,3072]{1,0:T(8,128)(2,1)} %get-tuple-element.291) | copy-start | bytes 7077892
  570.6 68.6 %collective-permute-start.33 = (bf16[768,3072]{1,0:T(8,128)(2,1)}, bf16[768,3072]{1,0:T(8,128)(2,1)}, u32[]{:S(2)}, u32[]{:S(2)}) collective-permute-start(bf16[768,3072]{1,0:T(8,128)(2,1)} %convolution_convert_fusion.1), channel_id=1, source_target_pairs={{0,1},{1,0},{2,3},{3,2},{4,5},{5,4},{6,7},{7,6},{8,9},{9,8},{10,11... | collective-permute-start | bytes 14155784 | tf_op jit(solution)/shard_map/ppermute | solution.py:366
  570.6 54.1 %collective-permute-start.24 = (bf16[384,3072]{1,0:T(8,128)(2,1)S(1)}, bf16[384,3072]{1,0:T(8,128)(2,1)S(1)}, u32[]{:S(2)}, u32[]{:S(2)}) collective-permute-start(bf16[384,3072]{1,0:T(8,128)(2,1)S(1)} %copy-done.14), channel_id=1, source_target_pairs={{0,2},{1,3},{2,0},{3,1},{4,6},{5,7},{6,4},{7,5},{8,10},{9,11},{10,... | collective-permute-start | bytes 7077896 | tf_op jit(solution)/shard_map/ppermute | solution.py:366
  570.6 103.8 %collective-permute-start.32 = (bf16[384,3072]{1,0:T(8,128)(2,1)}, bf16[384,3072]{1,0:T(8,128)(2,1)}, u32[]{:S(2)}, u32[]{:S(2)}) collective-permute-start(bf16[384,3072]{1,0:T(8,128)(2,1)} %get-tuple-element.372), channel_id=1, source_target_pairs={{0,3},{1,2},{2,1},{3,0},{4,7},{5,6},{6,5},{7,4},{8,11},{9,10},{10,... | collective-permute-start | bytes 7077896 | tf_op jit(solution)/shard_map/ppermute | solution.py:366
  639.0 36.1 %collective-permute-start.31 = (bf16[384,3072]{1,0:T(8,128)(2,1)}, bf16[384,3072]{1,0:T(8,128)(2,1)}, u32[]{:S(2)}, u32[]{:S(2)}) collective-permute-start(bf16[384,3072]{1,0:T(8,128)(2,1)} %get-tuple-element.371), channel_id=1, source_target_pairs={{0,1},{1,0},{2,3},{3,2},{4,5},{5,4},{6,7},{7,6},{8,9},{9,8},{10,11... | collective-permute-start | bytes 7077896 | tf_op jit(solution)/shard_map/ppermute | solution.py:366
  639.1 86.9 %collective-permute-start.36 = (bf16[384,3072]{1,0:T(8,128)(2,1)}, bf16[384,3072]{1,0:T(8,128)(2,1)}, u32[]{:S(2)}, u32[]{:S(2)}) collective-permute-start(bf16[384,3072]{1,0:T(8,128)(2,1)} %grad_in.3), channel_id=1, source_target_pairs={{0,2},{1,3},{2,0},{3,1},{4,6},{5,7},{6,4},{7,5},{8,10},{9,11},{10,... | collective-permute-start | bytes 7077896 | tf_op jit(solution)/shard_map/ppermute | solution.py:366
  639.1 94.7 %collective-permute-start.37 = (bf16[3072,384]{1,0:T(8,128)(2,1)}, bf16[3072,384]{1,0:T(8,128)(2,1)}, u32[]{:S(2)}, u32[]{:S(2)}) collective-permute-start(bf16[3072,384]{1,0:T(8,128)(2,1)} %add_convert_fusion), channel_id=1, source_target_pairs={{0,6},{1,7},{2,4},{3,5},{4,2},{5,3},{6,0},{7,1},{8,14},{9,15},{10,... | collective-permute-start | bytes 7077896 | tf_op jit(solution)/shard_map/ppermute | solution.py:366
  639.2 110.1 %collective-permute-start.38 = (bf16[3072,256]{1,0:T(8,128)(2,1)}, bf16[3072,256]{1,0:T(8,128)(2,1)}, u32[]{:S(2)}, u32[]{:S(2)}) collective-permute-start(bf16[3072,256]{1,0:T(8,128)(2,1)} %fusion), channel_id=1, source_target_pairs={{0,6},{1,7},{2,4},{3,5},{4,2},{5,3},{6,0},{7,1},{8,14},{9,15},{10,... | collective-permute-start | bytes 4718600 | tf_op jit(solution)/shard_map/ppermute | solution.py:366
  655.3 19.2 %copy-start.8 = (bf16[384,3072]{1,0:T(8,128)(2,1)S(1)}, bf16[384,3072]{1,0:T(8,128)(2,1)}, u32[]{:S(2)}) copy-start(bf16[384,3072]{1,0:T(8,128)(2,1)} %grad_in.4) | copy-start | bytes 7077892
  674.5 101.1 %collective-permute-start.35 = (bf16[384,3072]{1,0:T(8,128)(2,1)S(1)}, bf16[384,3072]{1,0:T(8,128)(2,1)}, u32[]{:S(2)}, u32[]{:S(2)}) collective-permute-start(bf16[384,3072]{1,0:T(8,128)(2,1)S(1)} %copy-done.8), channel_id=1, source_target_pairs={{0,3},{1,2},{2,1},{3,0},{4,7},{5,6},{6,5},{7,4},{8,11},{9,10},{10,... | collective-permute-start | bytes 7077896 | tf_op jit(solution)/shard_map/ppermute | solution.py:366
  733.8 41.8 %collective-permute-start.34 = (bf16[384,3072]{1,0:T(8,128)(2,1)}, bf16[384,3072]{1,0:T(8,128)(2,1)}, u32[]{:S(2)}, u32[]{:S(2)}) collective-permute-start(bf16[384,3072]{1,0:T(8,128)(2,1)} %get-tuple-element.388), channel_id=1, source_target_pairs={{0,1},{1,0},{2,3},{3,2},{4,5},{5,4},{6,7},{7,6},{8,9},{9,8},{10,11... | collective-permute-start | bytes 7077896 | tf_op jit(solution)/shard_map/ppermute | solution.py:366
  733.9 10.9 %slice-start.3 = ((s8[9437184]{0:T(1024)(128)(4,1)}), s8[4194304]{0:T(1024)(128)(4,1)S(1)}, s32[]{:S(2)}) async-start(s8[9437184]{0:T(1024)(128)(4,1)} %bitcast.73), calls=%async_computation.3 | async-start | bytes 8388608
  733.9 10.9 %slice-start.4 = ((s8[9437184]{0:T(1024)(128)(4,1)}), s8[4194304]{0:T(1024)(128)(4,1)S(1)}, s32[]{:S(2)}) async-start(s8[9437184]{0:T(1024)(128)(4,1)} %bitcast.73), calls=%async_computation.4 | async-start | bytes 8388608
  734.0 10.9 %slice-start.5 = ((s8[9437184]{0:T(1024)(128)(4,1)}), s8[1048576]{0:T(1024)(128)(4,1)S(1)}, s32[]{:S(2)}) async-start(s8[9437184]{0:T(1024)(128)(4,1)} %bitcast.73), calls=%async_computation.5 | async-start | bytes 2097152
  734.0 10.9 %copy-start.3 = (bf16[4,8,48,512]{3,2,1,0:T(8,128)(2,1)S(1)}, bf16[4,8,48,512]{3,2,1,0:T(8,128)(2,1)}, u32[]{:S(2)}) copy-start(bf16[4,8,48,512]{3,2,1,0:T(8,128)(2,1)} %add_convert_fusion.1) | copy-start | bytes 4718596
  734.0 55.2 %collective-permute-start.42 = (bf16[384,3072]{1,0:T(8,128)(2,1)}, bf16[384,3072]{1,0:T(8,128)(2,1)}, u32[]{:S(2)}, u32[]{:S(2)}) collective-permute-start(bf16[384,3072]{1,0:T(8,128)(2,1)} %get-tuple-element.412), channel_id=1, source_target_pairs={{0,6},{1,7},{2,4},{3,5},{4,2},{5,3},{6,0},{7,1},{8,14},{9,15},{10,... | collective-permute-start | bytes 7077896 | tf_op jit(solution)/shard_map/ppermute | solution.py:366
  784.3 1.5 collective-permute-start.39
  785.9 3.7 collective-permute-start.40
  789.6 6.2 collective-permute-start.41
  (9 other events, 52.6 us)
